TPU v7x, 1024 devices: a whole 4x8x16 slice. The times are simulated.
1024 devices in a mesh: gx: 4 (over x), gy: 16 (over y, z_hi), gz: 16 (over z_lo, core).
Axes of the slice: x: 4, y: 8, z: 16 (z_hi: 2, z_lo: 8; z = z_hi * 8 + z_lo), core: 2. Of those that a mesh axis runs over, the one named last changes fastest.
Arguments:
- fields: float32 [4, 32, 256, 2048], P(None, 'gx', 'gy', 'gz'), may hold values from 0 to 1
- grain_ids: int32 [32, 256], P('gx', 'gy'), may hold values from 0 to 63
- grain_angle: float32 [64], replicated, may hold values from -3.140625 to 3.140625
- melt_planes: float32 [2, 4, 32, 256, 16], P(None, None, 'gx', 'gy'), may hold values from 0 to 1
- shifts: int32 [2], replicated, may hold values from 1 to 16, as said below
Outputs:
- fields_out: float32 [4, 32, 256, 2048], P(None, 'gx', 'gy', 'gz')
Inputs may be any that keep to these rules, and one draw needn't show every extreme that they name: `shifts`: one of the two entries equals 16.
All inputs are finite; a program needn't handle non-finite values.
Results may differ from a plain program's by a relative error of at most 0.0001.
Values sent between devices are 32-bit elements; how exact they have to be, the bound alone decides.
No kernel may reach another device: no remote copies, remote signals or barrier semaphores. Data moves between devices by JAX's collectives and lax.ppermute only.
A program may use at most 32 MiB of HBM per device.

v0:
```python
import jax
import jax.numpy as jnp
from jax import lax
from jax.sharding import PartitionSpec as P

STEPS = 4


time_step = 0.05
well_weight = 1.5
grad_weight = 0.05
aniso_weight = 0.6
couple_weights = (0.3, -0.2, 0.1)
solute_slopes = (0.5, 0.8, 1.1)


def shifted(value, axis, by):
    devices = lax.axis_size(axis)
    pairs = [(i, i + by) for i in range(devices) if 0 <= i + by < devices]
    return lax.ppermute(value, axis, pairs)


def with_halo(value, sides, width, wrap):
    for axis, dim in sides:
        devices, length = (lax.axis_size(axis), value.shape[dim])
        up = [(i, (i + 1) % devices) for i in range(devices if wrap else devices - 1)]
        down = [(j, i) for i, j in up]
        last = lax.slice_in_dim(value, length - width, length, axis=dim)
        first = lax.slice_in_dim(value, 0, width, axis=dim)
        before = lax.ppermute(last, axis, up)
        after = lax.ppermute(first, axis, down)
        value = jnp.concatenate([before, value, after], axis=dim)
    return value


def laplace(field):
    middle = field[..., 1:-1, 1:-1, 1:-1]
    summed = field[..., 2:, 1:-1, 1:-1] + field[..., :-2, 1:-1, 1:-1]
    summed = summed + field[..., 1:-1, 2:, 1:-1] + field[..., 1:-1, :-2, 1:-1]
    summed = summed + field[..., 1:-1, 1:-1, 2:] + field[..., 1:-1, 1:-1, :-2]
    return summed - 6.0 * middle


def mobility_of(grain_ids, grain_angle):
    number_list = jnp.arange(grain_angle.shape[0], dtype=jnp.int32)
    onehot = (grain_ids[None, :, :] == number_list[:, None, None]).astype(jnp.float32)
    angle_map = jnp.sum(onehot * grain_angle[:, None, None], axis=0)
    return jnp.stack(
        [
            1.0 + aniso_weight * jnp.cos(4.0 * angle_map + 2.0944 * phase_idx)
            for phase_idx in range(3)
        ]
    )


def heat_distribution(solidifying_direction, slice_count):
    return (2.0 * solidifying_direction.astype(jnp.float32) + 1.0) / slice_count - 1.0


def step_core(padded, mobility, heat_gradient_curve):
    solute_wide = padded[3]
    potential = solute_wide[1:-1, 1:-1, 1:-1] - grad_weight * laplace(solute_wide)
    for phase_idx in range(3):
        potential = potential + couple_weights[phase_idx] * padded[phase_idx, 1:-1, 1:-1, 1:-1]
    dopant_current = laplace(potential)
    interior = padded[:, 2:-2, 2:-2, 2:-2]
    phases_in = interior[:3]
    solute_in = interior[3]
    phase_lap = laplace(padded[:3, 1:-1, 1:-1, 1:-1])
    squares = jnp.sum(phases_in * phases_in, axis=0)
    results = []
    for phase_idx in range(3):
        value = phases_in[phase_idx]
        well = 2.0 * value * (1.0 - value) * (1.0 - 2.0 * value) + well_weight * value * (
            squares - value * value
        )
        drive = (
            6.0
            * value
            * (1.0 - value)
            * (heat_gradient_curve + solute_slopes[phase_idx] * (solute_in - 0.5))
        )
        update = mobility[phase_idx][:, :, None] * (phase_lap[phase_idx] - well) - drive
        results.append(value + time_step * update)
    results.append(solute_in + time_step * dopant_current)
    return jnp.stack(results)


def join_parts(phases_padded, solute_padded):
    phases_full = jnp.pad(phases_padded, ((0, 0), (1, 1), (1, 1), (1, 1)))
    return jnp.concatenate([phases_full, solute_padded], axis=0)


def advance_window(fields, melt_planes, shifts, advance):
    depth = melt_planes.shape[4]
    planes = fields.shape[3]
    lowest_planes = fields[:, :, :, :depth]
    arriving = shifted(lowest_planes, "gz", -1)
    upper_boundary = lax.axis_index("gz") == lax.axis_size("gz") - 1
    arriving = jnp.where(upper_boundary, melt_planes[advance], arriving)
    combined = jnp.concatenate([fields, arriving], axis=3)
    return lax.dynamic_slice_in_dim(combined, shifts[advance], planes, 3)


def body(fields, grain_ids, grain_angle, melt_planes, shifts):
    planes = fields.shape[3]
    slice_count = planes * lax.axis_size("gz")
    z_start = lax.axis_index("gz") * planes
    mobility = mobility_of(grain_ids, grain_angle)
    shard_position = jnp.arange(planes, dtype=jnp.int32) + z_start
    heat_gradient_curve = heat_distribution(shard_position, slice_count)
    for turn_index in range(STEPS):
        phase_side = with_halo(fields[:3], (("gx", 1), ("gy", 2)), 1, True)
        phase_pad = with_halo(phase_side, (("gz", 3),), 1, False)
        solute_side = with_halo(fields[3:], (("gx", 1), ("gy", 2)), 2, True)
        solute_pad = with_halo(solute_side, (("gz", 3),), 2, False)
        fields = step_core(join_parts(phase_pad, solute_pad), mobility, heat_gradient_curve)
        if turn_index % 2 == 1:
            fields = advance_window(fields, melt_planes, shifts, turn_index // 2)
    return fields


def solution(mesh):
    placed = (P(None, "gx", "gy", "gz"), P("gx", "gy"), P(), P(None, None, "gx", "gy", None), P())
    return jax.shard_map(
        body, mesh=mesh, in_specs=placed, out_specs=P(None, "gx", "gy", "gz"), check_vma=False
    )
```

profile of v0, /device:TPU:203, one launch (start us, length us, event | category | flops | bytes accessed | tf_op | source)
XLA Modules:
  0.0 345.4 jit_solution(10778959767839125590)
XLA Ops:
  14.5 16.4 %collective-permute-start.3 = (f32[3,10,1,128]{3,2,1,0:T(1,128)S(1)}, f32[3,10,1,128]{3,2,1,0:T(1,128)S(1)}, u32[]{:S(2)}, u32[]{:S(2)}) collective-permute-start(f32[3,10,1,128]{3,2,1,0:T(1,128)S(1)} %get-tuple-element.47), channel_id=1, source_target_pairs={{0,16},{16,32},{32,48},{48,64},{64,80},{80,96},{96,112},{112,128},... | collective-permute-start | bytes 46088 | tf_op jit(solution)/shard_map/ppermute | solution.py:30
  32.9 11.2 %collective-permute-done.2 = f32[3,10,1,128]{3,2,1,0:T(1,128)S(1)} collective-permute-done((f32[3,10,1,128]{3,2,1,0:T(1,128)S(1)}, f32[3,10,1,128]{3,2,1,0:T(1,128)S(1)}, u32[]{:S(2)}, u32[]{:S(2)}) %collective-permute-start.2) | collective-permute-done | bytes 15392 | tf_op jit(solution)/shard_map/ppermute | solution.py:31
  44.3 6.0 %collective-permute-start.4 = (f32[3,10,18,1]{3,2,1,0:T(8,128)S(1)}, f32[3,10,18,1]{3,2,1,0:T(8,128)S(1)}, u32[]{:S(2)}, u32[]{:S(2)}) collective-permute-start(f32[3,10,18,1]{3,2,1,0:T(8,128)S(1)} %get-tuple-element.21), channel_id=1, source_target_pairs={{1,0},{2,1},{3,2},{4,3},{5,4},{6,5},{7,6},{8,7},{9,8},{10,9},{11,1... | collective-permute-start | bytes 6488 | tf_op jit(solution)/shard_map/ppermute | solution.py:31
  61.0 12.3 %collective-permute-start.15 = (f32[1,12,2,128]{3,2,1,0:T(2,128)S(1)}, f32[1,12,2,128]{3,2,1,0:T(2,128)S(1)}, u32[]{:S(2)}, u32[]{:S(2)}) collective-permute-start(f32[1,12,2,128]{3,2,1,0:T(2,128)S(1)} %get-tuple-element.72), channel_id=1, source_target_pairs={{16,0},{32,16},{48,32},{64,48},{80,64},{96,80},{112,96},{128,112},... | collective-permute-start | bytes 36872 | tf_op jit(solution)/shard_map/ppermute | solution.py:31
  79.2 6.7 %collective-permute-start.16 = (f32[1,12,20,2]{3,2,1,0:T(8,128)S(1)}, f32[1,12,20,2]{3,2,1,0:T(8,128)S(1)}, u32[]{:S(2)}, u32[]{:S(2)}) collective-permute-start(f32[1,12,20,2]{3,2,1,0:T(8,128)S(1)} %get-tuple-element.63), channel_id=1, source_target_pairs={{0,1},{1,2},{2,3},{3,4},{4,5},{5,6},{6,7},{7,8},{8,9},{9,10},{10,1... | collective-permute-start | bytes 5768 | tf_op jit(solution)/shard_map/ppermute | solution.py:30
  87.9 8.6 %collective-permute-start.9 = (f32[3,10,1,128]{3,2,1,0:T(1,128)S(1)}, f32[3,10,1,128]{3,2,1,0:T(1,128)S(1)}, u32[]{:S(2)}, u32[]{:S(2)}) collective-permute-start(f32[3,10,1,128]{3,2,1,0:T(1,128)S(1)} %get-tuple-element.45), channel_id=1, source_target_pairs={{0,16},{16,32},{32,48},{48,64},{64,80},{80,96},{96,112},{112,128},... | collective-permute-start | bytes 46088 | tf_op jit(solution)/shard_map/ppermute | solution.py:30
  96.5 6.3 %collective-permute-start.8 = (f32[3,10,1,128]{3,2,1,0:T(1,128)S(1)}, f32[3,10,1,128]{3,2,1,0:T(1,128)S(1)}, u32[]{:S(2)}, u32[]{:S(2)}) collective-permute-start(f32[3,10,1,128]{3,2,1,0:T(1,128)S(1)} %get-tuple-element.46), channel_id=1, source_target_pairs={{16,0},{32,16},{48,32},{64,48},{80,64},{96,80},{112,96},{128,112},... | collective-permute-start | bytes 46088 | tf_op jit(solution)/shard_map/ppermute | solution.py:31
  103.1 6.6 %collective-permute-done.8 = f32[3,10,1,128]{3,2,1,0:T(1,128)S(1)} collective-permute-done((f32[3,10,1,128]{3,2,1,0:T(1,128)S(1)}, f32[3,10,1,128]{3,2,1,0:T(1,128)S(1)}, u32[]{:S(2)}, u32[]{:S(2)}) %collective-permute-start.8) | collective-permute-done | bytes 15392 | tf_op jit(solution)/shard_map/ppermute | solution.py:31
  112.7 5.4 %collective-permute-start.11 = (f32[3,10,18,1]{3,2,1,0:T(8,128)S(1)}, f32[3,10,18,1]{3,2,1,0:T(8,128)S(1)}, u32[]{:S(2)}, u32[]{:S(2)}) collective-permute-start(f32[3,10,18,1]{3,2,1,0:T(8,128)S(1)} %get-tuple-element.20), channel_id=1, source_target_pairs={{0,1},{1,2},{2,3},{3,4},{4,5},{5,6},{6,7},{7,8},{8,9},{9,10},{10,1... | collective-permute-start | bytes 6488 | tf_op jit(solution)/shard_map/ppermute | solution.py:30
  131.6 7.3 %collective-permute-start.20 = (f32[1,12,2,128]{3,2,1,0:T(2,128)S(1)}, f32[1,12,2,128]{3,2,1,0:T(2,128)S(1)}, u32[]{:S(2)}, u32[]{:S(2)}) collective-permute-start(f32[1,12,2,128]{3,2,1,0:T(2,128)S(1)} %get-tuple-element.69), channel_id=1, source_target_pairs={{0,16},{16,32},{32,48},{48,64},{64,80},{80,96},{96,112},{112,128},... | collective-permute-start | bytes 36872 | tf_op jit(solution)/shard_map/ppermute | solution.py:30
  138.9 7.6 %collective-permute-start.21 = (f32[1,12,2,128]{3,2,1,0:T(2,128)S(1)}, f32[1,12,2,128]{3,2,1,0:T(2,128)S(1)}, u32[]{:S(2)}, u32[]{:S(2)}) collective-permute-start(f32[1,12,2,128]{3,2,1,0:T(2,128)S(1)} %get-tuple-element.70), channel_id=1, source_target_pairs={{16,0},{32,16},{48,32},{64,48},{80,64},{96,80},{112,96},{128,112},... | collective-permute-start | bytes 36872 | tf_op jit(solution)/shard_map/ppermute | solution.py:31
  146.7 5.4 %collective-permute-done.21 = f32[1,12,2,128]{3,2,1,0:T(2,128)S(1)} collective-permute-done((f32[1,12,2,128]{3,2,1,0:T(2,128)S(1)}, f32[1,12,2,128]{3,2,1,0:T(2,128)S(1)}, u32[]{:S(2)}, u32[]{:S(2)}) %collective-permute-start.21) | collective-permute-done | bytes 12320 | tf_op jit(solution)/shard_map/ppermute | solution.py:31
  152.2 8.2 %collective-permute-start.22 = (f32[1,12,20,2]{3,2,1,0:T(8,128)S(1)}, f32[1,12,20,2]{3,2,1,0:T(8,128)S(1)}, u32[]{:S(2)}, u32[]{:S(2)}) collective-permute-start(f32[1,12,20,2]{3,2,1,0:T(8,128)S(1)} %get-tuple-element.61), channel_id=1, source_target_pairs={{0,1},{1,2},{2,3},{3,4},{4,5},{5,6},{6,7},{7,8},{8,9},{9,10},{10,1... | collective-permute-start | bytes 5768 | tf_op jit(solution)/shard_map/ppermute | solution.py:30
  162.8 5.2 %collective-permute-done.23 = f32[1,12,20,2]{3,2,1,0:T(8,128)S(1)} collective-permute-done((f32[1,12,20,2]{3,2,1,0:T(8,128)S(1)}, f32[1,12,20,2]{3,2,1,0:T(8,128)S(1)}, u32[]{:S(2)}, u32[]{:S(2)}) %collective-permute-start.23) | collective-permute-done | bytes 1952 | tf_op jit(solution)/shard_map/ppermute | solution.py:31
  173.5 4.4 %collective-permute-done.24 = f32[4,8,16,16]{3,2,1,0:T(8,128)S(1)} collective-permute-done((f32[4,8,16,16]{3,2,1,0:T(8,128)S(1)}, f32[4,8,16,16]{3,2,1,0:T(8,128)S(1)}, u32[]{:S(2)}, u32[]{:S(2)}) %collective-permute-start.24) | collective-permute-done | bytes 32800 | tf_op jit(solution)/shard_map/ppermute | solution.py:20
  187.2 7.9 %collective-permute-start.28 = (f32[3,10,1,128]{3,2,1,0:T(1,128)S(1)}, f32[3,10,1,128]{3,2,1,0:T(1,128)S(1)}, u32[]{:S(2)}, u32[]{:S(2)}) collective-permute-start(f32[3,10,1,128]{3,2,1,0:T(1,128)S(1)} %get-tuple-element.43), channel_id=1, source_target_pairs={{0,16},{16,32},{32,48},{48,64},{64,80},{80,96},{96,112},{112,128},... | collective-permute-start | bytes 46088 | tf_op jit(solution)/shard_map/ppermute | solution.py:30
  195.1 7.0 %collective-permute-start.27 = (f32[3,10,1,128]{3,2,1,0:T(1,128)S(1)}, f32[3,10,1,128]{3,2,1,0:T(1,128)S(1)}, u32[]{:S(2)}, u32[]{:S(2)}) collective-permute-start(f32[3,10,1,128]{3,2,1,0:T(1,128)S(1)} %get-tuple-element.44), channel_id=1, source_target_pairs={{16,0},{32,16},{48,32},{64,48},{80,64},{96,80},{112,96},{128,112},... | collective-permute-start | bytes 46088 | tf_op jit(solution)/shard_map/ppermute | solution.py:31
  202.1 6.2 %collective-permute-done.27 = f32[3,10,1,128]{3,2,1,0:T(1,128)S(1)} collective-permute-done((f32[3,10,1,128]{3,2,1,0:T(1,128)S(1)}, f32[3,10,1,128]{3,2,1,0:T(1,128)S(1)}, u32[]{:S(2)}, u32[]{:S(2)}) %collective-permute-start.27) | collective-permute-done | bytes 15392 | tf_op jit(solution)/shard_map/ppermute | solution.py:31
  210.5 4.9 %collective-permute-start.30 = (f32[3,10,18,1]{3,2,1,0:T(8,128)S(1)}, f32[3,10,18,1]{3,2,1,0:T(8,128)S(1)}, u32[]{:S(2)}, u32[]{:S(2)}) collective-permute-start(f32[3,10,18,1]{3,2,1,0:T(8,128)S(1)} %get-tuple-element.18), channel_id=1, source_target_pairs={{0,1},{1,2},{2,3},{3,4},{4,5},{5,6},{6,7},{7,8},{8,9},{9,10},{10,1... | collective-permute-start | bytes 6488 | tf_op jit(solution)/shard_map/ppermute | solution.py:30
  222.7 8.5 %collective-permute-start.39 = (f32[1,12,2,128]{3,2,1,0:T(2,128)S(1)}, f32[1,12,2,128]{3,2,1,0:T(2,128)S(1)}, u32[]{:S(2)}, u32[]{:S(2)}) collective-permute-start(f32[1,12,2,128]{3,2,1,0:T(2,128)S(1)} %get-tuple-element.67), channel_id=1, source_target_pairs={{0,16},{16,32},{32,48},{48,64},{64,80},{80,96},{96,112},{112,128},... | collective-permute-start | bytes 36872 | tf_op jit(solution)/shard_map/ppermute | solution.py:30
  231.2 6.4 %collective-permute-start.40 = (f32[1,12,2,128]{3,2,1,0:T(2,128)S(1)}, f32[1,12,2,128]{3,2,1,0:T(2,128)S(1)}, u32[]{:S(2)}, u32[]{:S(2)}) collective-permute-start(f32[1,12,2,128]{3,2,1,0:T(2,128)S(1)} %get-tuple-element.68), channel_id=1, source_target_pairs={{16,0},{32,16},{48,32},{64,48},{80,64},{96,80},{112,96},{128,112},... | collective-permute-start | bytes 36872 | tf_op jit(solution)/shard_map/ppermute | solution.py:31
  244.5 5.0 %collective-permute-start.41 = (f32[1,12,20,2]{3,2,1,0:T(8,128)S(1)}, f32[1,12,20,2]{3,2,1,0:T(8,128)S(1)}, u32[]{:S(2)}, u32[]{:S(2)}) collective-permute-start(f32[1,12,20,2]{3,2,1,0:T(8,128)S(1)} %get-tuple-element.59), channel_id=1, source_target_pairs={{0,1},{1,2},{2,3},{3,4},{4,5},{5,6},{6,7},{7,8},{8,9},{9,10},{10,1... | collective-permute-start | bytes 5768 | tf_op jit(solution)/shard_map/ppermute | solution.py:30
  251.5 9.8 %collective-permute-start.34 = (f32[3,10,1,128]{3,2,1,0:T(1,128)S(1)}, f32[3,10,1,128]{3,2,1,0:T(1,128)S(1)}, u32[]{:S(2)}, u32[]{:S(2)}) collective-permute-start(f32[3,10,1,128]{3,2,1,0:T(1,128)S(1)} %get-tuple-element.41), channel_id=1, source_target_pairs={{0,16},{16,32},{32,48},{48,64},{64,80},{80,96},{96,112},{112,128},... | collective-permute-start | bytes 46088 | tf_op jit(solution)/shard_map/ppermute | solution.py:30
  261.3 5.1 %collective-permute-start.33 = (f32[3,10,1,128]{3,2,1,0:T(1,128)S(1)}, f32[3,10,1,128]{3,2,1,0:T(1,128)S(1)}, u32[]{:S(2)}, u32[]{:S(2)}) collective-permute-start(f32[3,10,1,128]{3,2,1,0:T(1,128)S(1)} %get-tuple-element.42), channel_id=1, source_target_pairs={{16,0},{32,16},{48,32},{64,48},{80,64},{96,80},{112,96},{128,112},... | collective-permute-start | bytes 46088 | tf_op jit(solution)/shard_map/ppermute | solution.py:31
  266.7 7.9 %collective-permute-done.33 = f32[3,10,1,128]{3,2,1,0:T(1,128)S(1)} collective-permute-done((f32[3,10,1,128]{3,2,1,0:T(1,128)S(1)}, f32[3,10,1,128]{3,2,1,0:T(1,128)S(1)}, u32[]{:S(2)}, u32[]{:S(2)}) %collective-permute-start.33) | collective-permute-done | bytes 15392 | tf_op jit(solution)/shard_map/ppermute | solution.py:31
  277.1 5.8 %collective-permute-start.36 = (f32[3,10,18,1]{3,2,1,0:T(8,128)S(1)}, f32[3,10,18,1]{3,2,1,0:T(8,128)S(1)}, u32[]{:S(2)}, u32[]{:S(2)}) collective-permute-start(f32[3,10,18,1]{3,2,1,0:T(8,128)S(1)} %get-tuple-element.16), channel_id=1, source_target_pairs={{0,1},{1,2},{2,3},{3,4},{4,5},{5,6},{6,7},{7,8},{8,9},{9,10},{10,1... | collective-permute-start | bytes 6488 | tf_op jit(solution)/shard_map/ppermute | solution.py:30
  295.3 10.0 %collective-permute-start.45 = (f32[1,12,2,128]{3,2,1,0:T(2,128)S(1)}, f32[1,12,2,128]{3,2,1,0:T(2,128)S(1)}, u32[]{:S(2)}, u32[]{:S(2)}) collective-permute-start(f32[1,12,2,128]{3,2,1,0:T(2,128)S(1)} %get-tuple-element.65), channel_id=1, source_target_pairs={{0,16},{16,32},{32,48},{48,64},{64,80},{80,96},{96,112},{112,128},... | collective-permute-start | bytes 36872 | tf_op jit(solution)/shard_map/ppermute | solution.py:30
  305.3 4.9 %collective-permute-start.46 = (f32[1,12,2,128]{3,2,1,0:T(2,128)S(1)}, f32[1,12,2,128]{3,2,1,0:T(2,128)S(1)}, u32[]{:S(2)}, u32[]{:S(2)}) collective-permute-start(f32[1,12,2,128]{3,2,1,0:T(2,128)S(1)} %get-tuple-element.66), channel_id=1, source_target_pairs={{16,0},{32,16},{48,32},{64,48},{80,64},{96,80},{112,96},{128,112},... | collective-permute-start | bytes 36872 | tf_op jit(solution)/shard_map/ppermute | solution.py:31
  310.3 8.1 %collective-permute-done.46 = f32[1,12,2,128]{3,2,1,0:T(2,128)S(1)} collective-permute-done((f32[1,12,2,128]{3,2,1,0:T(2,128)S(1)}, f32[1,12,2,128]{3,2,1,0:T(2,128)S(1)}, u32[]{:S(2)}, u32[]{:S(2)}) %collective-permute-start.46) | collective-permute-done | bytes 12320 | tf_op jit(solution)/shard_map/ppermute | solution.py:31
  318.6 8.3 %collective-permute-start.47 = (f32[1,12,20,2]{3,2,1,0:T(8,128)S(1)}, f32[1,12,20,2]{3,2,1,0:T(8,128)S(1)}, u32[]{:S(2)}, u32[]{:S(2)}) collective-permute-start(f32[1,12,20,2]{3,2,1,0:T(8,128)S(1)} %get-tuple-element.57), channel_id=1, source_target_pairs={{0,1},{1,2},{2,3},{3,4},{4,5},{5,6},{6,7},{7,8},{8,9},{9,10},{10,1... | collective-permute-start | bytes 5768 | tf_op jit(solution)/shard_map/ppermute | solution.py:30
  329.3 5.2 %collective-permute-done.48 = f32[1,12,20,2]{3,2,1,0:T(8,128)S(1)} collective-permute-done((f32[1,12,20,2]{3,2,1,0:T(8,128)S(1)}, f32[1,12,20,2]{3,2,1,0:T(8,128)S(1)}, u32[]{:S(2)}, u32[]{:S(2)}) %collective-permute-start.48) | collective-permute-done | bytes 1952 | tf_op jit(solution)/shard_map/ppermute | solution.py:31
  339.5 4.9 %collective-permute-done.49 = f32[4,8,16,16]{3,2,1,0:T(8,128)S(1)} collective-permute-done((f32[4,8,16,16]{3,2,1,0:T(8,128)S(1)}, f32[4,8,16,16]{3,2,1,0:T(8,128)S(1)}, u32[]{:S(2)}, u32[]{:S(2)}) %collective-permute-start.49) | collective-permute-done | bytes 32800 | tf_op jit(solution)/shard_map/ppermute | solution.py:20
  (148 shorter events, 106.8 us)
Async XLA Ops:
  0.7 57.5 %collective-permute-start.12 = (f32[1,2,16,128]{3,2,1,0:T(8,128)S(1)}, f32[1,2,16,128]{3,2,1,0:T(8,128)S(1)}, u32[]{:S(2)}, u32[]{:S(2)}) collective-permute-start(f32[1,2,16,128]{3,2,1,0:T(8,128)S(1)} %get-tuple-element.34), channel_id=1, source_target_pairs={{0,256},{256,512},{512,768},{768,0},{1,257},{257,513},{513,769},{7... | collective-permute-start | bytes 49160 | tf_op jit(solution)/shard_map/ppermute | solution.py:30
  3.9 54.4 %collective-permute-start.13 = (f32[1,2,16,128]{3,2,1,0:T(8,128)S(1)}, f32[1,2,16,128]{3,2,1,0:T(8,128)S(1)}, u32[]{:S(2)}, u32[]{:S(2)}) collective-permute-start(f32[1,2,16,128]{3,2,1,0:T(8,128)S(1)} %get-tuple-element.35), channel_id=1, source_target_pairs={{256,0},{512,256},{768,512},{0,768},{257,1},{513,257},{769,513},{1... | collective-permute-start | bytes 49160 | tf_op jit(solution)/shard_map/ppermute | solution.py:31
  14.5 18.4 %collective-permute-start.3 = (f32[3,10,1,128]{3,2,1,0:T(1,128)S(1)}, f32[3,10,1,128]{3,2,1,0:T(1,128)S(1)}, u32[]{:S(2)}, u32[]{:S(2)}) collective-permute-start(f32[3,10,1,128]{3,2,1,0:T(1,128)S(1)} %get-tuple-element.47), channel_id=1, source_target_pairs={{0,16},{16,32},{32,48},{48,64},{64,80},{80,96},{96,112},{112,128},... | collective-permute-start | bytes 46088 | tf_op jit(solution)/shard_map/ppermute | solution.py:30
  30.9 13.2 %collective-permute-start.2 = (f32[3,10,1,128]{3,2,1,0:T(1,128)S(1)}, f32[3,10,1,128]{3,2,1,0:T(1,128)S(1)}, u32[]{:S(2)}, u32[]{:S(2)}) collective-permute-start(f32[3,10,1,128]{3,2,1,0:T(1,128)S(1)} %get-tuple-element.48), channel_id=1, source_target_pairs={{16,0},{32,16},{48,32},{64,48},{80,64},{96,80},{112,96},{128,112},... | collective-permute-start | bytes 46088 | tf_op jit(solution)/shard_map/ppermute | solution.py:31
  44.3 12.3 %collective-permute-start.4 = (f32[3,10,18,1]{3,2,1,0:T(8,128)S(1)}, f32[3,10,18,1]{3,2,1,0:T(8,128)S(1)}, u32[]{:S(2)}, u32[]{:S(2)}) collective-permute-start(f32[3,10,18,1]{3,2,1,0:T(8,128)S(1)} %get-tuple-element.21), channel_id=1, source_target_pairs={{1,0},{2,1},{3,2},{4,3},{5,4},{6,5},{7,6},{8,7},{9,8},{10,9},{11,1... | collective-permute-start | bytes 6488 | tf_op jit(solution)/shard_map/ppermute | solution.py:31
  58.3 20.7 %collective-permute-start.14 = (f32[1,12,2,128]{3,2,1,0:T(2,128)S(1)}, f32[1,12,2,128]{3,2,1,0:T(2,128)S(1)}, u32[]{:S(2)}, u32[]{:S(2)}) collective-permute-start(f32[1,12,2,128]{3,2,1,0:T(2,128)S(1)} %get-tuple-element.71), channel_id=1, source_target_pairs={{0,16},{16,32},{32,48},{48,64},{64,80},{80,96},{96,112},{112,128},... | collective-permute-start | bytes 36872 | tf_op jit(solution)/shard_map/ppermute | solution.py:30
  61.0 18.1 %collective-permute-start.15 = (f32[1,12,2,128]{3,2,1,0:T(2,128)S(1)}, f32[1,12,2,128]{3,2,1,0:T(2,128)S(1)}, u32[]{:S(2)}, u32[]{:S(2)}) collective-permute-start(f32[1,12,2,128]{3,2,1,0:T(2,128)S(1)} %get-tuple-element.72), channel_id=1, source_target_pairs={{16,0},{32,16},{48,32},{64,48},{80,64},{96,80},{112,96},{128,112},... | collective-permute-start | bytes 36872 | tf_op jit(solution)/shard_map/ppermute | solution.py:31
  73.3 14.6 %collective-permute-start.7 = (f32[3,1,16,128]{3,2,1,0:T(8,128)S(1)}, f32[3,1,16,128]{3,2,1,0:T(8,128)S(1)}, u32[]{:S(2)}, u32[]{:S(2)}) collective-permute-start(f32[3,1,16,128]{3,2,1,0:T(8,128)S(1)} %get-tuple-element.55), channel_id=1, source_target_pairs={{0,256},{256,512},{512,768},{768,0},{1,257},{257,513},{513,769},{7... | collective-permute-start | bytes 73736 | tf_op jit(solution)/shard_map/ppermute | solution.py:30
  76.1 11.8 %collective-permute-start.6 = (f32[3,1,16,128]{3,2,1,0:T(8,128)S(1)}, f32[3,1,16,128]{3,2,1,0:T(8,128)S(1)}, u32[]{:S(2)}, u32[]{:S(2)}) collective-permute-start(f32[3,1,16,128]{3,2,1,0:T(8,128)S(1)} %get-tuple-element.56), channel_id=1, source_target_pairs={{256,0},{512,256},{768,512},{0,768},{257,1},{513,257},{769,513},{1... | collective-permute-start | bytes 73736 | tf_op jit(solution)/shard_map/ppermute | solution.py:31
  79.2 23.6 %collective-permute-start.16 = (f32[1,12,20,2]{3,2,1,0:T(8,128)S(1)}, f32[1,12,20,2]{3,2,1,0:T(8,128)S(1)}, u32[]{:S(2)}, u32[]{:S(2)}) collective-permute-start(f32[1,12,20,2]{3,2,1,0:T(8,128)S(1)} %get-tuple-element.63), channel_id=1, source_target_pairs={{0,1},{1,2},{2,3},{3,4},{4,5},{5,6},{6,7},{7,8},{8,9},{9,10},{10,1... | collective-permute-start | bytes 5768 | tf_op jit(solution)/shard_map/ppermute | solution.py:30
  85.9 16.9 %collective-permute-start.17 = (f32[1,12,20,2]{3,2,1,0:T(8,128)S(1)}, f32[1,12,20,2]{3,2,1,0:T(8,128)S(1)}, u32[]{:S(2)}, u32[]{:S(2)}) collective-permute-start(f32[1,12,20,2]{3,2,1,0:T(8,128)S(1)} %get-tuple-element.64), channel_id=1, source_target_pairs={{1,0},{2,1},{3,2},{4,3},{5,4},{6,5},{7,6},{8,7},{9,8},{10,9},{11,1... | collective-permute-start | bytes 5768 | tf_op jit(solution)/shard_map/ppermute | solution.py:31
  87.9 15.2 %collective-permute-start.9 = (f32[3,10,1,128]{3,2,1,0:T(1,128)S(1)}, f32[3,10,1,128]{3,2,1,0:T(1,128)S(1)}, u32[]{:S(2)}, u32[]{:S(2)}) collective-permute-start(f32[3,10,1,128]{3,2,1,0:T(1,128)S(1)} %get-tuple-element.45), channel_id=1, source_target_pairs={{0,16},{16,32},{32,48},{48,64},{64,80},{80,96},{96,112},{112,128},... | collective-permute-start | bytes 46088 | tf_op jit(solution)/shard_map/ppermute | solution.py:30
  96.5 13.2 %collective-permute-start.8 = (f32[3,10,1,128]{3,2,1,0:T(1,128)S(1)}, f32[3,10,1,128]{3,2,1,0:T(1,128)S(1)}, u32[]{:S(2)}, u32[]{:S(2)}) collective-permute-start(f32[3,10,1,128]{3,2,1,0:T(1,128)S(1)} %get-tuple-element.46), channel_id=1, source_target_pairs={{16,0},{32,16},{48,32},{64,48},{80,64},{96,80},{112,96},{128,112},... | collective-permute-start | bytes 46088 | tf_op jit(solution)/shard_map/ppermute | solution.py:31
  110.0 11.5 %collective-permute-start.10 = (f32[3,10,18,1]{3,2,1,0:T(8,128)S(1)}, f32[3,10,18,1]{3,2,1,0:T(8,128)S(1)}, u32[]{:S(2)}, u32[]{:S(2)}) collective-permute-start(f32[3,10,18,1]{3,2,1,0:T(8,128)S(1)} %get-tuple-element.19), channel_id=1, source_target_pairs={{1,0},{2,1},{3,2},{4,3},{5,4},{6,5},{7,6},{8,7},{9,8},{10,9},{11,1... | collective-permute-start | bytes 6488 | tf_op jit(solution)/shard_map/ppermute | solution.py:31
  131.6 15.0 %collective-permute-start.20 = (f32[1,12,2,128]{3,2,1,0:T(2,128)S(1)}, f32[1,12,2,128]{3,2,1,0:T(2,128)S(1)}, u32[]{:S(2)}, u32[]{:S(2)}) collective-permute-start(f32[1,12,2,128]{3,2,1,0:T(2,128)S(1)} %get-tuple-element.69), channel_id=1, source_target_pairs={{0,16},{16,32},{32,48},{48,64},{64,80},{80,96},{96,112},{112,128},... | collective-permute-start | bytes 36872 | tf_op jit(solution)/shard_map/ppermute | solution.py:30
  138.9 13.2 %collective-permute-start.21 = (f32[1,12,2,128]{3,2,1,0:T(2,128)S(1)}, f32[1,12,2,128]{3,2,1,0:T(2,128)S(1)}, u32[]{:S(2)}, u32[]{:S(2)}) collective-permute-start(f32[1,12,2,128]{3,2,1,0:T(2,128)S(1)} %get-tuple-element.70), channel_id=1, source_target_pairs={{16,0},{32,16},{48,32},{64,48},{80,64},{96,80},{112,96},{128,112},... | collective-permute-start | bytes 36872 | tf_op jit(solution)/shard_map/ppermute | solution.py:31
  152.2 10.6 %collective-permute-start.22 = (f32[1,12,20,2]{3,2,1,0:T(8,128)S(1)}, f32[1,12,20,2]{3,2,1,0:T(8,128)S(1)}, u32[]{:S(2)}, u32[]{:S(2)}) collective-permute-start(f32[1,12,20,2]{3,2,1,0:T(8,128)S(1)} %get-tuple-element.61), channel_id=1, source_target_pairs={{0,1},{1,2},{2,3},{3,4},{4,5},{5,6},{6,7},{7,8},{8,9},{9,10},{10,1... | collective-permute-start | bytes 5768 | tf_op jit(solution)/shard_map/ppermute | solution.py:30
  187.2 14.9 %collective-permute-start.28 = (f32[3,10,1,128]{3,2,1,0:T(1,128)S(1)}, f32[3,10,1,128]{3,2,1,0:T(1,128)S(1)}, u32[]{:S(2)}, u32[]{:S(2)}) collective-permute-start(f32[3,10,1,128]{3,2,1,0:T(1,128)S(1)} %get-tuple-element.43), channel_id=1, source_target_pairs={{0,16},{16,32},{32,48},{48,64},{64,80},{80,96},{96,112},{112,128},... | collective-permute-start | bytes 46088 | tf_op jit(solution)/shard_map/ppermute | solution.py:30
  195.1 13.2 %collective-permute-start.27 = (f32[3,10,1,128]{3,2,1,0:T(1,128)S(1)}, f32[3,10,1,128]{3,2,1,0:T(1,128)S(1)}, u32[]{:S(2)}, u32[]{:S(2)}) collective-permute-start(f32[3,10,1,128]{3,2,1,0:T(1,128)S(1)} %get-tuple-element.44), channel_id=1, source_target_pairs={{16,0},{32,16},{48,32},{64,48},{80,64},{96,80},{112,96},{128,112},... | collective-permute-start | bytes 46088 | tf_op jit(solution)/shard_map/ppermute | solution.py:31
  208.5 12.1 %collective-permute-start.29 = (f32[3,10,18,1]{3,2,1,0:T(8,128)S(1)}, f32[3,10,18,1]{3,2,1,0:T(8,128)S(1)}, u32[]{:S(2)}, u32[]{:S(2)}) collective-permute-start(f32[3,10,18,1]{3,2,1,0:T(8,128)S(1)} %get-tuple-element.17), channel_id=1, source_target_pairs={{1,0},{2,1},{3,2},{4,3},{5,4},{6,5},{7,6},{8,7},{9,8},{10,9},{11,1... | collective-permute-start | bytes 6488 | tf_op jit(solution)/shard_map/ppermute | solution.py:31
  222.7 20.7 %collective-permute-start.39 = (f32[1,12,2,128]{3,2,1,0:T(2,128)S(1)}, f32[1,12,2,128]{3,2,1,0:T(2,128)S(1)}, u32[]{:S(2)}, u32[]{:S(2)}) collective-permute-start(f32[1,12,2,128]{3,2,1,0:T(2,128)S(1)} %get-tuple-element.67), channel_id=1, source_target_pairs={{0,16},{16,32},{32,48},{48,64},{64,80},{80,96},{96,112},{112,128},... | collective-permute-start | bytes 36872 | tf_op jit(solution)/shard_map/ppermute | solution.py:30
  231.2 13.2 %collective-permute-start.40 = (f32[1,12,2,128]{3,2,1,0:T(2,128)S(1)}, f32[1,12,2,128]{3,2,1,0:T(2,128)S(1)}, u32[]{:S(2)}, u32[]{:S(2)}) collective-permute-start(f32[1,12,2,128]{3,2,1,0:T(2,128)S(1)} %get-tuple-element.68), channel_id=1, source_target_pairs={{16,0},{32,16},{48,32},{64,48},{80,64},{96,80},{112,96},{128,112},... | collective-permute-start | bytes 36872 | tf_op jit(solution)/shard_map/ppermute | solution.py:31
  237.6 13.8 %collective-permute-start.32 = (f32[3,1,16,128]{3,2,1,0:T(8,128)S(1)}, f32[3,1,16,128]{3,2,1,0:T(8,128)S(1)}, u32[]{:S(2)}, u32[]{:S(2)}) collective-permute-start(f32[3,1,16,128]{3,2,1,0:T(8,128)S(1)} %get-tuple-element.51), channel_id=1, source_target_pairs={{0,256},{256,512},{512,768},{768,0},{1,257},{257,513},{513,769},{7... | collective-permute-start | bytes 73736 | tf_op jit(solution)/shard_map/ppermute | solution.py:30
  240.8 10.7 %collective-permute-start.31 = (f32[3,1,16,128]{3,2,1,0:T(8,128)S(1)}, f32[3,1,16,128]{3,2,1,0:T(8,128)S(1)}, u32[]{:S(2)}, u32[]{:S(2)}) collective-permute-start(f32[3,1,16,128]{3,2,1,0:T(8,128)S(1)} %get-tuple-element.52), channel_id=1, source_target_pairs={{256,0},{512,256},{768,512},{0,768},{257,1},{513,257},{769,513},{1... | collective-permute-start | bytes 73736 | tf_op jit(solution)/shard_map/ppermute | solution.py:31
  244.5 21.9 %collective-permute-start.41 = (f32[1,12,20,2]{3,2,1,0:T(8,128)S(1)}, f32[1,12,20,2]{3,2,1,0:T(8,128)S(1)}, u32[]{:S(2)}, u32[]{:S(2)}) collective-permute-start(f32[1,12,20,2]{3,2,1,0:T(8,128)S(1)} %get-tuple-element.59), channel_id=1, source_target_pairs={{0,1},{1,2},{2,3},{3,4},{4,5},{5,6},{6,7},{7,8},{8,9},{9,10},{10,1... | collective-permute-start | bytes 5768 | tf_op jit(solution)/shard_map/ppermute | solution.py:30
  249.5 16.9 %collective-permute-start.42 = (f32[1,12,20,2]{3,2,1,0:T(8,128)S(1)}, f32[1,12,20,2]{3,2,1,0:T(8,128)S(1)}, u32[]{:S(2)}, u32[]{:S(2)}) collective-permute-start(f32[1,12,20,2]{3,2,1,0:T(8,128)S(1)} %get-tuple-element.60), channel_id=1, source_target_pairs={{1,0},{2,1},{3,2},{4,3},{5,4},{6,5},{7,6},{8,7},{9,8},{10,9},{11,1... | collective-permute-start | bytes 5768 | tf_op jit(solution)/shard_map/ppermute | solution.py:31
  251.5 15.2 %collective-permute-start.34 = (f32[3,10,1,128]{3,2,1,0:T(1,128)S(1)}, f32[3,10,1,128]{3,2,1,0:T(1,128)S(1)}, u32[]{:S(2)}, u32[]{:S(2)}) collective-permute-start(f32[3,10,1,128]{3,2,1,0:T(1,128)S(1)} %get-tuple-element.41), channel_id=1, source_target_pairs={{0,16},{16,32},{32,48},{48,64},{64,80},{80,96},{96,112},{112,128},... | collective-permute-start | bytes 46088 | tf_op jit(solution)/shard_map/ppermute | solution.py:30
  261.3 13.3 %collective-permute-start.33 = (f32[3,10,1,128]{3,2,1,0:T(1,128)S(1)}, f32[3,10,1,128]{3,2,1,0:T(1,128)S(1)}, u32[]{:S(2)}, u32[]{:S(2)}) collective-permute-start(f32[3,10,1,128]{3,2,1,0:T(1,128)S(1)} %get-tuple-element.42), channel_id=1, source_target_pairs={{16,0},{32,16},{48,32},{64,48},{80,64},{96,80},{112,96},{128,112},... | collective-permute-start | bytes 46088 | tf_op jit(solution)/shard_map/ppermute | solution.py:31
  274.8 11.4 %collective-permute-start.35 = (f32[3,10,18,1]{3,2,1,0:T(8,128)S(1)}, f32[3,10,18,1]{3,2,1,0:T(8,128)S(1)}, u32[]{:S(2)}, u32[]{:S(2)}) collective-permute-start(f32[3,10,18,1]{3,2,1,0:T(8,128)S(1)} %get-tuple-element.15), channel_id=1, source_target_pairs={{1,0},{2,1},{3,2},{4,3},{5,4},{6,5},{7,6},{8,7},{9,8},{10,9},{11,1... | collective-permute-start | bytes 6488 | tf_op jit(solution)/shard_map/ppermute | solution.py:31
  295.3 15.0 %collective-permute-start.45 = (f32[1,12,2,128]{3,2,1,0:T(2,128)S(1)}, f32[1,12,2,128]{3,2,1,0:T(2,128)S(1)}, u32[]{:S(2)}, u32[]{:S(2)}) collective-permute-start(f32[1,12,2,128]{3,2,1,0:T(2,128)S(1)} %get-tuple-element.65), channel_id=1, source_target_pairs={{0,16},{16,32},{32,48},{48,64},{64,80},{80,96},{96,112},{112,128},... | collective-permute-start | bytes 36872 | tf_op jit(solution)/shard_map/ppermute | solution.py:30
  305.3 13.2 %collective-permute-start.46 = (f32[1,12,2,128]{3,2,1,0:T(2,128)S(1)}, f32[1,12,2,128]{3,2,1,0:T(2,128)S(1)}, u32[]{:S(2)}, u32[]{:S(2)}) collective-permute-start(f32[1,12,2,128]{3,2,1,0:T(2,128)S(1)} %get-tuple-element.66), channel_id=1, source_target_pairs={{16,0},{32,16},{48,32},{64,48},{80,64},{96,80},{112,96},{128,112},... | collective-permute-start | bytes 36872 | tf_op jit(solution)/shard_map/ppermute | solution.py:31
  318.6 10.7 %collective-permute-start.47 = (f32[1,12,20,2]{3,2,1,0:T(8,128)S(1)}, f32[1,12,20,2]{3,2,1,0:T(8,128)S(1)}, u32[]{:S(2)}, u32[]{:S(2)}) collective-permute-start(f32[1,12,20,2]{3,2,1,0:T(8,128)S(1)} %get-tuple-element.57), channel_id=1, source_target_pairs={{0,1},{1,2},{2,3},{3,4},{4,5},{5,6},{6,7},{7,8},{8,9},{9,10},{10,1... | collective-permute-start | bytes 5768 | tf_op jit(solution)/shard_map/ppermute | solution.py:30
  (23 other events, 146.0 us)
where the time goes:
time: 347 us; the launch traced here: 345 us
  starting transfers between devices  237 us (68%)
  waiting for transfers between devices  89.9 us (26%)
  other arithmetic  10.2 us (3%)
  between operations  5.09 us (1%)
    ppermute x24, starting transfers between devices, with_halo(): before = lax.ppermute(last, axis, up)  143 us
    ppermute x24, starting transfers between devices, with_halo(): after = lax.ppermute(first, axis, down)  90.2 us
    ppermute x24, waiting for transfers between devices, with_halo(): after = lax.ppermute(first, axis, down)  77 us
    ppermute x2, waiting for transfers between devices, shifted(): return lax.ppermute(value, axis, pairs)  9.27 us
  transfers between devices with their start and end apart: 50, of which 22 were waited for; matrix products, arithmetic and copies ran while one was open for 2% of the time, Pallas kernels for 0%

commit v1 on v0

v1 whole, which is shorter than its diff:
```python
import jax
import jax.numpy as jnp
from jax import lax
from jax.experimental import pallas as pl
from jax.experimental.pallas import tpu as pltpu
from jax.sharding import PartitionSpec as P


f32 = jnp.float32
SLOPES = (0.5, 0.8, 1.1)
ZE = 40

Y_ROWS = 224
Y_MELT, Y_IDS = 208, 218
Z_ROWS = 176
X1_ROWS = 512 + Z_ROWS + 8
Z2_TILES = 18
X2_ROWS = 280


def lanes(shape):
    return lax.broadcasted_iota(jnp.int32, shape, len(shape) - 1)


def subs(shape):
    return lax.broadcasted_iota(jnp.int32, shape, len(shape) - 2)


def three(a, b, c):
    lane = lanes(a.shape)
    out = jnp.where(lane < ZE, a, pltpu.roll(b, ZE, len(a.shape) - 1))
    return out if c is None else jnp.where(lane < 2 * ZE, out, pltpu.roll(c, 2 * ZE, len(a.shape) - 1))


def part(a, group):
    return a if group == 0 else pltpu.roll(a, 128 - ZE * group, len(a.shape) - 1)


def combined(c, p0, p1, p2):
    return c - 6.0 * p0 + 4.0 * p1 - 2.0 * p2


def pack_first(f_in, ids_in, melt_in, up, dn, f, ids, melt, sems):
    copies = [
        pltpu.make_async_copy(f_in, f, sems.at[0]),
        pltpu.make_async_copy(ids_in, ids, sems.at[1]),
        pltpu.make_async_copy(melt_in.at[0], melt, sems.at[2]),
    ]
    for copy in copies:
        copy.start()
    copies[0].wait()
    for x in range(8):
        up[8 * x : 8 * x + 8, :] = f[3, x, 8:16, :]
        up[8 * x : 8 * x + 1, :] = combined(f[3, x, 8:9, :], f[0, x, 9:10, :], f[1, x, 9:10, :], f[2, x, 9:10, :])
        dn[8 * x : 8 * x + 8, :] = f[3, x, 0:8, :]
        dn[8 * x + 7 : 8 * x + 8, :] = combined(f[3, x, 7:8, :], f[0, x, 6:7, :], f[1, x, 6:7, :], f[2, x, 6:7, :])
        for k in range(3):
            at = 64 + 18 * x + 6 * k
            up[at : at + 6, :] = f[k, x, 10:16, :]
            dn[at : at + 6, :] = f[k, x, 0:6, :]

    copies[1].wait()
    copies[2].wait()

    def beside(k, y):
        return jnp.concatenate([melt[k, x, y : y + 1, :] for x in range(8)], axis=1)

    m = Y_MELT
    up[m : m + 1, :] = combined(beside(3, 12), beside(0, 13), beside(1, 13), beside(2, 13))
    dn[m + 3 : m + 4, :] = combined(beside(3, 3), beside(0, 2), beside(1, 2), beside(2, 2))
    for j in range(3):
        up[m + 1 + j : m + 2 + j, :] = beside(3, 13 + j)
        dn[m + j : m + 1 + j, :] = beside(3, j)
    for k in range(3):
        for j in range(2):
            at = m + 4 + 2 * k + j
            up[at : at + 1, :] = beside(k, 14 + j)
            dn[at : at + 1, :] = beside(k, j)
    for out in (up, dn):
        out[Y_IDS : Y_IDS + 1, :] = jnp.concatenate([ids[x : x + 1, :].astype(f32) for x in range(8)], axis=1)
        out[Y_IDS + 1 : Y_ROWS, :] = jnp.zeros((Y_ROWS - Y_IDS - 1, 128), f32)


def pack_low(f, ids, zp, row):
    row[...] = jnp.zeros(row.shape, f32)
    row[0:1, :] = jnp.concatenate([ids[x : x + 1, :].astype(f32) for x in range(8)], axis=1)
    for x in range(8):
        zp[16 * x : 16 * x + 16, :] = three(f[0, x], f[1, x], f[2, x])
    for x in range(3):
        zp[128 + 16 * x : 144 + 16 * x, :] = three(f[3, x], f[3, x + 3], f[3, x + 6] if x < 2 else None)


def mobility_of(grain, angles):
    angle = jnp.zeros(grain.shape, f32)
    for g in range(angles.shape[0]):
        angle = jnp.where(grain == float(g), angles[g], angle)
    return [1.0 + 0.6 * jnp.cos(4.0 * angle + 2.0944 * k) for k in range(3)]


def pack_own(scal, angles, f, ids, z1, meltp, x1, zp, mob):
    mob[...] = jnp.zeros(mob.shape, f32)
    for k, row in enumerate(mobility_of(ids[0:1, :], angles)):
        mob[k : k + 1, :] = row
    top = scal[0] == scal[3] - 1
    own = jnp.where(top, meltp[...], z1[...])
    zp[...] = own
    for k in range(4):
        for x in range(8):
            at = 128 * k + 16 * x
            x1[at : at + 16, :] = f[k, x]
    x1[512 : 512 + Z_ROWS, :] = own
    x1[512 + Z_ROWS :, :] = mob[...]


def columns(mo, src, row, x, X, y, Y, n):
    hit = lanes((n, 128)) == 16 * x + y + subs((n, 128))
    for k in range(3):
        value = jnp.sum(jnp.where(hit, src[row + k : row + k + 1, :], 0.0), axis=1, keepdims=True)
        mo[k, X, Y : Y + n, :] = jnp.broadcast_to(0.05 * value, (n, 128))


def own_columns(mob, mown):
    for x in range(8):
        columns(mown, mob, 0, x, x, 0, 0, 16)


def tiles_of(src, base, side, dst):
    for x in range(8):
        dst[3, side, x] = src[base + 8 * x : base + 8 * x + 8, :]
        for k in range(3):
            at = base + 64 + 18 * x + 6 * k
            dst[k, side, x] = jnp.zeros((8, 128), f32)
            dst[k, side, x, 2 - 2 * side : 8 - 2 * side, :] = src[at : at + 6, :]


def unpack_y(lo, hi, yh, z2):
    tiles_of(lo, 0, 0, yh)
    tiles_of(hi, 0, 1, yh)

    def tile(t):
        return lo[8 * t : 8 * t + 8, :] if t < 26 else hi[8 * (t - 26) : 8 * (t - 26) + 8, :]

    for t in range(Z2_TILES):
        z2[8 * t : 8 * t + 8, :] = three(tile(t), tile(t + 18), tile(t + 36) if t + 36 < 52 else None)


def unpack_z(scal, angles, z2, lo, hi, yh, eh, up, dn, moby, flat):
    moby[...] = jnp.zeros(moby.shape, f32)
    for side, src in ((0, lo), (3, hi)):
        for k, row in enumerate(mobility_of(src[Y_IDS : Y_IDS + 1, :], angles)):
            moby[side + k : side + k + 1, :] = row

    for t in range(Z2_TILES):
        tile = z2[8 * t : 8 * t + 8, :]
        for g in range(3):
            if t + 18 * g < 52:
                flat[8 * (t + 18 * g) : 8 * (t + 18 * g) + 8, :] = part(tile, g)
    tiles_of(flat, 0, 0, eh)
    tiles_of(flat, 208, 1, eh)

    @pl.when(scal[0] == scal[3] - 1)
    def _():
        eh[...] = jnp.zeros(eh.shape, f32)
        for side, src in ((0, lo), (1, hi)):
            for x in range(8):
                rows = src[Y_MELT : Y_MELT + 10, :]
                if x:
                    rows = pltpu.roll(src[Y_MELT : Y_MELT + 16, :], 128 - 16 * x, 1)
                eh[3, side, x, 4 - 4 * side : 8 - 4 * side, :] = rows[0:4]
                for k in range(3):
                    eh[k, side, x, 6 - 6 * side : 8 - 6 * side, :] = rows[4 + 2 * k : 6 + 2 * k]

    sub = subs((8, 128))
    for out, col in ((up, lambda dx: 8 - dx), (dn, lambda dx: dx - 1)):

        def corner(src, k, dx):
            if k == 3:
                return jnp.where(sub >= dx, src[3, 0, col(dx)], src[3, 1, col(8 - dx)])
            return jnp.where(sub > dx, src[k, 0, col(dx)], src[k, 1, col(7 - dx)])

        at = 0
        for dx in range(1, 8):
            out[at : at + 8, :] = corner(yh, 3, dx)
            at += 8
        for k in range(3):
            for dx in range(1, 7):
                out[at : at + 8, :] = corner(yh, k, dx)
                at += 8
        for i in range(3):
            out[at : at + 8, :] = three(corner(eh, 3, 1 + i), corner(eh, 3, 4 + i), corner(eh, 3, 7) if i == 0 else None)
            at += 8
        for dx in range(1, 7):
            out[at : at + 8, :] = three(corner(eh, 0, dx), corner(eh, 1, dx), corner(eh, 2, dx))
            at += 8
        out[at : at + 8, :] = moby[...]


def steps(scal, f, zp, mown, x1lo, x1hi, moby, yh, eh, x2lo, x2hi, out, a, b, u, ex, mo):
    gz, s1, s2, top = scal[0], scal[1], scal[2], scal[0] == scal[3] - 1
    planes = scal[3] * 128

    for k in range(4):
        a[k, 8:16, 8:24, 0:128] = f[k]
        for x in range(8):
            at = 128 * k + 16 * x
            a[k, x, 8:24, 0:128] = x1lo[at : at + 16, :]
            a[k, 16 + x, 8:24, 0:128] = x1hi[at : at + 16, :]
            for src, base, X in ((zp, 0, 8), (x1lo, 512, 0), (x1hi, 512, 16)):
                r = base + (16 * x if k < 3 else 128 + 16 * (x % 3))
                ex[k, X + x, 8:24, :] = part(src[r : r + 16, :], k if k < 3 else x // 3)
        for side in range(2):
            a[k, 8:16, 24 * side : 24 * side + 8, 0:128] = yh[k, side]
            ex[k, 8:16, 24 * side : 24 * side + 8, :] = eh[k, side]
    for src, lo_col, hi_col in ((x2lo, lambda d: 8 - d, lambda d: 8 - d), (x2hi, lambda d: 15 + d, lambda d: 15 + d)):
        for k in (3, 0, 1, 2):
            for dx in range(1, 8 if k == 3 else 7):
                at = 8 * (dx - 1) if k == 3 else 56 + 48 * k + 8 * (dx - 1)
                tile = src[at : at + 8, :]
                if k == 3:
                    above = part(src[200 + 8 * ((dx - 1) % 3) : 208 + 8 * ((dx - 1) % 3), :], (dx - 1) // 3)
                    other = 8 - dx
                else:
                    above = part(src[224 + 8 * (dx - 1) : 232 + 8 * (dx - 1), :], k)
                    other = 7 - dx
                a[k, lo_col(dx), 0:8, 0:128] = tile
                a[k, hi_col(other), 24:32, 0:128] = tile
                ex[k, lo_col(dx), 0:8, :] = above
                ex[k, hi_col(other), 24:32, :] = above

    mo[:, 8:16, 8:24, :] = mown[...]
    for x in range(8):
        columns(mo, moby, 0, x, 8 + x, 8, 0, 8)
        columns(mo, moby, 3, x, 8 + x, 0, 24, 8)
        for src, second, X in ((x1lo, x2lo, x), (x1hi, x2hi, 16 + x)):
            if 3 <= X < 21:
                columns(mo, src, 512 + Z_ROWS, x, X, 0, 8, 16)
                columns(mo, second, 272, x, X, 8, 0, 8)
                columns(mo, second, 275, x, X, 0, 24, 8)

    plane = gz * 128 + lanes((1, 256))
    for k in range(4):
        for X in range(24):
            a[k, X, :, 128:256] = jnp.where(plane[:, 128:] < planes, ex[k, X], 0.0)

    first, second = plane[:, :128], plane[:, 128:]

    def one(src, dst, reach, moved, low, high, rows, melt):
        heat = (2.0 * (plane - moved).astype(f32) + 1.0) / planes.astype(f32) - 1.0
        warm = [0.3 * heat - 0.15 * slope for slope in SLOPES]

        def sides(v):
            return (pltpu.roll(v, 1, 0) + pltpu.roll(v, 31, 0)) + (pltpu.roll(v, 1, 1) + pltpu.roll(v, 255, 1))

        def potential(X, _):
            c = src[3, X]
            around = (src[3, X - 1] + src[3, X + 1]) + sides(c)
            u[X] = 1.3 * c - 0.05 * around + (0.3 * src[0, X] - 0.2 * src[1, X] + 0.1 * src[2, X])
            return _

        lax.fori_loop(8 - reach - 1, 16 + reach + 1, potential, 0)

        def update(X, _):
            v = u[X]
            c = src[3, X]
            around = (u[X - 1] + u[X + 1]) + sides(v)
            new = [None] * 4
            new[3] = c + (0.05 * around - 0.3 * v)
            p = [src[k, X] for k in range(3)]
            sq = [w * w for w in p]
            shared = 8.0 + 1.5 * ((sq[0] + sq[1]) + sq[2])
            for k in range(3):
                w = p[k]
                near = (src[k, X - 1] + src[k, X + 1]) + sides(w)
                rate = mo[k, X]
                rate = jnp.concatenate([rate, rate], axis=1)
                grow = w + rate * (near - w * (shared + w * (2.5 * w - 6.0)))
                new[k] = grow - (w - sq[k]) * (warm[k] + 0.3 * SLOPES[k] * c)
            for k in range(4):
                own, above = new[k][rows, :128], new[k][rows, 128:]
                if low is not None:
                    own = jnp.where(first >= low, own, 0.0)
                if melt:
                    above = jnp.where(top, ex[k, X], above)
                if high is not None:
                    above = jnp.where(second < high, above, 0.0)
                dst[k, X, rows, 0:128] = own
                dst[k, X, rows, 128:256] = above
            return _

        lax.fori_loop(8 - reach, 16 + reach, update, 0)

    every = slice(0, 32)
    one(a, b, 6, 0, None, planes, every, False)
    one(b, a, 4, 0, s1, planes + s1, every, True)
    one(a, b, 2, s1, s1, planes + s1, every, False)
    one(b, a, 0, s1, None, None, slice(8, 24), False)

    total = s1 + s2
    lane = lanes((1, 128))
    for k in range(4):
        for x in range(8):
            melt = pltpu.roll(ex[k, 8 + x, 8:24, :], (s1 + 112) % 128, 1)
            above = a[k, 8 + x, 8:24, 128:256]
            above = jnp.where(top & (lane >= s1), melt, above)
            own = pltpu.roll(a[k, 8 + x, 8:24, 0:128], 128 - total, 1)
            above = pltpu.roll(above, 128 - total, 1)
            out[k, x] = jnp.where(lane < 128 - total, own, above)


def kernel(fn, mib, out_shapes, scratch=(), scalars=0, hbm=False):
    def call(*args):
        specs = [pl.BlockSpec(memory_space=pltpu.HBM if hbm else pltpu.VMEM) for _ in args]
        specs[:scalars] = [pl.BlockSpec(memory_space=pltpu.SMEM)] * scalars
        return pl.pallas_call(
            fn,
            in_specs=specs,
            out_specs=[pl.BlockSpec(memory_space=pltpu.VMEM) for _ in out_shapes],
            out_shape=[jax.ShapeDtypeStruct(s, f32) for s in out_shapes],
            scratch_shapes=[pltpu.VMEM(s, f32) if isinstance(s, tuple) else s for s in scratch],
            compiler_params=pltpu.CompilerParams(vmem_limit_bytes=mib if mib > 1000 else mib << 20),
        )(*args)

    return call


def ring(value, axis, by):
    n = lax.axis_size(axis)
    return lax.ppermute(value, axis, [(i, (i + by) % n) for i in range(n)])


def from_above(value):
    n = lax.axis_size("gz")
    return lax.ppermute(value, "gz", [(i, i - 1) for i in range(1, n)])


def melt_above(melt):
    both = jnp.concatenate([melt[0], melt[1], jnp.zeros(melt.shape[1:4] + (ZE - 32,), f32)], axis=-1)
    phases = jnp.pad(jnp.concatenate([both[0], both[1], both[2]], axis=-1).reshape(128, 3 * ZE), ((0, 0), (0, 8)))
    c = jnp.pad(both[3], ((0, 1), (0, 0), (0, 0)))
    solute = jnp.pad(jnp.concatenate([c[0:3], c[3:6], c[6:9]], axis=-1).reshape(48, 3 * ZE), ((0, 0), (0, 8)))
    return jnp.concatenate([phases, solute], axis=0)


def body(fields, grain_ids, grain_angle, melt_planes, shifts):
    inputs = [fields.shape, pltpu.VMEM(grain_ids.shape, jnp.int32), melt_planes.shape[1:], pltpu.SemaphoreType.DMA((3,))]
    up, dn = kernel(pack_first, 4, [(Y_ROWS, 128)] * 2, inputs, hbm=True)(fields, grain_ids, melt_planes)
    ylo = ring(up, "gy", 1)
    yhi = ring(dn, "gy", -1)
    low, ids = kernel(pack_low, 2, [(Z_ROWS, 128), (8, 128)])(fields, grain_ids)
    z1 = from_above(low)
    gz = lax.axis_index("gz").astype(jnp.int32)
    scal = jnp.stack([gz, shifts[0], shifts[1], jnp.int32(lax.axis_size("gz"))])
    x1, zp, mob = kernel(pack_own, 2, [(X1_ROWS, 128), (Z_ROWS, 128), (8, 128)], scalars=2)(
        scal, grain_angle, fields, ids, z1, melt_above(melt_planes)
    )
    (mown,) = kernel(own_columns, 2, [(3, 8, 16, 128)])(mob)
    x1lo = ring(x1, "gx", 1)
    x1hi = ring(x1, "gx", -1)
    tiles = (4, 2, 8, 8, 128)
    yh, z2 = kernel(unpack_y, 2, [tiles, (8 * Z2_TILES, 128)])(ylo, yhi)
    z2 = from_above(z2)
    shapes = [tiles, (X2_ROWS, 128), (X2_ROWS, 128), (8, 128)]
    eh, up2, dn2, moby = kernel(unpack_z, 4, shapes, [(416, 128)], scalars=2)(scal, grain_angle, z2, ylo, yhi, yh)
    x2lo = ring(up2, "gx", 1)
    x2hi = ring(dn2, "gx", -1)
    block = (4, 24, 32, 256)
    (out,) = kernel(
        steps, 24, [(4, 8, 16, 128)], [block, block, block[1:], (4, 24, 32, 128), (3, 24, 32, 128)], scalars=1
    )(scal, fields, zp, mown, x1lo, x1hi, moby, yh, eh, x2lo, x2hi)
    return out


def solution(mesh):
    placed = (P(None, "gx", "gy", "gz"), P("gx", "gy"), P(), P(None, None, "gx", "gy", None), P())
    return jax.shard_map(
        body, mesh=mesh, in_specs=placed, out_specs=P(None, "gx", "gy", "gz"), check_vma=False
    )
```

time: 347 us -> 95.4 us (0.27)
  the two profiles are of different devices: /device:TPU:203 before, /device:TPU:6 now
where the time goes in v1:
time: 95.4 us; the launch traced here: 95 us
  starting transfers between devices  48.7 us (51%)
  waiting for transfers between devices  22.6 us (24%)
  Pallas kernels  19 us (20%)
  local copies, waits for them, and re-layouts  4.14 us (4%)
    ppermute x6, starting transfers between devices, ring(): return lax.ppermute(value, axis, [(i, (i + by) % n) for i in range(n)])  46.1 us
    ppermute x6, waiting for transfers between devices, ring(): return lax.ppermute(value, axis, [(i, (i + by) % n) for i in range(n)])  20.7 us
    pallas_call x7, Pallas kernels, call(): pl.pallas_call(fn, in_specs=specs, out_specs=[pl.BlockSpec(memory_space=p...  19 us
    unnamed x14, local copies, waits for them, and re-layouts  2.96 us
    ppermute x2, starting transfers between devices, from_above(): return lax.ppermute(value, 'gz', [(i, i - 1) for i in range(1, n)])  2.58 us
  transfers between devices with their start and end apart: 8, of which 5 were waited for; matrix products, arithmetic and copies ran while one was open for 2% of the time, Pallas kernels for 2%

profile of v1, /device:TPU:6, one launch (start us, length us, event | category | flops | bytes accessed | tf_op | source)
XLA Modules:
  0.0 95.0 jit_solution(1196037743530441017)
XLA Ops:
  0.0 0.9 copy-done
  1.0 0.7 copy-done.3
  1.6 0.1 shard_map.55
  1.8 1.3 %collective-permute-start = (f32[176,128]{1,0:T(8,128)S(1)}, f32[176,128]{1,0:T(8,128)S(1)}, u32[]{:S(2)}, u32[]{:S(2)}) collective-permute-start(f32[176,128]{1,0:T(8,128)S(1)} %get-tuple-element.19), channel_id=1, source_target_pairs={{1,0},{2,1},{3,2},{4,3},{5,4},{6,5},{7,6},{8,7},{9,8},{10,9},{11,1... | collective-permute-start | bytes 270344 | tf_op jit(solution)/shard_map/ppermute | solution.py:333
  3.1 1.1 %slice_bitcast_fusion.1 = (f32[4,8,16,16]{3,2,1,0:T(8,128)S(1)}, f32[4,8,16,16]{3,2,1,0:T(8,128)S(1)}) fusion(f32[2,4,8,16,16]{4,3,2,1,0:T(8,128)} %melt_in.1), kind=kLoop, calls=%fused_computation.2 | loop fusion | bytes 131072 | tf_op jit(solution)/shard_map/squeeze | solution.py:337
  4.1 0.1 pad.25.clone
  4.2 0.1 maximum_maximum_fusion
  4.4 0.1 select_maximum_fusion
  4.5 0.1 select_maximum_fusion.2
  4.7 0.0 copy-start.6
  4.7 0.6 copy-done.6
  5.3 0.1 pad_add_fusion.scal
  5.4 0.0 copy-done.1
  5.4 0.6 copy-done.5
  6.1 0.6 shard_map.56
  6.7 15.0 %collective-permute-start.1 = (f32[696,128]{1,0:T(8,128)S(1)}, f32[696,128]{1,0:T(8,128)S(1)}, u32[]{:S(2)}, u32[]{:S(2)}) collective-permute-start(f32[696,128]{1,0:T(8,128)S(1)} %get-tuple-element.22), channel_id=1, source_target_pairs={{0,256},{256,512},{512,768},{768,0},{1,257},{257,513},{513,769},{7... | collective-permute-start | bytes 1069064 | tf_op jit(solution)/shard_map/ppermute | solution.py:328
  21.7 1.9 %collective-permute-start.2 = (f32[696,128]{1,0:T(8,128)S(1)}, f32[696,128]{1,0:T(8,128)S(1)}, u32[]{:S(2)}, u32[]{:S(2)}) collective-permute-start(f32[696,128]{1,0:T(8,128)S(1)} %get-tuple-element.22), channel_id=1, source_target_pairs={{0,768},{256,0},{512,256},{768,512},{1,769},{257,1},{513,257},{769... | collective-permute-start | bytes 1069064 | tf_op jit(solution)/shard_map/ppermute | solution.py:328
  23.7 0.4 shard_map.58
  24.1 8.3 %collective-permute-start.3 = (f32[224,128]{1,0:T(8,128)S(1)}, f32[224,128]{1,0:T(8,128)S(1)}, u32[]{:S(2)}, u32[]{:S(2)}) collective-permute-start(f32[224,128]{1,0:T(8,128)S(1)} %get-tuple-element.23), channel_id=1, source_target_pairs={{0,16},{16,32},{32,48},{48,64},{64,80},{80,96},{96,112},{112,128},... | collective-permute-start | bytes 344072 | tf_op jit(solution)/shard_map/ppermute | solution.py:328
  32.3 8.4 %collective-permute-start.4 = (f32[224,128]{1,0:T(8,128)S(1)}, f32[224,128]{1,0:T(8,128)S(1)}, u32[]{:S(2)}, u32[]{:S(2)}) collective-permute-start(f32[224,128]{1,0:T(8,128)S(1)} %get-tuple-element.24), channel_id=1, source_target_pairs={{0,240},{16,0},{32,16},{48,32},{64,48},{80,64},{96,80},{112,96},{1... | collective-permute-start | bytes 344072 | tf_op jit(solution)/shard_map/ppermute | solution.py:328
  40.7 2.2 %collective-permute-done.3.lo = f32[224,128]{1,0:T(8,128)S(1)} collective-permute-done((f32[224,128]{1,0:T(8,128)S(1)}, f32[224,128]{1,0:T(8,128)S(1)}, u32[]{:S(2)}, u32[]{:S(2)}) %collective-permute-start.3) | collective-permute-done | bytes 114720 | tf_op jit(solution)/shard_map/ppermute | solution.py:328
  42.9 12.0 %collective-permute-done.4.hi = f32[224,128]{1,0:T(8,128)S(1)} collective-permute-done((f32[224,128]{1,0:T(8,128)S(1)}, f32[224,128]{1,0:T(8,128)S(1)}, u32[]{:S(2)}, u32[]{:S(2)}) %collective-permute-start.4) | collective-permute-done | bytes 114720 | tf_op jit(solution)/shard_map/ppermute | solution.py:328
  54.9 0.1 shard_map.59
  55.0 1.3 %collective-permute-start.5 = (f32[144,128]{1,0:T(8,128)S(1)}, f32[144,128]{1,0:T(8,128)S(1)}, u32[]{:S(2)}, u32[]{:S(2)}) collective-permute-start(f32[144,128]{1,0:T(8,128)S(1)} %get-tuple-element.25), channel_id=1, source_target_pairs={{1,0},{2,1},{3,2},{4,3},{5,4},{6,5},{7,6},{8,7},{9,8},{10,9},{11,1... | collective-permute-start | bytes 221192 | tf_op jit(solution)/shard_map/ppermute | solution.py:333
  56.3 1.9 %collective-permute-done.5.z2 = f32[144,128]{1,0:T(8,128)S(1)} collective-permute-done((f32[144,128]{1,0:T(8,128)S(1)}, f32[144,128]{1,0:T(8,128)S(1)}, u32[]{:S(2)}, u32[]{:S(2)}) %collective-permute-start.5) | collective-permute-done | bytes 73760 | tf_op jit(solution)/shard_map/ppermute | solution.py:333
  58.2 0.8 shard_map.60
  59.0 10.6 %collective-permute-start.6 = (f32[280,128]{1,0:T(8,128)S(1)}, f32[280,128]{1,0:T(8,128)S(1)}, u32[]{:S(2)}, u32[]{:S(2)}) collective-permute-start(f32[280,128]{1,0:T(8,128)S(1)} %get-tuple-element.29), channel_id=1, source_target_pairs={{0,256},{256,512},{512,768},{768,0},{1,257},{257,513},{513,769},{7... | collective-permute-start | bytes 430088 | tf_op jit(solution)/shard_map/ppermute | solution.py:328
  69.6 1.9 %collective-permute-start.7 = (f32[280,128]{1,0:T(8,128)S(1)}, f32[280,128]{1,0:T(8,128)S(1)}, u32[]{:S(2)}, u32[]{:S(2)}) collective-permute-start(f32[280,128]{1,0:T(8,128)S(1)} %get-tuple-element.30), channel_id=1, source_target_pairs={{0,768},{256,0},{512,256},{768,512},{1,769},{257,1},{513,257},{769... | collective-permute-start | bytes 430088 | tf_op jit(solution)/shard_map/ppermute | solution.py:328
  71.5 0.1 shard_map.57.mown
  71.6 1.3 %collective-permute-done.6.x2lo = f32[280,128]{1,0:T(8,128)S(1)} collective-permute-done((f32[280,128]{1,0:T(8,128)S(1)}, f32[280,128]{1,0:T(8,128)S(1)}, u32[]{:S(2)}, u32[]{:S(2)}) %collective-permute-start.6) | collective-permute-done | bytes 143392 | tf_op jit(solution)/shard_map/ppermute | solution.py:328
  72.9 5.3 %collective-permute-done.7.x2hi = f32[280,128]{1,0:T(8,128)S(1)} collective-permute-done((f32[280,128]{1,0:T(8,128)S(1)}, f32[280,128]{1,0:T(8,128)S(1)}, u32[]{:S(2)}, u32[]{:S(2)}) %collective-permute-start.7) | collective-permute-done | bytes 143392 | tf_op jit(solution)/shard_map/ppermute | solution.py:328
  78.2 16.8 %shard_map.61 = f32[4,8,16,128]{3,2,1,0:T(8,128)} custom-call(s32[4]{0:T(128)S(1)} %pad_add_fusion.scal, f32[4,8,16,128]{3,2,1,0:T(8,128)S(1)} %copy-done.1, f32[176,128]{1,0:T(8,128)S(1)} %get-tuple-element.20.zp, f32[3,8,16,128]{3,2,1,0:T(8,128)S(1)} %shard_map.57.mown, f32[696,128]{1,0:T(8,128)S(1)} %collective-permute-done.1.x1lo, ...), custom_call_target="tpu_custom_call" | custom-call | tf_op jit(solution)/shard_map/pallas_call | solution.py:314
  (16 shorter events, 0.1 us)
Async XLA Ops:
  0.0 0.9 copy-start
  1.0 0.7 copy-start.3
  1.8 3.6 %collective-permute-start = (f32[176,128]{1,0:T(8,128)S(1)}, f32[176,128]{1,0:T(8,128)S(1)}, u32[]{:S(2)}, u32[]{:S(2)}) collective-permute-start(f32[176,128]{1,0:T(8,128)S(1)} %get-tuple-element.19), channel_id=1, source_target_pairs={{1,0},{2,1},{3,2},{4,3},{5,4},{6,5},{7,6},{8,7},{9,8},{10,9},{11,1... | collective-permute-start | bytes 270344 | tf_op jit(solution)/shard_map/ppermute | solution.py:333
  4.4 19.3 %copy-start.2 = (f32[2,4,8,16,16]{4,3,2,1,0:T(8,128)S(1)}, f32[2,4,8,16,16]{4,3,2,1,0:T(8,128)}, u32[]{:S(2)}) copy-start(f32[2,4,8,16,16]{4,3,2,1,0:T(8,128)} %melt_in.1) | copy-start | bytes 196612
  4.4 1.0 %copy-start.1 = (f32[4,8,16,128]{3,2,1,0:T(8,128)S(1)}, f32[4,8,16,128]{3,2,1,0:T(8,128)}, u32[]{:S(2)}) copy-start(f32[4,8,16,128]{3,2,1,0:T(8,128)} %f.5) | copy-start | bytes 786436
  4.7 0.7 copy-start.6
  5.4 0.7 copy-start.5
  6.1 17.6 %copy-start.4 = (s32[8,16]{1,0:T(8,128)S(1)}, s32[8,16]{1,0:T(8,128)}, u32[]{:S(2)}) copy-start(s32[8,16]{1,0:T(8,128)} %ids_in.1) | copy-start | bytes 1540
  6.7 71.5 %collective-permute-start.1 = (f32[696,128]{1,0:T(8,128)S(1)}, f32[696,128]{1,0:T(8,128)S(1)}, u32[]{:S(2)}, u32[]{:S(2)}) collective-permute-start(f32[696,128]{1,0:T(8,128)S(1)} %get-tuple-element.22), channel_id=1, source_target_pairs={{0,256},{256,512},{512,768},{768,0},{1,257},{257,513},{513,769},{7... | collective-permute-start | bytes 1069064 | tf_op jit(solution)/shard_map/ppermute | solution.py:328
  21.7 56.5 %collective-permute-start.2 = (f32[696,128]{1,0:T(8,128)S(1)}, f32[696,128]{1,0:T(8,128)S(1)}, u32[]{:S(2)}, u32[]{:S(2)}) collective-permute-start(f32[696,128]{1,0:T(8,128)S(1)} %get-tuple-element.22), channel_id=1, source_target_pairs={{0,768},{256,0},{512,256},{768,512},{1,769},{257,1},{513,257},{769... | collective-permute-start | bytes 1069064 | tf_op jit(solution)/shard_map/ppermute | solution.py:328
  24.1 18.9 %collective-permute-start.3 = (f32[224,128]{1,0:T(8,128)S(1)}, f32[224,128]{1,0:T(8,128)S(1)}, u32[]{:S(2)}, u32[]{:S(2)}) collective-permute-start(f32[224,128]{1,0:T(8,128)S(1)} %get-tuple-element.23), channel_id=1, source_target_pairs={{0,16},{16,32},{32,48},{48,64},{64,80},{80,96},{96,112},{112,128},... | collective-permute-start | bytes 344072 | tf_op jit(solution)/shard_map/ppermute | solution.py:328
  32.3 22.5 %collective-permute-start.4 = (f32[224,128]{1,0:T(8,128)S(1)}, f32[224,128]{1,0:T(8,128)S(1)}, u32[]{:S(2)}, u32[]{:S(2)}) collective-permute-start(f32[224,128]{1,0:T(8,128)S(1)} %get-tuple-element.24), channel_id=1, source_target_pairs={{0,240},{16,0},{32,16},{48,32},{64,48},{80,64},{96,80},{112,96},{1... | collective-permute-start | bytes 344072 | tf_op jit(solution)/shard_map/ppermute | solution.py:328
  55.0 3.2 %collective-permute-start.5 = (f32[144,128]{1,0:T(8,128)S(1)}, f32[144,128]{1,0:T(8,128)S(1)}, u32[]{:S(2)}, u32[]{:S(2)}) collective-permute-start(f32[144,128]{1,0:T(8,128)S(1)} %get-tuple-element.25), channel_id=1, source_target_pairs={{1,0},{2,1},{3,2},{4,3},{5,4},{6,5},{7,6},{8,7},{9,8},{10,9},{11,1... | collective-permute-start | bytes 221192 | tf_op jit(solution)/shard_map/ppermute | solution.py:333
  59.0 13.9 %collective-permute-start.6 = (f32[280,128]{1,0:T(8,128)S(1)}, f32[280,128]{1,0:T(8,128)S(1)}, u32[]{:S(2)}, u32[]{:S(2)}) collective-permute-start(f32[280,128]{1,0:T(8,128)S(1)} %get-tuple-element.29), channel_id=1, source_target_pairs={{0,256},{256,512},{512,768},{768,0},{1,257},{257,513},{513,769},{7... | collective-permute-start | bytes 430088 | tf_op jit(solution)/shard_map/ppermute | solution.py:328
  69.6 8.6 %collective-permute-start.7 = (f32[280,128]{1,0:T(8,128)S(1)}, f32[280,128]{1,0:T(8,128)S(1)}, u32[]{:S(2)}, u32[]{:S(2)}) collective-permute-start(f32[280,128]{1,0:T(8,128)S(1)} %get-tuple-element.30), channel_id=1, source_target_pairs={{0,768},{256,0},{512,256},{768,512},{1,769},{257,1},{513,257},{769... | collective-permute-start | bytes 430088 | tf_op jit(solution)/shard_map/ppermute | solution.py:328

commit v2 on v1

--- a/solution.py
+++ b/solution.py
@@ -13,9 +13,9 @@
 Y_ROWS = 224
 Y_MELT, Y_IDS = 208, 218
 Z_ROWS = 176
-X1_ROWS = 512 + Z_ROWS + 8
 Z2_TILES = 18
-X2_ROWS = 280
+X2_ZP, X2_MOB = 272, 272 + Z_ROWS
+X2_ROWS = X2_MOB + 16
 
 
 def lanes(shape):
@@ -81,9 +81,8 @@
         out[Y_IDS + 1 : Y_ROWS, :] = jnp.zeros((Y_ROWS - Y_IDS - 1, 128), f32)
 
 
-def pack_low(f, ids, zp, row):
-    row[...] = jnp.zeros(row.shape, f32)
-    row[0:1, :] = jnp.concatenate([ids[x : x + 1, :].astype(f32) for x in range(8)], axis=1)
+def pack_low(f, zp, own):
+    own[...] = f[...]
     for x in range(8):
         zp[16 * x : 16 * x + 16, :] = three(f[0, x], f[1, x], f[2, x])
     for x in range(3):
@@ -97,21 +96,6 @@
     return [1.0 + 0.6 * jnp.cos(4.0 * angle + 2.0944 * k) for k in range(3)]
 
 
-def pack_own(scal, angles, f, ids, z1, meltp, x1, zp, mob):
-    mob[...] = jnp.zeros(mob.shape, f32)
-    for k, row in enumerate(mobility_of(ids[0:1, :], angles)):
-        mob[k : k + 1, :] = row
-    top = scal[0] == scal[3] - 1
-    own = jnp.where(top, meltp[...], z1[...])
-    zp[...] = own
-    for k in range(4):
-        for x in range(8):
-            at = 128 * k + 16 * x
-            x1[at : at + 16, :] = f[k, x]
-    x1[512 : 512 + Z_ROWS, :] = own
-    x1[512 + Z_ROWS :, :] = mob[...]
-
-
 def columns(mo, src, row, x, X, y, Y, n):
     hit = lanes((n, 128)) == 16 * x + y + subs((n, 128))
     for k in range(3):
@@ -119,7 +103,11 @@
         mo[k, X, Y : Y + n, :] = jnp.broadcast_to(0.05 * value, (n, 128))
 
 
-def own_columns(mob, mown):
+def own_columns(angles, ids, mob, mown):
+    grain = jnp.concatenate([ids[x : x + 1, :].astype(f32) for x in range(8)], axis=1)
+    mob[...] = jnp.zeros(mob.shape, f32)
+    for k, row in enumerate(mobility_of(grain, angles)):
+        mob[k : k + 1, :] = row
     for x in range(8):
         columns(mown, mob, 0, x, x, 0, 0, 16)
 
@@ -144,7 +132,9 @@
         z2[8 * t : 8 * t + 8, :] = three(tile(t), tile(t + 18), tile(t + 36) if t + 36 < 52 else None)
 
 
-def unpack_z(scal, angles, z2, lo, hi, yh, eh, up, dn, moby, flat):
+def unpack_z(scal, angles, z1, meltp, mob, z2, lo, hi, yh, zp, eh, up, dn, moby, flat):
+    top = scal[0] == scal[3] - 1
+    zp[...] = jnp.where(top, meltp[...], z1[...])
     moby[...] = jnp.zeros(moby.shape, f32)
     for side, src in ((0, lo), (3, hi)):
         for k, row in enumerate(mobility_of(src[Y_IDS : Y_IDS + 1, :], angles)):
@@ -158,7 +148,7 @@
     tiles_of(flat, 0, 0, eh)
     tiles_of(flat, 208, 1, eh)
 
-    @pl.when(scal[0] == scal[3] - 1)
+    @pl.when(top)
     def _():
         eh[...] = jnp.zeros(eh.shape, f32)
         for side, src in ((0, lo), (1, hi)):
@@ -192,24 +182,25 @@
         for dx in range(1, 7):
             out[at : at + 8, :] = three(corner(eh, 0, dx), corner(eh, 1, dx), corner(eh, 2, dx))
             at += 8
-        out[at : at + 8, :] = moby[...]
-
-
-def steps(scal, f, zp, mown, x1lo, x1hi, moby, yh, eh, x2lo, x2hi, out, a, b, u, ex, mo):
+        out[X2_ZP:X2_MOB, :] = zp[...]
+        out[X2_MOB : X2_MOB + 8, :] = moby[...]
+        out[X2_MOB + 8 :, :] = mob[...]
+
+
+def steps(scal, f, zp, mown, x1lo, x1hi, moby, yh, eh, x2lo, x2hi, out, a0, a1, b0, b1, u0, u1, ex, mo):
     gz, s1, s2, top = scal[0], scal[1], scal[2], scal[0] == scal[3] - 1
     planes = scal[3] * 128
 
     for k in range(4):
-        a[k, 8:16, 8:24, 0:128] = f[k]
+        a0[k, 8:16, 8:24, :] = f[k]
         for x in range(8):
-            at = 128 * k + 16 * x
-            a[k, x, 8:24, 0:128] = x1lo[at : at + 16, :]
-            a[k, 16 + x, 8:24, 0:128] = x1hi[at : at + 16, :]
-            for src, base, X in ((zp, 0, 8), (x1lo, 512, 0), (x1hi, 512, 16)):
+            a0[k, x, 8:24, :] = x1lo[k, x]
+            a0[k, 16 + x, 8:24, :] = x1hi[k, x]
+            for src, base, X in ((zp, 0, 8), (x2lo, X2_ZP, 0), (x2hi, X2_ZP, 16)):
                 r = base + (16 * x if k < 3 else 128 + 16 * (x % 3))
                 ex[k, X + x, 8:24, :] = part(src[r : r + 16, :], k if k < 3 else x // 3)
         for side in range(2):
-            a[k, 8:16, 24 * side : 24 * side + 8, 0:128] = yh[k, side]
+            a0[k, 8:16, 24 * side : 24 * side + 8, :] = yh[k, side]
             ex[k, 8:16, 24 * side : 24 * side + 8, :] = eh[k, side]
     for src, lo_col, hi_col in ((x2lo, lambda d: 8 - d, lambda d: 8 - d), (x2hi, lambda d: 15 + d, lambda d: 15 + d)):
         for k in (3, 0, 1, 2):
@@ -222,8 +213,8 @@
                 else:
                     above = part(src[224 + 8 * (dx - 1) : 232 + 8 * (dx - 1), :], k)
                     other = 7 - dx
-                a[k, lo_col(dx), 0:8, 0:128] = tile
-                a[k, hi_col(other), 24:32, 0:128] = tile
+                a0[k, lo_col(dx), 0:8, :] = tile
+                a0[k, hi_col(other), 24:32, :] = tile
                 ex[k, lo_col(dx), 0:8, :] = above
                 ex[k, hi_col(other), 24:32, :] = above
 
@@ -231,80 +222,101 @@
     for x in range(8):
         columns(mo, moby, 0, x, 8 + x, 8, 0, 8)
         columns(mo, moby, 3, x, 8 + x, 0, 24, 8)
-        for src, second, X in ((x1lo, x2lo, x), (x1hi, x2hi, 16 + x)):
+        for src, X in ((x2lo, x), (x2hi, 16 + x)):
             if 3 <= X < 21:
-                columns(mo, src, 512 + Z_ROWS, x, X, 0, 8, 16)
-                columns(mo, second, 272, x, X, 8, 0, 8)
-                columns(mo, second, 275, x, X, 0, 24, 8)
-
-    plane = gz * 128 + lanes((1, 256))
+                columns(mo, src, X2_MOB + 8, x, X, 0, 8, 16)
+                columns(mo, src, X2_MOB, x, X, 8, 0, 8)
+                columns(mo, src, X2_MOB + 3, x, X, 0, 24, 8)
+
+    lane = lanes((8, 128))
+    first = gz * 128 + lane
+    second = first + 128
     for k in range(4):
         for X in range(24):
-            a[k, X, :, 128:256] = jnp.where(plane[:, 128:] < planes, ex[k, X], 0.0)
-
-    first, second = plane[:, :128], plane[:, 128:]
-
-    def one(src, dst, reach, moved, low, high, rows, melt):
-        heat = (2.0 * (plane - moved).astype(f32) + 1.0) / planes.astype(f32) - 1.0
-        warm = [0.3 * heat - 0.15 * slope for slope in SLOPES]
-
-        def sides(v):
-            return (pltpu.roll(v, 1, 0) + pltpu.roll(v, 31, 0)) + (pltpu.roll(v, 1, 1) + pltpu.roll(v, 255, 1))
-
-        def potential(X, _):
-            c = src[3, X]
-            around = (src[3, X - 1] + src[3, X + 1]) + sides(c)
-            u[X] = 1.3 * c - 0.05 * around + (0.3 * src[0, X] - 0.2 * src[1, X] + 0.1 * src[2, X])
-            return _
-
-        lax.fori_loop(8 - reach - 1, 16 + reach + 1, potential, 0)
-
-        def update(X, _):
-            v = u[X]
-            c = src[3, X]
-            around = (u[X - 1] + u[X + 1]) + sides(v)
-            new = [None] * 4
-            new[3] = c + (0.05 * around - 0.3 * v)
-            p = [src[k, X] for k in range(3)]
-            sq = [w * w for w in p]
-            shared = 8.0 + 1.5 * ((sq[0] + sq[1]) + sq[2])
-            for k in range(3):
-                w = p[k]
-                near = (src[k, X - 1] + src[k, X + 1]) + sides(w)
-                rate = mo[k, X]
-                rate = jnp.concatenate([rate, rate], axis=1)
-                grow = w + rate * (near - w * (shared + w * (2.5 * w - 6.0)))
-                new[k] = grow - (w - sq[k]) * (warm[k] + 0.3 * SLOPES[k] * c)
-            for k in range(4):
-                own, above = new[k][rows, :128], new[k][rows, 128:]
-                if low is not None:
-                    own = jnp.where(first >= low, own, 0.0)
-                if melt:
-                    above = jnp.where(top, ex[k, X], above)
-                if high is not None:
-                    above = jnp.where(second < high, above, 0.0)
-                dst[k, X, rows, 0:128] = own
-                dst[k, X, rows, 128:256] = above
-            return _
-
-        lax.fori_loop(8 - reach, 16 + reach, update, 0)
-
-    every = slice(0, 32)
-    one(a, b, 6, 0, None, planes, every, False)
-    one(b, a, 4, 0, s1, planes + s1, every, True)
-    one(a, b, 2, s1, s1, planes + s1, every, False)
-    one(b, a, 0, s1, None, None, slice(8, 24), False)
+            for s in range(0, 32, 8):
+                a1[k, X, s : s + 8, :] = jnp.where(second < planes, ex[k, X, s : s + 8, :], 0.0)
+
+    def beside_z(m, e):
+        m1, e1, m9, e9 = pltpu.roll(m, 1, 1), pltpu.roll(e, 1, 1), pltpu.roll(m, 127, 1), pltpu.roll(e, 127, 1)
+        return m1 + jnp.where(lane == 127, e9, m9), jnp.where(lane == 0, m1, e1) + e9
+
+    def beside_xy(ref, pre, X, s, v):
+        low = pltpu.roll(v, 1, 0) if s == 0 else ref[(*pre, X, slice(s - 1, s + 7))]
+        across = ref[(*pre, X - 1, slice(s, s + 8))] + ref[(*pre, X + 1, slice(s, s + 8))]
+        return across + (low + ref[(*pre, X, slice(s + 1, s + 9))])
+
+    def both(refs, pre, X, s):
+        m, e = refs[0][(*pre, X, slice(s, s + 8))], refs[1][(*pre, X, slice(s, s + 8))]
+        zm, ze = beside_z(m, e)
+        return (m, beside_xy(refs[0], pre, X, s, m) + zm), (e, beside_xy(refs[1], pre, X, s, e) + ze)
+
+    def one(src, dst, reach, moved, low, high, melt, u_tiles, tiles):
+        warm = []
+        for plane in (first, second):
+            heat = (2.0 * (plane - moved).astype(f32) + 1.0) / planes.astype(f32) - 1.0
+            warm.append([0.3 * heat - 0.15 * slope for slope in SLOPES])
+
+        def potential(X, s):
+            for half, (c, around) in enumerate(both(src, (3,), X, s)):
+                p = [src[half][k, X, s : s + 8, :] for k in range(3)]
+                value = (1.3 * c - 0.05 * around) + (0.3 * p[0] - 0.2 * p[1] + 0.1 * p[2])
+                (u0, u1)[half][X, s : s + 8, :] = value
+
+        def update(X, s):
+            rows = slice(s, s + 8)
+            flow = both((u0, u1), (), X, s)
+            phases = [both(src, (k,), X, s) for k in range(3)]
+            rates = [mo[k, X, rows, :] for k in range(3)]
+            for half in range(2):
+                c = src[half][3, X, rows, :]
+                v, around = flow[half]
+                new = [None, None, None, c + (0.05 * around - 0.3 * v)]
+                sq = [w * w for w, _ in (p[half] for p in phases)]
+                shared = 8.0 + 1.5 * ((sq[0] + sq[1]) + sq[2])
+                for k in range(3):
+                    w, near = phases[k][half]
+                    grow = w + rates[k] * (near - w * (shared + w * (2.5 * w - 6.0)))
+                    new[k] = grow - (w - sq[k]) * (warm[half][k] + 0.3 * SLOPES[k] * c)
+                for k in range(4):
+                    value = new[k]
+                    if half == 0 and low is not None:
+                        value = jnp.where(first >= low, value, 0.0)
+                    if half == 1 and melt:
+                        value = jnp.where(top, ex[k, X, rows, :], value)
+                    if half == 1 and high is not None:
+                        value = jnp.where(second < high, value, 0.0)
+                    dst[half][k, X, rows, :] = value
+
+        for X in range(7 - reach, 10 - reach):
+            for s in u_tiles:
+                potential(X, s)
+
+        def row(X, carry):
+            for ahead in u_tiles:
+                potential(X + 2, ahead)
+            for s in tiles:
+                update(X, s)
+            return carry
+
+        lax.fori_loop(8 - reach, 16 + reach, row, 0, unroll=4)
+
+    a, b = (a0, a1), (b0, b1)
+    every = (0, 8, 16, 24)
+    one(a, b, 6, 0, None, planes, False, every, every)
+    one(b, a, 4, 0, s1, planes + s1, True, every, (4, 12, 20))
+    one(a, b, 2, s1, s1, planes + s1, False, (5, 13, 21), (6, 14, 22))
+    one(b, a, 0, s1, None, None, False, (7, 15, 23), (8, 16))
 
     total = s1 + s2
-    lane = lanes((1, 128))
     for k in range(4):
         for x in range(8):
-            melt = pltpu.roll(ex[k, 8 + x, 8:24, :], (s1 + 112) % 128, 1)
-            above = a[k, 8 + x, 8:24, 128:256]
-            above = jnp.where(top & (lane >= s1), melt, above)
-            own = pltpu.roll(a[k, 8 + x, 8:24, 0:128], 128 - total, 1)
-            above = pltpu.roll(above, 128 - total, 1)
-            out[k, x] = jnp.where(lane < 128 - total, own, above)
+            for s in (0, 8):
+                rows = slice(8 + s, 16 + s)
+                melt = pltpu.roll(ex[k, 8 + x, rows, :], (s1 + 112) % 128, 1)
+                above = jnp.where(top & (lane >= s1), melt, a1[k, 8 + x, rows, :])
+                own = pltpu.roll(a0[k, 8 + x, rows, :], 128 - total, 1)
+                above = pltpu.roll(above, 128 - total, 1)
+                out[k, x, s : s + 8, :] = jnp.where(lane < 128 - total, own, above)
 
 
 def kernel(fn, mib, out_shapes, scratch=(), scalars=0, hbm=False):
@@ -343,30 +355,31 @@
 
 def body(fields, grain_ids, grain_angle, melt_planes, shifts):
     inputs = [fields.shape, pltpu.VMEM(grain_ids.shape, jnp.int32), melt_planes.shape[1:], pltpu.SemaphoreType.DMA((3,))]
-    up, dn = kernel(pack_first, 4, [(Y_ROWS, 128)] * 2, inputs, hbm=True)(fields, grain_ids, melt_planes)
+    up, dn = kernel(pack_first, 4, [(Y_ROWS, 128)] * 2, inputs, hbm=True)(
+        fields, pltpu.with_memory_space_constraint(grain_ids, pltpu.HBM), pltpu.with_memory_space_constraint(melt_planes, pltpu.HBM)
+    )
     ylo = ring(up, "gy", 1)
     yhi = ring(dn, "gy", -1)
-    low, ids = kernel(pack_low, 2, [(Z_ROWS, 128), (8, 128)])(fields, grain_ids)
+    x1lo = ring(fields, "gx", 1)
+    x1hi = ring(fields, "gx", -1)
+    low, own = kernel(pack_low, 2, [(Z_ROWS, 128), fields.shape])(fields)
     z1 = from_above(low)
     gz = lax.axis_index("gz").astype(jnp.int32)
     scal = jnp.stack([gz, shifts[0], shifts[1], jnp.int32(lax.axis_size("gz"))])
-    x1, zp, mob = kernel(pack_own, 2, [(X1_ROWS, 128), (Z_ROWS, 128), (8, 128)], scalars=2)(
-        scal, grain_angle, fields, ids, z1, melt_above(melt_planes)
-    )
-    (mown,) = kernel(own_columns, 2, [(3, 8, 16, 128)])(mob)
-    x1lo = ring(x1, "gx", 1)
-    x1hi = ring(x1, "gx", -1)
+    mob, mown = kernel(own_columns, 2, [(8, 128), (3, 8, 16, 128)], scalars=1)(grain_angle, grain_ids)
     tiles = (4, 2, 8, 8, 128)
     yh, z2 = kernel(unpack_y, 2, [tiles, (8 * Z2_TILES, 128)])(ylo, yhi)
     z2 = from_above(z2)
-    shapes = [tiles, (X2_ROWS, 128), (X2_ROWS, 128), (8, 128)]
-    eh, up2, dn2, moby = kernel(unpack_z, 4, shapes, [(416, 128)], scalars=2)(scal, grain_angle, z2, ylo, yhi, yh)
+    shapes = [(Z_ROWS, 128), tiles, (X2_ROWS, 128), (X2_ROWS, 128), (8, 128)]
+    zp, eh, up2, dn2, moby = kernel(unpack_z, 4, shapes, [(416, 128)], scalars=2)(
+        scal, grain_angle, z1, melt_above(melt_planes), mob, z2, ylo, yhi, yh
+    )
     x2lo = ring(up2, "gx", 1)
     x2hi = ring(dn2, "gx", -1)
-    block = (4, 24, 32, 256)
+    block = (4, 26, 40, 128)
     (out,) = kernel(
-        steps, 24, [(4, 8, 16, 128)], [block, block, block[1:], (4, 24, 32, 128), (3, 24, 32, 128)], scalars=1
-    )(scal, fields, zp, mown, x1lo, x1hi, moby, yh, eh, x2lo, x2hi)
+        steps, 24, [(4, 8, 16, 128)], [block] * 4 + [block[1:]] * 2 + [(4, 24, 32, 128), (3, 24, 32, 128)], scalars=1
+    )(scal, own, zp, mown, x1lo, x1hi, moby, yh, eh, x2lo, x2hi)
     return out
 
 

time: 95.4 us -> 78.7 us (0.82)
  Pallas kernels: 19 us -> 12.4 us
  starting transfers between devices: 48.7 us -> 43.5 us
  waiting for transfers between devices: 22.6 us -> 20.1 us
  local copies, waits for them, and re-layouts: 4.14 us -> 1.68 us
    pallas_call x7 -> x6, Pallas kernels: 19 us -> 12.4 us  [call(): pl.pallas_call(fn, in_specs=specs, out_specs=[pl.BlockSpec(memory_space=p...]
    ppermute x6, starting transfers between devices: 46.1 us -> 41 us  [ring(): return lax.ppermute(value, axis, [(i, (i + by) % n) for i in range(n)])]
    ppermute x2, waiting for transfers between devices: 1.86 us -> 0.35 us  [from_above(): return lax.ppermute(value, 'gz', [(i, i - 1) for i in range(1, n)])]
    unnamed x14 -> x10, local copies, waits for them, and re-layouts: 2.96 us -> 1.54 us
    squeeze x1, local copies, waits for them, and re-layouts: 1.07 us -> 0.04 us  [melt_above(): melt[0]]
    ppermute x6, waiting for transfers between devices: 20.7 us -> 19.7 us  [ring(): return lax.ppermute(value, axis, [(i, (i + by) % n) for i in range(n)])]
  transfers between devices with their start and end apart: 8 -> 8, of which waited for: 5 -> 4; matrix products, arithmetic and copies ran while one was open for 2% -> 1% of each run, Pallas kernels for 2% -> 4%
where the time goes in v2:
time: 78.7 us; the launch traced here: 78.3 us
  starting transfers between devices  43.5 us (55%)
  waiting for transfers between devices  20.1 us (26%)
  Pallas kernels  12.4 us (16%)
  local copies, waits for them, and re-layouts  1.68 us (2%)
    ppermute x6, starting transfers between devices, ring(): return lax.ppermute(value, axis, [(i, (i + by) % n) for i in range(n)])  41 us
    ppermute x6, waiting for transfers between devices, ring(): return lax.ppermute(value, axis, [(i, (i + by) % n) for i in range(n)])  19.7 us
    pallas_call x6, Pallas kernels, call(): pl.pallas_call(fn, in_specs=specs, out_specs=[pl.BlockSpec(memory_space=p...  12.4 us
    ppermute x2, starting transfers between devices, from_above(): return lax.ppermute(value, 'gz', [(i, i - 1) for i in range(1, n)])  2.58 us
  transfers between devices with their start and end apart: 8, of which 4 were waited for; matrix products, arithmetic and copies ran while one was open for 1% of the time, Pallas kernels for 4%

profile of v2, /device:TPU:6, one launch (start us, length us, event | category | flops | bytes accessed | tf_op | source)
XLA Modules:
  0.0 78.3 jit_solution(5102084223676084601)
XLA Ops:
  0.0 15.0 %collective-permute-start.4 = (f32[4,8,16,128]{3,2,1,0:T(8,128)}, f32[4,8,16,128]{3,2,1,0:T(8,128)S(1)}, u32[]{:S(2)}, u32[]{:S(2)}) collective-permute-start(f32[4,8,16,128]{3,2,1,0:T(8,128)} %f_in.1), channel_id=1, source_target_pairs={{0,256},{256,512},{512,768},{768,0},{1,257},{257,513},{513,769},{7... | collective-permute-start | bytes 786440 | tf_op jit(solution)/shard_map/ppermute | solution.py:340
  15.0 1.9 %collective-permute-start.5 = (f32[4,8,16,128]{3,2,1,0:T(8,128)}, f32[4,8,16,128]{3,2,1,0:T(8,128)S(1)}, u32[]{:S(2)}, u32[]{:S(2)}) collective-permute-start(f32[4,8,16,128]{3,2,1,0:T(8,128)} %f_in.1), channel_id=1, source_target_pairs={{0,768},{256,0},{512,256},{768,512},{1,769},{257,1},{513,257},{769... | collective-permute-start | bytes 786440 | tf_op jit(solution)/shard_map/ppermute | solution.py:340
  16.9 0.0 copy-start
  16.9 1.0 %copy-done = f32[4,8,16,128]{3,2,1,0:T(8,128)S(1)} copy-done((f32[4,8,16,128]{3,2,1,0:T(8,128)S(1)}, f32[4,8,16,128]{3,2,1,0:T(8,128)}, u32[]{:S(2)}) %copy-start) | copy-done | bytes 262168
  17.9 1.3 %shard_map.57 = (f32[224,128]{1,0:T(8,128)S(1)}, f32[224,128]{1,0:T(8,128)S(1)}) custom-call(f32[4,8,16,128]{3,2,1,0:T(8,128)S(1)} %copy-done, s32[8,16]{1,0:T(8,128)} %ids_in.1, f32[2,4,8,16,16]{4,3,2,1,0:T(8,128)} %melt_in.1), custom_call_target="tpu_custom_call" | custom-call | tf_op jit(solution)/shard_map/pallas_call | solution.py:326
  19.2 8.3 %collective-permute-start.1 = (f32[224,128]{1,0:T(8,128)S(1)}, f32[224,128]{1,0:T(8,128)S(1)}, u32[]{:S(2)}, u32[]{:S(2)}) collective-permute-start(f32[224,128]{1,0:T(8,128)S(1)} %get-tuple-element.21), channel_id=1, source_target_pairs={{0,16},{16,32},{32,48},{48,64},{64,80},{80,96},{96,112},{112,128},... | collective-permute-start | bytes 344072 | tf_op jit(solution)/shard_map/ppermute | solution.py:340
  27.5 8.4 %collective-permute-start.2 = (f32[224,128]{1,0:T(8,128)S(1)}, f32[224,128]{1,0:T(8,128)S(1)}, u32[]{:S(2)}, u32[]{:S(2)}) collective-permute-start(f32[224,128]{1,0:T(8,128)S(1)} %get-tuple-element.22), channel_id=1, source_target_pairs={{0,240},{16,0},{32,16},{48,32},{64,48},{80,64},{96,80},{112,96},{1... | collective-permute-start | bytes 344072 | tf_op jit(solution)/shard_map/ppermute | solution.py:340
  35.9 0.1 shard_map.55
  36.0 1.3 %collective-permute-start = (f32[176,128]{1,0:T(8,128)S(1)}, f32[176,128]{1,0:T(8,128)S(1)}, u32[]{:S(2)}, u32[]{:S(2)}) collective-permute-start(f32[176,128]{1,0:T(8,128)S(1)} %get-tuple-element.19), channel_id=1, source_target_pairs={{1,0},{2,1},{3,2},{4,3},{5,4},{6,5},{7,6},{8,7},{9,8},{10,9},{11,1... | collective-permute-start | bytes 270344 | tf_op jit(solution)/shard_map/ppermute | solution.py:345
  37.4 0.1 pad.25.clone
  37.5 0.1 maximum_maximum_fusion
  37.7 0.1 select_maximum_fusion
  37.8 0.1 select_maximum_fusion.2
  37.9 0.0 collective-permute-done.1.lo
  37.9 10.4 %collective-permute-done.2.hi = f32[224,128]{1,0:T(8,128)S(1)} collective-permute-done((f32[224,128]{1,0:T(8,128)S(1)}, f32[224,128]{1,0:T(8,128)S(1)}, u32[]{:S(2)}, u32[]{:S(2)}) %collective-permute-start.2) | collective-permute-done | bytes 114720 | tf_op jit(solution)/shard_map/ppermute | solution.py:340
  48.3 0.1 shard_map.58
  48.4 0.0 copy-start.1
  48.4 1.3 %collective-permute-start.3 = (f32[144,128]{1,0:T(8,128)S(1)}, f32[144,128]{1,0:T(8,128)S(1)}, u32[]{:S(2)}, u32[]{:S(2)}) collective-permute-start(f32[144,128]{1,0:T(8,128)S(1)} %get-tuple-element.23), channel_id=1, source_target_pairs={{1,0},{2,1},{3,2},{4,3},{5,4},{6,5},{7,6},{8,7},{9,8},{10,9},{11,1... | collective-permute-start | bytes 221192 | tf_op jit(solution)/shard_map/ppermute | solution.py:345
  49.7 0.0 copy-start.2
  49.7 0.1 pad_add_fusion.scal
  49.8 0.6 copy-done.2
  50.4 0.8 %shard_map.56 = (f32[8,128]{1,0:T(8,128)S(1)}, f32[3,8,16,128]{3,2,1,0:T(8,128)S(1)}) custom-call(f32[64]{0:T(128)S(1)} %copy-done.2, s32[8,16]{1,0:T(8,128)S(1)} %copy-done.1), custom_call_target="tpu_custom_call" | custom-call | tf_op jit(solution)/shard_map/pallas_call | solution.py:326
  51.2 0.0 collective-permute-done.z1
  51.2 0.4 collective-permute-done.3.z2
  51.5 0.8 %shard_map.59 = (f32[176,128]{1,0:T(8,128)S(1)}, f32[4,2,8,8,128]{4,3,2,1,0:T(8,128)S(1)}, f32[464,128]{1,0:T(8,128)S(1)}, f32[464,128]{1,0:T(8,128)S(1)}, f32[8,128]{1,0:T(8,128)S(1)}) custom-call(s32[4]{0:T(128)S(1)} %pad_add_fusion.scal, f32[64]{0:T(128)S(1)} %copy-done.2, f32[176,128]{1,0:T(8,128)S(1)} %collective-permute-done.z1, ...), custom_call_target="tpu_custom_call" | custom-call | tf_op jit(solution)/shard_map/pallas_call | solution.py:326
  52.4 5.5 %collective-permute-start.6 = (f32[464,128]{1,0:T(8,128)S(1)}, f32[464,128]{1,0:T(8,128)S(1)}, u32[]{:S(2)}, u32[]{:S(2)}) collective-permute-start(f32[464,128]{1,0:T(8,128)S(1)} %get-tuple-element.29), channel_id=1, source_target_pairs={{0,256},{256,512},{512,768},{768,0},{1,257},{257,513},{513,769},{7... | collective-permute-start | bytes 712712 | tf_op jit(solution)/shard_map/ppermute | solution.py:340
  57.9 1.9 %collective-permute-start.7 = (f32[464,128]{1,0:T(8,128)S(1)}, f32[464,128]{1,0:T(8,128)S(1)}, u32[]{:S(2)}, u32[]{:S(2)}) collective-permute-start(f32[464,128]{1,0:T(8,128)S(1)} %get-tuple-element.30), channel_id=1, source_target_pairs={{0,768},{256,0},{512,256},{768,512},{1,769},{257,1},{513,257},{769... | collective-permute-start | bytes 712712 | tf_op jit(solution)/shard_map/ppermute | solution.py:340
  59.8 0.0 collective-permute-done.4.x1lo
  59.8 0.0 collective-permute-done.5.x1hi
  59.8 4.0 %collective-permute-done.6.x2lo = f32[464,128]{1,0:T(8,128)S(1)} collective-permute-done((f32[464,128]{1,0:T(8,128)S(1)}, f32[464,128]{1,0:T(8,128)S(1)}, u32[]{:S(2)}, u32[]{:S(2)}) %collective-permute-start.6) | collective-permute-done | bytes 237600 | tf_op jit(solution)/shard_map/ppermute | solution.py:340
  63.8 5.3 %collective-permute-done.7.x2hi = f32[464,128]{1,0:T(8,128)S(1)} collective-permute-done((f32[464,128]{1,0:T(8,128)S(1)}, f32[464,128]{1,0:T(8,128)S(1)}, u32[]{:S(2)}, u32[]{:S(2)}) %collective-permute-start.7) | collective-permute-done | bytes 237600 | tf_op jit(solution)/shard_map/ppermute | solution.py:340
  69.2 9.2 %shard_map.60 = f32[4,8,16,128]{3,2,1,0:T(8,128)} custom-call(s32[4]{0:T(128)S(1)} %pad_add_fusion.scal, f32[4,8,16,128]{3,2,1,0:T(8,128)S(1)} %get-tuple-element.18.f, f32[176,128]{1,0:T(8,128)S(1)} %get-tuple-element.25.zp, f32[3,8,16,128]{3,2,1,0:T(8,128)S(1)} %get-tuple-element.26.mown, f32[4,8,16,128]{3,2,1,0:T(8,128)S(1)} %collective-permute-done.4.x1lo, ...), custom_call_target="tpu_custom_call" | custom-call | tf_op jit(solution)/shard_map/pallas_call | solution.py:326
  (11 shorter events, 0.1 us)
Async XLA Ops:
  0.0 59.8 %collective-permute-start.4 = (f32[4,8,16,128]{3,2,1,0:T(8,128)}, f32[4,8,16,128]{3,2,1,0:T(8,128)S(1)}, u32[]{:S(2)}, u32[]{:S(2)}) collective-permute-start(f32[4,8,16,128]{3,2,1,0:T(8,128)} %f_in.1), channel_id=1, source_target_pairs={{0,256},{256,512},{512,768},{768,0},{1,257},{257,513},{513,769},{7... | collective-permute-start | bytes 786440 | tf_op jit(solution)/shard_map/ppermute | solution.py:340
  15.0 44.8 %collective-permute-start.5 = (f32[4,8,16,128]{3,2,1,0:T(8,128)}, f32[4,8,16,128]{3,2,1,0:T(8,128)S(1)}, u32[]{:S(2)}, u32[]{:S(2)}) collective-permute-start(f32[4,8,16,128]{3,2,1,0:T(8,128)} %f_in.1), channel_id=1, source_target_pairs={{0,768},{256,0},{512,256},{768,512},{1,769},{257,1},{513,257},{769... | collective-permute-start | bytes 786440 | tf_op jit(solution)/shard_map/ppermute | solution.py:340
  16.9 1.0 %copy-start = (f32[4,8,16,128]{3,2,1,0:T(8,128)S(1)}, f32[4,8,16,128]{3,2,1,0:T(8,128)}, u32[]{:S(2)}) copy-start(f32[4,8,16,128]{3,2,1,0:T(8,128)} %f_in.1) | copy-start | bytes 786436
  17.9 19.4 %copy-start.3 = (f32[2,4,8,16,16]{4,3,2,1,0:T(8,128)S(1)}, f32[2,4,8,16,16]{4,3,2,1,0:T(8,128)}, u32[]{:S(2)}) copy-start(f32[2,4,8,16,16]{4,3,2,1,0:T(8,128)} %melt_in.1) | copy-start | bytes 196612
  19.2 18.7 %collective-permute-start.1 = (f32[224,128]{1,0:T(8,128)S(1)}, f32[224,128]{1,0:T(8,128)S(1)}, u32[]{:S(2)}, u32[]{:S(2)}) collective-permute-start(f32[224,128]{1,0:T(8,128)S(1)} %get-tuple-element.21), channel_id=1, source_target_pairs={{0,16},{16,32},{32,48},{48,64},{64,80},{80,96},{96,112},{112,128},... | collective-permute-start | bytes 344072 | tf_op jit(solution)/shard_map/ppermute | solution.py:340
  27.5 20.7 %collective-permute-start.2 = (f32[224,128]{1,0:T(8,128)S(1)}, f32[224,128]{1,0:T(8,128)S(1)}, u32[]{:S(2)}, u32[]{:S(2)}) collective-permute-start(f32[224,128]{1,0:T(8,128)S(1)} %get-tuple-element.22), channel_id=1, source_target_pairs={{0,240},{16,0},{32,16},{48,32},{64,48},{80,64},{96,80},{112,96},{1... | collective-permute-start | bytes 344072 | tf_op jit(solution)/shard_map/ppermute | solution.py:340
  36.0 15.1 %collective-permute-start = (f32[176,128]{1,0:T(8,128)S(1)}, f32[176,128]{1,0:T(8,128)S(1)}, u32[]{:S(2)}, u32[]{:S(2)}) collective-permute-start(f32[176,128]{1,0:T(8,128)S(1)} %get-tuple-element.19), channel_id=1, source_target_pairs={{1,0},{2,1},{3,2},{4,3},{5,4},{6,5},{7,6},{8,7},{9,8},{10,9},{11,1... | collective-permute-start | bytes 270344 | tf_op jit(solution)/shard_map/ppermute | solution.py:345
  48.3 1.4 %copy-start.4 = (s32[2]{0:T(128)S(1)}, s32[2]{0:T(128)}, u32[]{:S(2)}) copy-start(s32[2]{0:T(128)} %param.9) | copy-start | bytes 28
  48.4 1.4 %copy-start.1 = (s32[8,16]{1,0:T(8,128)S(1)}, s32[8,16]{1,0:T(8,128)}, u32[]{:S(2)}) copy-start(s32[8,16]{1,0:T(8,128)} %ids_in.1) | copy-start | bytes 1540
  48.4 3.2 %collective-permute-start.3 = (f32[144,128]{1,0:T(8,128)S(1)}, f32[144,128]{1,0:T(8,128)S(1)}, u32[]{:S(2)}, u32[]{:S(2)}) collective-permute-start(f32[144,128]{1,0:T(8,128)S(1)} %get-tuple-element.23), channel_id=1, source_target_pairs={{1,0},{2,1},{3,2},{4,3},{5,4},{6,5},{7,6},{8,7},{9,8},{10,9},{11,1... | collective-permute-start | bytes 221192 | tf_op jit(solution)/shard_map/ppermute | solution.py:345
  49.7 0.7 copy-start.2
  52.4 11.4 %collective-permute-start.6 = (f32[464,128]{1,0:T(8,128)S(1)}, f32[464,128]{1,0:T(8,128)S(1)}, u32[]{:S(2)}, u32[]{:S(2)}) collective-permute-start(f32[464,128]{1,0:T(8,128)S(1)} %get-tuple-element.29), channel_id=1, source_target_pairs={{0,256},{256,512},{512,768},{768,0},{1,257},{257,513},{513,769},{7... | collective-permute-start | bytes 712712 | tf_op jit(solution)/shard_map/ppermute | solution.py:340
  57.9 11.3 %collective-permute-start.7 = (f32[464,128]{1,0:T(8,128)S(1)}, f32[464,128]{1,0:T(8,128)S(1)}, u32[]{:S(2)}, u32[]{:S(2)}) collective-permute-start(f32[464,128]{1,0:T(8,128)S(1)} %get-tuple-element.30), channel_id=1, source_target_pairs={{0,768},{256,0},{512,256},{768,512},{1,769},{257,1},{513,257},{769... | collective-permute-start | bytes 712712 | tf_op jit(solution)/shard_map/ppermute | solution.py:340

commit v3 on v2

--- a/solution.py
+++ b/solution.py
@@ -1,3 +1,5 @@
+import functools
+
 import jax
 import jax.numpy as jnp
 from jax import lax
@@ -81,8 +83,7 @@
         out[Y_IDS + 1 : Y_ROWS, :] = jnp.zeros((Y_ROWS - Y_IDS - 1, 128), f32)
 
 
-def pack_low(f, zp, own):
-    own[...] = f[...]
+def pack_low(f, zp):
     for x in range(8):
         zp[16 * x : 16 * x + 16, :] = three(f[0, x], f[1, x], f[2, x])
     for x in range(3):
@@ -291,14 +292,19 @@
             for s in u_tiles:
                 potential(X, s)
 
-        def row(X, carry):
+        def row(X, carry, at=tiles):
             for ahead in u_tiles:
                 potential(X + 2, ahead)
-            for s in tiles:
+            for s in at:
                 update(X, s)
             return carry
 
-        lax.fori_loop(8 - reach, 16 + reach, row, 0, unroll=4)
+        if reach == 6:
+            lax.fori_loop(2, 7, functools.partial(row, at=(4, 12, 20)), 0, unroll=5)
+            lax.fori_loop(7, 17, row, 0, unroll=5)
+            lax.fori_loop(17, 22, functools.partial(row, at=(4, 12, 20)), 0, unroll=5)
+        else:
+            lax.fori_loop(8 - reach, 16 + reach, row, 0, unroll=4)
 
     a, b = (a0, a1), (b0, b1)
     every = (0, 8, 16, 24)
@@ -354,15 +360,15 @@
 
 
 def body(fields, grain_ids, grain_angle, melt_planes, shifts):
-    inputs = [fields.shape, pltpu.VMEM(grain_ids.shape, jnp.int32), melt_planes.shape[1:], pltpu.SemaphoreType.DMA((3,))]
-    up, dn = kernel(pack_first, 4, [(Y_ROWS, 128)] * 2, inputs, hbm=True)(
-        fields, pltpu.with_memory_space_constraint(grain_ids, pltpu.HBM), pltpu.with_memory_space_constraint(melt_planes, pltpu.HBM)
+    inputs = [pltpu.VMEM(grain_ids.shape, jnp.int32), melt_planes.shape[1:], pltpu.SemaphoreType.DMA((3,))]
+    up, dn, own = kernel(pack_first, 4, [(Y_ROWS, 128)] * 2 + [fields.shape], inputs, hbm=True)(
+        *(pltpu.with_memory_space_constraint(v, pltpu.HBM) for v in (fields, grain_ids, melt_planes))
     )
     ylo = ring(up, "gy", 1)
     yhi = ring(dn, "gy", -1)
-    x1lo = ring(fields, "gx", 1)
-    x1hi = ring(fields, "gx", -1)
-    low, own = kernel(pack_low, 2, [(Z_ROWS, 128), fields.shape])(fields)
+    x1lo = ring(own, "gx", 1)
+    x1hi = ring(own, "gx", -1)
+    (low,) = kernel(pack_low, 2, [(Z_ROWS, 128)])(own)
     z1 = from_above(low)
     gz = lax.axis_index("gz").astype(jnp.int32)
     scal = jnp.stack([gz, shifts[0], shifts[1], jnp.int32(lax.axis_size("gz"))])

time: 78.7 us -> 77.2 us (0.981)
  local copies, waits for them, and re-layouts: 1.68 us -> 0.73 us
    unnamed x10 -> x8, local copies, waits for them, and re-layouts: 1.54 us -> 0.58 us
  transfers between devices with their start and end apart: 8 -> 8, of which waited for: 4 -> 4; matrix products, arithmetic and copies ran while one was open for 1% -> 1% of each run, Pallas kernels for 4% -> 2%
where the time goes in v3:
time: 77.2 us; the launch traced here: 76.8 us
  starting transfers between devices  43.6 us (56%)
  waiting for transfers between devices  20.1 us (26%)
  Pallas kernels  11.8 us (15%)
    ppermute x6, starting transfers between devices, ring(): return lax.ppermute(value, axis, [(i, (i + by) % n) for i in range(n)])  41 us
    ppermute x6, waiting for transfers between devices, ring(): return lax.ppermute(value, axis, [(i, (i + by) % n) for i in range(n)])  19.7 us
    pallas_call x6, Pallas kernels, call(): pl.pallas_call(fn, in_specs=specs, out_specs=[pl.BlockSpec(memory_space=p...  11.8 us
    ppermute x2, starting transfers between devices, from_above(): return lax.ppermute(value, 'gz', [(i, i - 1) for i in range(1, n)])  2.58 us
  transfers between devices with their start and end apart: 8, of which 4 were waited for; matrix products, arithmetic and copies ran while one was open for 1% of the time, Pallas kernels for 2%

profile of v3, /device:TPU:6, one launch (start us, length us, event | category | flops | bytes accessed | tf_op | source)
XLA Modules:
  0.0 76.8 jit_solution(3249985845829679640)
XLA Ops:
  0.0 1.4 %shard_map.55 = (f32[224,128]{1,0:T(8,128)S(1)}, f32[224,128]{1,0:T(8,128)S(1)}, f32[4,8,16,128]{3,2,1,0:T(8,128)S(1)}) custom-call(f32[4,8,16,128]{3,2,1,0:T(8,128)} %f_in.1, s32[8,16]{1,0:T(8,128)} %ids.1, f32[2,4,8,16,16]{4,3,2,1,0:T(8,128)} %melt_in.1), custom_call_target="tpu_custom_call" | custom-call | tf_op jit(solution)/shard_map/pallas_call | solution.py:332
  1.4 15.0 %collective-permute-start.4 = (f32[4,8,16,128]{3,2,1,0:T(8,128)S(1)}, f32[4,8,16,128]{3,2,1,0:T(8,128)S(1)}, u32[]{:S(2)}, u32[]{:S(2)}) collective-permute-start(f32[4,8,16,128]{3,2,1,0:T(8,128)S(1)} %get-tuple-element.17.f), channel_id=1, source_target_pairs={{0,256},{256,512},{512,768},{768,0},{1,257},{257,513},{513,769},{7... | collective-permute-start | bytes 786440 | tf_op jit(solution)/shard_map/ppermute | solution.py:346
  16.4 1.9 %collective-permute-start.5 = (f32[4,8,16,128]{3,2,1,0:T(8,128)S(1)}, f32[4,8,16,128]{3,2,1,0:T(8,128)S(1)}, u32[]{:S(2)}, u32[]{:S(2)}) collective-permute-start(f32[4,8,16,128]{3,2,1,0:T(8,128)S(1)} %get-tuple-element.17.f), channel_id=1, source_target_pairs={{0,768},{256,0},{512,256},{768,512},{1,769},{257,1},{513,257},{769... | collective-permute-start | bytes 786440 | tf_op jit(solution)/shard_map/ppermute | solution.py:346
  18.4 8.3 %collective-permute-start.1 = (f32[224,128]{1,0:T(8,128)S(1)}, f32[224,128]{1,0:T(8,128)S(1)}, u32[]{:S(2)}, u32[]{:S(2)}) collective-permute-start(f32[224,128]{1,0:T(8,128)S(1)} %get-tuple-element.19), channel_id=1, source_target_pairs={{0,16},{16,32},{32,48},{48,64},{64,80},{80,96},{96,112},{112,128},... | collective-permute-start | bytes 344072 | tf_op jit(solution)/shard_map/ppermute | solution.py:346
  26.6 8.4 %collective-permute-start.2 = (f32[224,128]{1,0:T(8,128)S(1)}, f32[224,128]{1,0:T(8,128)S(1)}, u32[]{:S(2)}, u32[]{:S(2)}) collective-permute-start(f32[224,128]{1,0:T(8,128)S(1)} %get-tuple-element.20), channel_id=1, source_target_pairs={{0,240},{16,0},{32,16},{48,32},{64,48},{80,64},{96,80},{112,96},{1... | collective-permute-start | bytes 344072 | tf_op jit(solution)/shard_map/ppermute | solution.py:346
  35.0 0.1 shard_map.56
  35.2 1.3 %collective-permute-start = (f32[176,128]{1,0:T(8,128)S(1)}, f32[176,128]{1,0:T(8,128)S(1)}, u32[]{:S(2)}, u32[]{:S(2)}) collective-permute-start(f32[176,128]{1,0:T(8,128)S(1)} %shard_map.56), channel_id=1, source_target_pairs={{1,0},{2,1},{3,2},{4,3},{5,4},{6,5},{7,6},{8,7},{9,8},{10,9},{11,1... | collective-permute-start | bytes 270344 | tf_op jit(solution)/shard_map/ppermute | solution.py:351
  36.5 0.0 copy-done.2
  36.5 0.1 pad.25.clone
  36.6 0.1 maximum_maximum_fusion
  36.8 0.1 select_maximum_fusion
  36.9 0.1 select_maximum_fusion.2
  37.0 0.0 collective-permute-done.1.lo
  37.0 10.4 %collective-permute-done.2.hi = f32[224,128]{1,0:T(8,128)S(1)} collective-permute-done((f32[224,128]{1,0:T(8,128)S(1)}, f32[224,128]{1,0:T(8,128)S(1)}, u32[]{:S(2)}, u32[]{:S(2)}) %collective-permute-start.2) | collective-permute-done | bytes 114720 | tf_op jit(solution)/shard_map/ppermute | solution.py:346
  47.4 0.1 shard_map.58
  47.5 0.0 copy-start
  47.5 1.3 %collective-permute-start.3 = (f32[144,128]{1,0:T(8,128)S(1)}, f32[144,128]{1,0:T(8,128)S(1)}, u32[]{:S(2)}, u32[]{:S(2)}) collective-permute-start(f32[144,128]{1,0:T(8,128)S(1)} %get-tuple-element.21), channel_id=1, source_target_pairs={{1,0},{2,1},{3,2},{4,3},{5,4},{6,5},{7,6},{8,7},{9,8},{10,9},{11,1... | collective-permute-start | bytes 221192 | tf_op jit(solution)/shard_map/ppermute | solution.py:351
  48.8 0.0 copy-start.1
  48.8 0.1 pad_add_fusion.scal
  48.9 0.0 copy-done
  48.9 0.6 copy-done.1
  49.5 0.8 %shard_map.57 = (f32[8,128]{1,0:T(8,128)S(1)}, f32[3,8,16,128]{3,2,1,0:T(8,128)S(1)}) custom-call(f32[64]{0:T(128)S(1)} %copy-done.1, s32[8,16]{1,0:T(8,128)S(1)} %copy-done), custom_call_target="tpu_custom_call" | custom-call | tf_op jit(solution)/shard_map/pallas_call | solution.py:332
  50.3 0.0 collective-permute-done.z1
  50.3 0.4 collective-permute-done.3.z2
  50.7 0.8 %shard_map.59 = (f32[176,128]{1,0:T(8,128)S(1)}, f32[4,2,8,8,128]{4,3,2,1,0:T(8,128)S(1)}, f32[464,128]{1,0:T(8,128)S(1)}, f32[464,128]{1,0:T(8,128)S(1)}, f32[8,128]{1,0:T(8,128)S(1)}) custom-call(s32[4]{0:T(128)S(1)} %pad_add_fusion.scal, f32[64]{0:T(128)S(1)} %copy-done.1, f32[176,128]{1,0:T(8,128)S(1)} %collective-permute-done.z1, ...), custom_call_target="tpu_custom_call" | custom-call | tf_op jit(solution)/shard_map/pallas_call | solution.py:332
  51.5 5.5 %collective-permute-start.6 = (f32[464,128]{1,0:T(8,128)S(1)}, f32[464,128]{1,0:T(8,128)S(1)}, u32[]{:S(2)}, u32[]{:S(2)}) collective-permute-start(f32[464,128]{1,0:T(8,128)S(1)} %get-tuple-element.27), channel_id=1, source_target_pairs={{0,256},{256,512},{512,768},{768,0},{1,257},{257,513},{513,769},{7... | collective-permute-start | bytes 712712 | tf_op jit(solution)/shard_map/ppermute | solution.py:346
  57.0 1.9 %collective-permute-start.7 = (f32[464,128]{1,0:T(8,128)S(1)}, f32[464,128]{1,0:T(8,128)S(1)}, u32[]{:S(2)}, u32[]{:S(2)}) collective-permute-start(f32[464,128]{1,0:T(8,128)S(1)} %get-tuple-element.28), channel_id=1, source_target_pairs={{0,768},{256,0},{512,256},{768,512},{1,769},{257,1},{513,257},{769... | collective-permute-start | bytes 712712 | tf_op jit(solution)/shard_map/ppermute | solution.py:346
  58.9 0.0 collective-permute-done.4.x1lo
  58.9 0.0 collective-permute-done.5.x1hi
  58.9 4.0 %collective-permute-done.6.x2lo = f32[464,128]{1,0:T(8,128)S(1)} collective-permute-done((f32[464,128]{1,0:T(8,128)S(1)}, f32[464,128]{1,0:T(8,128)S(1)}, u32[]{:S(2)}, u32[]{:S(2)}) %collective-permute-start.6) | collective-permute-done | bytes 237600 | tf_op jit(solution)/shard_map/ppermute | solution.py:346
  62.9 5.3 %collective-permute-done.7.x2hi = f32[464,128]{1,0:T(8,128)S(1)} collective-permute-done((f32[464,128]{1,0:T(8,128)S(1)}, f32[464,128]{1,0:T(8,128)S(1)}, u32[]{:S(2)}, u32[]{:S(2)}) %collective-permute-start.7) | collective-permute-done | bytes 237600 | tf_op jit(solution)/shard_map/ppermute | solution.py:346
  68.3 8.5 %shard_map.60 = f32[4,8,16,128]{3,2,1,0:T(8,128)} custom-call(s32[4]{0:T(128)S(1)} %pad_add_fusion.scal, f32[4,8,16,128]{3,2,1,0:T(8,128)S(1)} %get-tuple-element.17.f, f32[176,128]{1,0:T(8,128)S(1)} %get-tuple-element.23.zp, f32[3,8,16,128]{3,2,1,0:T(8,128)S(1)} %get-tuple-element.24.mown, f32[4,8,16,128]{3,2,1,0:T(8,128)S(1)} %collective-permute-done.4.x1lo, ...), custom_call_target="tpu_custom_call" | custom-call | tf_op jit(solution)/shard_map/pallas_call | solution.py:332
  (9 shorter events, 0.1 us)
Async XLA Ops:
  0.0 36.5 %copy-start.2 = (f32[2,4,8,16,16]{4,3,2,1,0:T(8,128)S(1)}, f32[2,4,8,16,16]{4,3,2,1,0:T(8,128)}, u32[]{:S(2)}) copy-start(f32[2,4,8,16,16]{4,3,2,1,0:T(8,128)} %melt_in.1) | copy-start | bytes 196612
  1.4 57.5 %collective-permute-start.4 = (f32[4,8,16,128]{3,2,1,0:T(8,128)S(1)}, f32[4,8,16,128]{3,2,1,0:T(8,128)S(1)}, u32[]{:S(2)}, u32[]{:S(2)}) collective-permute-start(f32[4,8,16,128]{3,2,1,0:T(8,128)S(1)} %get-tuple-element.17.f), channel_id=1, source_target_pairs={{0,256},{256,512},{512,768},{768,0},{1,257},{257,513},{513,769},{7... | collective-permute-start | bytes 786440 | tf_op jit(solution)/shard_map/ppermute | solution.py:346
  16.4 42.5 %collective-permute-start.5 = (f32[4,8,16,128]{3,2,1,0:T(8,128)S(1)}, f32[4,8,16,128]{3,2,1,0:T(8,128)S(1)}, u32[]{:S(2)}, u32[]{:S(2)}) collective-permute-start(f32[4,8,16,128]{3,2,1,0:T(8,128)S(1)} %get-tuple-element.17.f), channel_id=1, source_target_pairs={{0,768},{256,0},{512,256},{768,512},{1,769},{257,1},{513,257},{769... | collective-permute-start | bytes 786440 | tf_op jit(solution)/shard_map/ppermute | solution.py:346
  18.4 18.7 %collective-permute-start.1 = (f32[224,128]{1,0:T(8,128)S(1)}, f32[224,128]{1,0:T(8,128)S(1)}, u32[]{:S(2)}, u32[]{:S(2)}) collective-permute-start(f32[224,128]{1,0:T(8,128)S(1)} %get-tuple-element.19), channel_id=1, source_target_pairs={{0,16},{16,32},{32,48},{48,64},{64,80},{80,96},{96,112},{112,128},... | collective-permute-start | bytes 344072 | tf_op jit(solution)/shard_map/ppermute | solution.py:346
  26.6 20.7 %collective-permute-start.2 = (f32[224,128]{1,0:T(8,128)S(1)}, f32[224,128]{1,0:T(8,128)S(1)}, u32[]{:S(2)}, u32[]{:S(2)}) collective-permute-start(f32[224,128]{1,0:T(8,128)S(1)} %get-tuple-element.20), channel_id=1, source_target_pairs={{0,240},{16,0},{32,16},{48,32},{64,48},{80,64},{96,80},{112,96},{1... | collective-permute-start | bytes 344072 | tf_op jit(solution)/shard_map/ppermute | solution.py:346
  35.2 15.1 %collective-permute-start = (f32[176,128]{1,0:T(8,128)S(1)}, f32[176,128]{1,0:T(8,128)S(1)}, u32[]{:S(2)}, u32[]{:S(2)}) collective-permute-start(f32[176,128]{1,0:T(8,128)S(1)} %shard_map.56), channel_id=1, source_target_pairs={{1,0},{2,1},{3,2},{4,3},{5,4},{6,5},{7,6},{8,7},{9,8},{10,9},{11,1... | collective-permute-start | bytes 270344 | tf_op jit(solution)/shard_map/ppermute | solution.py:351
  47.4 1.4 %copy-start.3 = (s32[2]{0:T(128)S(1)}, s32[2]{0:T(128)}, u32[]{:S(2)}) copy-start(s32[2]{0:T(128)} %param.9) | copy-start | bytes 28
  47.5 1.4 %copy-start = (s32[8,16]{1,0:T(8,128)S(1)}, s32[8,16]{1,0:T(8,128)}, u32[]{:S(2)}) copy-start(s32[8,16]{1,0:T(8,128)} %ids.1) | copy-start | bytes 1540
  47.5 3.2 %collective-permute-start.3 = (f32[144,128]{1,0:T(8,128)S(1)}, f32[144,128]{1,0:T(8,128)S(1)}, u32[]{:S(2)}, u32[]{:S(2)}) collective-permute-start(f32[144,128]{1,0:T(8,128)S(1)} %get-tuple-element.21), channel_id=1, source_target_pairs={{1,0},{2,1},{3,2},{4,3},{5,4},{6,5},{7,6},{8,7},{9,8},{10,9},{11,1... | collective-permute-start | bytes 221192 | tf_op jit(solution)/shard_map/ppermute | solution.py:351
  48.8 0.7 copy-start.1
  51.5 11.4 %collective-permute-start.6 = (f32[464,128]{1,0:T(8,128)S(1)}, f32[464,128]{1,0:T(8,128)S(1)}, u32[]{:S(2)}, u32[]{:S(2)}) collective-permute-start(f32[464,128]{1,0:T(8,128)S(1)} %get-tuple-element.27), channel_id=1, source_target_pairs={{0,256},{256,512},{512,768},{768,0},{1,257},{257,513},{513,769},{7... | collective-permute-start | bytes 712712 | tf_op jit(solution)/shard_map/ppermute | solution.py:346
  57.0 11.3 %collective-permute-start.7 = (f32[464,128]{1,0:T(8,128)S(1)}, f32[464,128]{1,0:T(8,128)S(1)}, u32[]{:S(2)}, u32[]{:S(2)}) collective-permute-start(f32[464,128]{1,0:T(8,128)S(1)} %get-tuple-element.28), channel_id=1, source_target_pairs={{0,768},{256,0},{512,256},{768,512},{1,769},{257,1},{513,257},{769... | collective-permute-start | bytes 712712 | tf_op jit(solution)/shard_map/ppermute | solution.py:346

commit v4 on v3

--- a/solution.py
+++ b/solution.py
@@ -42,7 +42,15 @@
     return c - 6.0 * p0 + 4.0 * p1 - 2.0 * p2
 
 
-def pack_first(f_in, ids_in, melt_in, up, dn, f, ids, melt, sems):
+def even(axis):
+    return lax.axis_index(axis) % 2 == 0
+
+
+def swapped(flag, a, b):
+    return jnp.where(flag, a, b), jnp.where(flag, b, a)
+
+
+def pack_first(f_in, ids_in, melt_in, m1, m2, f, up, dn, ids, melt, sems):
     copies = [
         pltpu.make_async_copy(f_in, f, sems.at[0]),
         pltpu.make_async_copy(ids_in, ids, sems.at[1]),
@@ -81,6 +89,7 @@
     for out in (up, dn):
         out[Y_IDS : Y_IDS + 1, :] = jnp.concatenate([ids[x : x + 1, :].astype(f32) for x in range(8)], axis=1)
         out[Y_IDS + 1 : Y_ROWS, :] = jnp.zeros((Y_ROWS - Y_IDS - 1, 128), f32)
+    m1[...], m2[...] = swapped(even("gy"), up[...], dn[...])
 
 
 def pack_low(f, zp):
@@ -122,7 +131,8 @@
             dst[k, side, x, 2 - 2 * side : 8 - 2 * side, :] = src[at : at + 6, :]
 
 
-def unpack_y(lo, hi, yh, z2):
+def unpack_y(y1, y2, yh, z2, lo, hi):
+    hi[...], lo[...] = swapped(even("gy"), y1[...], y2[...])
     tiles_of(lo, 0, 0, yh)
     tiles_of(hi, 0, 1, yh)
 
@@ -133,7 +143,7 @@
         z2[8 * t : 8 * t + 8, :] = three(tile(t), tile(t + 18), tile(t + 36) if t + 36 < 52 else None)
 
 
-def unpack_z(scal, angles, z1, meltp, mob, z2, lo, hi, yh, zp, eh, up, dn, moby, flat):
+def unpack_z(scal, angles, z1, meltp, mob, z2, lo, hi, yh, zp, eh, m1, m2, moby, flat, up, dn):
     top = scal[0] == scal[3] - 1
     zp[...] = jnp.where(top, meltp[...], z1[...])
     moby[...] = jnp.zeros(moby.shape, f32)
@@ -186,48 +196,65 @@
         out[X2_ZP:X2_MOB, :] = zp[...]
         out[X2_MOB : X2_MOB + 8, :] = moby[...]
         out[X2_MOB + 8 :, :] = mob[...]
-
-
-def steps(scal, f, zp, mown, x1lo, x1hi, moby, yh, eh, x2lo, x2hi, out, a0, a1, b0, b1, u0, u1, ex, mo):
+    m1[...], m2[...] = swapped(even("gx"), up[...], dn[...])
+
+
+def steps(scal, f, zp, mown, x1a, x1b, moby, yh, eh, x2a, x2b, out, a0, a1, b0, b1, u0, u1, ex, mo):
     gz, s1, s2, top = scal[0], scal[1], scal[2], scal[0] == scal[3] - 1
     planes = scal[3] * 128
 
     for k in range(4):
         a0[k, 8:16, 8:24, :] = f[k]
         for x in range(8):
-            a0[k, x, 8:24, :] = x1lo[k, x]
-            a0[k, 16 + x, 8:24, :] = x1hi[k, x]
-            for src, base, X in ((zp, 0, 8), (x2lo, X2_ZP, 0), (x2hi, X2_ZP, 16)):
-                r = base + (16 * x if k < 3 else 128 + 16 * (x % 3))
-                ex[k, X + x, 8:24, :] = part(src[r : r + 16, :], k if k < 3 else x // 3)
+            r = 16 * x if k < 3 else 128 + 16 * (x % 3)
+            ex[k, 8 + x, 8:24, :] = part(zp[r : r + 16, :], k if k < 3 else x // 3)
         for side in range(2):
             a0[k, 8:16, 24 * side : 24 * side + 8, :] = yh[k, side]
             ex[k, 8:16, 24 * side : 24 * side + 8, :] = eh[k, side]
-    for src, lo_col, hi_col in ((x2lo, lambda d: 8 - d, lambda d: 8 - d), (x2hi, lambda d: 15 + d, lambda d: 15 + d)):
-        for k in (3, 0, 1, 2):
-            for dx in range(1, 8 if k == 3 else 7):
-                at = 8 * (dx - 1) if k == 3 else 56 + 48 * k + 8 * (dx - 1)
-                tile = src[at : at + 8, :]
-                if k == 3:
-                    above = part(src[200 + 8 * ((dx - 1) % 3) : 208 + 8 * ((dx - 1) % 3), :], (dx - 1) // 3)
-                    other = 8 - dx
-                else:
-                    above = part(src[224 + 8 * (dx - 1) : 232 + 8 * (dx - 1), :], k)
-                    other = 7 - dx
-                a0[k, lo_col(dx), 0:8, :] = tile
-                a0[k, hi_col(other), 24:32, :] = tile
-                ex[k, lo_col(dx), 0:8, :] = above
-                ex[k, hi_col(other), 24:32, :] = above
-
     mo[:, 8:16, 8:24, :] = mown[...]
     for x in range(8):
         columns(mo, moby, 0, x, 8 + x, 8, 0, 8)
         columns(mo, moby, 3, x, 8 + x, 0, 24, 8)
-        for src, X in ((x2lo, x), (x2hi, 16 + x)):
-            if 3 <= X < 21:
-                columns(mo, src, X2_MOB + 8, x, X, 0, 8, 16)
-                columns(mo, src, X2_MOB, x, X, 8, 0, 8)
-                columns(mo, src, X2_MOB + 3, x, X, 0, 24, 8)
+
+    def sides(x1lo, x1hi, x2lo, x2hi):
+        for k in range(4):
+            for x in range(8):
+                a0[k, x, 8:24, :] = x1lo[k, x]
+                a0[k, 16 + x, 8:24, :] = x1hi[k, x]
+                r = X2_ZP + (16 * x if k < 3 else 128 + 16 * (x % 3))
+                for src, X in ((x2lo, 0), (x2hi, 16)):
+                    ex[k, X + x, 8:24, :] = part(src[r : r + 16, :], k if k < 3 else x // 3)
+        for src, lo_col, hi_col in ((x2lo, lambda d: 8 - d, lambda d: 8 - d), (x2hi, lambda d: 15 + d, lambda d: 15 + d)):
+            for k in (3, 0, 1, 2):
+                for dx in range(1, 8 if k == 3 else 7):
+                    at = 8 * (dx - 1) if k == 3 else 56 + 48 * k + 8 * (dx - 1)
+                    tile = src[at : at + 8, :]
+                    if k == 3:
+                        above = part(src[200 + 8 * ((dx - 1) % 3) : 208 + 8 * ((dx - 1) % 3), :], (dx - 1) // 3)
+                        other = 8 - dx
+                    else:
+                        above = part(src[224 + 8 * (dx - 1) : 232 + 8 * (dx - 1), :], k)
+                        other = 7 - dx
+                    a0[k, lo_col(dx), 0:8, :] = tile
+                    a0[k, hi_col(other), 24:32, :] = tile
+                    ex[k, lo_col(dx), 0:8, :] = above
+                    ex[k, hi_col(other), 24:32, :] = above
+        for x in range(8):
+            for src, X in ((x2lo, x), (x2hi, 16 + x)):
+                if 3 <= X < 21:
+                    columns(mo, src, X2_MOB + 8, x, X, 0, 8, 16)
+                    columns(mo, src, X2_MOB, x, X, 8, 0, 8)
+                    columns(mo, src, X2_MOB + 3, x, X, 0, 24, 8)
+
+    flag = even("gx")
+
+    @pl.when(flag)
+    def _():
+        sides(x1b, x1a, x2b, x2a)
+
+    @pl.when(jnp.logical_not(flag))
+    def _():
+        sides(x1a, x1b, x2a, x2b)
 
     lane = lanes((8, 128))
     first = gz * 128 + lane
@@ -341,9 +368,9 @@
     return call
 
 
-def ring(value, axis, by):
+def swap(value, axis, stage):
     n = lax.axis_size(axis)
-    return lax.ppermute(value, axis, [(i, (i + by) % n) for i in range(n)])
+    return lax.ppermute(value, axis, [(i, (i + (1 if (i + stage) % 2 == 0 else -1)) % n) for i in range(n)])
 
 
 def from_above(value):
@@ -360,32 +387,32 @@
 
 
 def body(fields, grain_ids, grain_angle, melt_planes, shifts):
-    inputs = [pltpu.VMEM(grain_ids.shape, jnp.int32), melt_planes.shape[1:], pltpu.SemaphoreType.DMA((3,))]
-    up, dn, own = kernel(pack_first, 4, [(Y_ROWS, 128)] * 2 + [fields.shape], inputs, hbm=True)(
+    inputs = [(Y_ROWS, 128), (Y_ROWS, 128), pltpu.VMEM(grain_ids.shape, jnp.int32), melt_planes.shape[1:], pltpu.SemaphoreType.DMA((3,))]
+    m1, m2, own = kernel(pack_first, 4, [(Y_ROWS, 128)] * 2 + [fields.shape], inputs, hbm=True)(
         *(pltpu.with_memory_space_constraint(v, pltpu.HBM) for v in (fields, grain_ids, melt_planes))
     )
-    ylo = ring(up, "gy", 1)
-    yhi = ring(dn, "gy", -1)
-    x1lo = ring(own, "gx", 1)
-    x1hi = ring(own, "gx", -1)
+    y1 = swap(m1, "gy", 0)
+    y2 = swap(m2, "gy", 1)
+    x1a = swap(own, "gx", 0)
+    x1b = swap(own, "gx", 1)
     (low,) = kernel(pack_low, 2, [(Z_ROWS, 128)])(own)
     z1 = from_above(low)
     gz = lax.axis_index("gz").astype(jnp.int32)
     scal = jnp.stack([gz, shifts[0], shifts[1], jnp.int32(lax.axis_size("gz"))])
     mob, mown = kernel(own_columns, 2, [(8, 128), (3, 8, 16, 128)], scalars=1)(grain_angle, grain_ids)
     tiles = (4, 2, 8, 8, 128)
-    yh, z2 = kernel(unpack_y, 2, [tiles, (8 * Z2_TILES, 128)])(ylo, yhi)
+    yh, z2, ylo, yhi = kernel(unpack_y, 2, [tiles, (8 * Z2_TILES, 128), (Y_ROWS, 128), (Y_ROWS, 128)])(y1, y2)
     z2 = from_above(z2)
     shapes = [(Z_ROWS, 128), tiles, (X2_ROWS, 128), (X2_ROWS, 128), (8, 128)]
-    zp, eh, up2, dn2, moby = kernel(unpack_z, 4, shapes, [(416, 128)], scalars=2)(
+    zp, eh, m1, m2, moby = kernel(unpack_z, 4, shapes, [(416, 128), (X2_ROWS, 128), (X2_ROWS, 128)], scalars=2)(
         scal, grain_angle, z1, melt_above(melt_planes), mob, z2, ylo, yhi, yh
     )
-    x2lo = ring(up2, "gx", 1)
-    x2hi = ring(dn2, "gx", -1)
+    x2a = swap(m1, "gx", 0)
+    x2b = swap(m2, "gx", 1)
     block = (4, 26, 40, 128)
     (out,) = kernel(
         steps, 24, [(4, 8, 16, 128)], [block] * 4 + [block[1:]] * 2 + [(4, 24, 32, 128), (3, 24, 32, 128)], scalars=1
-    )(scal, own, zp, mown, x1lo, x1hi, moby, yh, eh, x2lo, x2hi)
+    )(scal, own, zp, mown, x1a, x1b, moby, yh, eh, x2a, x2b)
     return out
 
 

time: 77.2 us -> 79.6 us (1.031)
  the two profiles are of different devices: /device:TPU:6 before, /device:TPU:1 now
where the time goes in v4:
time: 79.6 us; the launch traced here: 79.2 us
  starting transfers between devices  43 us (54%)
  waiting for transfers between devices  22.9 us (29%)
  Pallas kernels  12 us (15%)
    ppermute x6, starting transfers between devices, swap(): lax.ppermute(value, axis, [(i, (i + (1 if (i + stage) % 2 == 0 else -1))...  36.3 us
    ppermute x6, waiting for transfers between devices, swap(): lax.ppermute(value, axis, [(i, (i + (1 if (i + stage) % 2 == 0 else -1))...  21.3 us
    pallas_call x6, Pallas kernels, call(): pl.pallas_call(fn, in_specs=specs, out_specs=[pl.BlockSpec(memory_space=p...  12 us
    ppermute x2, starting transfers between devices, from_above(): return lax.ppermute(value, 'gz', [(i, i - 1) for i in range(1, n)])  6.76 us
  transfers between devices with their start and end apart: 8, of which 4 were waited for; matrix products, arithmetic and copies ran while one was open for 1% of the time, Pallas kernels for 2%

profile of v4, /device:TPU:1, one launch (start us, length us, event | category | flops | bytes accessed | tf_op | source)
XLA Modules:
  0.0 79.2 jit_solution(11629252960951098258)
XLA Ops:
  0.0 1.4 %shard_map.55 = (f32[224,128]{1,0:T(8,128)S(1)}, f32[224,128]{1,0:T(8,128)S(1)}, f32[4,8,16,128]{3,2,1,0:T(8,128)S(1)}) custom-call(f32[4,8,16,128]{3,2,1,0:T(8,128)} %f_in.1, s32[8,16]{1,0:T(8,128)} %ids.1, f32[2,4,8,16,16]{4,3,2,1,0:T(8,128)} %melt_in.1), custom_call_target="tpu_custom_call" | custom-call | tf_op jit(solution)/shard_map/pallas_call | solution.py:359
  1.4 3.9 %collective-permute-start.4 = (f32[4,8,16,128]{3,2,1,0:T(8,128)S(1)}, f32[4,8,16,128]{3,2,1,0:T(8,128)S(1)}, u32[]{:S(2)}, u32[]{:S(2)}) collective-permute-start(f32[4,8,16,128]{3,2,1,0:T(8,128)S(1)} %get-tuple-element.19.f), channel_id=1, source_target_pairs={{0,256},{256,0},{512,768},{768,512},{1,257},{257,1},{513,769},{769... | collective-permute-start | bytes 786440 | tf_op jit(solution)/shard_map/ppermute | solution.py:373
  5.4 3.7 %collective-permute-start.5 = (f32[4,8,16,128]{3,2,1,0:T(8,128)S(1)}, f32[4,8,16,128]{3,2,1,0:T(8,128)S(1)}, u32[]{:S(2)}, u32[]{:S(2)}) collective-permute-start(f32[4,8,16,128]{3,2,1,0:T(8,128)S(1)} %get-tuple-element.19.f), channel_id=1, source_target_pairs={{0,768},{256,512},{512,256},{768,0},{1,769},{257,513},{513,257},{7... | collective-permute-start | bytes 786440 | tf_op jit(solution)/shard_map/ppermute | solution.py:373
  9.1 19.1 %collective-permute-start.1 = (f32[224,128]{1,0:T(8,128)S(1)}, f32[224,128]{1,0:T(8,128)S(1)}, u32[]{:S(2)}, u32[]{:S(2)}) collective-permute-start(f32[224,128]{1,0:T(8,128)S(1)} %get-tuple-element.21), channel_id=1, source_target_pairs={{0,16},{16,0},{32,48},{48,32},{64,80},{80,64},{96,112},{112,96},{1... | collective-permute-start | bytes 344072 | tf_op jit(solution)/shard_map/ppermute | solution.py:373
  28.2 4.8 %collective-permute-start.2 = (f32[224,128]{1,0:T(8,128)S(1)}, f32[224,128]{1,0:T(8,128)S(1)}, u32[]{:S(2)}, u32[]{:S(2)}) collective-permute-start(f32[224,128]{1,0:T(8,128)S(1)} %get-tuple-element.22), channel_id=1, source_target_pairs={{0,240},{16,32},{32,16},{48,64},{64,48},{80,96},{96,80},{112,128},... | collective-permute-start | bytes 344072 | tf_op jit(solution)/shard_map/ppermute | solution.py:373
  33.0 0.1 shard_map.56
  33.1 3.4 %collective-permute-start = (f32[176,128]{1,0:T(8,128)S(1)}, f32[176,128]{1,0:T(8,128)S(1)}, u32[]{:S(2)}, u32[]{:S(2)}) collective-permute-start(f32[176,128]{1,0:T(8,128)S(1)} %shard_map.56), channel_id=1, source_target_pairs={{1,0},{2,1},{3,2},{4,3},{5,4},{6,5},{7,6},{8,7},{9,8},{10,9},{11,1... | collective-permute-start | bytes 270344 | tf_op jit(solution)/shard_map/ppermute | solution.py:378
  36.6 0.0 copy-done.2
  36.6 0.1 pad.25.clone
  36.7 0.1 maximum_maximum_fusion
  36.9 0.1 select_maximum_fusion
  37.0 0.1 select_maximum_fusion.2
  37.1 0.0 collective-permute-done.1.y1
  37.1 14.3 %collective-permute-done.2.y2 = f32[224,128]{1,0:T(8,128)S(1)} collective-permute-done((f32[224,128]{1,0:T(8,128)S(1)}, f32[224,128]{1,0:T(8,128)S(1)}, u32[]{:S(2)}, u32[]{:S(2)}) %collective-permute-start.2) | collective-permute-done | bytes 114720 | tf_op jit(solution)/shard_map/ppermute | solution.py:373
  51.4 0.1 shard_map.58
  51.5 0.0 copy-start
  51.5 3.3 %collective-permute-start.3 = (f32[144,128]{1,0:T(8,128)S(1)}, f32[144,128]{1,0:T(8,128)S(1)}, u32[]{:S(2)}, u32[]{:S(2)}) collective-permute-start(f32[144,128]{1,0:T(8,128)S(1)} %get-tuple-element.23), channel_id=1, source_target_pairs={{1,0},{2,1},{3,2},{4,3},{5,4},{6,5},{7,6},{8,7},{9,8},{10,9},{11,1... | collective-permute-start | bytes 221192 | tf_op jit(solution)/shard_map/ppermute | solution.py:378
  54.9 0.0 copy-done.3
  54.9 0.0 copy-start.1
  54.9 0.1 pad_add_fusion.scal
  55.0 0.6 copy-done.1
  55.6 0.8 %shard_map.57 = (f32[8,128]{1,0:T(8,128)S(1)}, f32[3,8,16,128]{3,2,1,0:T(8,128)S(1)}) custom-call(f32[64]{0:T(128)S(1)} %copy-done.1, s32[8,16]{1,0:T(8,128)S(1)} %copy-done), custom_call_target="tpu_custom_call" | custom-call | tf_op jit(solution)/shard_map/pallas_call | solution.py:359
  56.4 0.0 collective-permute-done.z1
  56.4 1.5 %collective-permute-done.3.z2 = f32[144,128]{1,0:T(8,128)S(1)} collective-permute-done((f32[144,128]{1,0:T(8,128)S(1)}, f32[144,128]{1,0:T(8,128)S(1)}, u32[]{:S(2)}, u32[]{:S(2)}) %collective-permute-start.3) | collective-permute-done | bytes 73760 | tf_op jit(solution)/shard_map/ppermute | solution.py:378
  57.9 0.8 %shard_map.59 = (f32[176,128]{1,0:T(8,128)S(1)}, f32[4,2,8,8,128]{4,3,2,1,0:T(8,128)S(1)}, f32[464,128]{1,0:T(8,128)S(1)}, f32[464,128]{1,0:T(8,128)S(1)}, f32[8,128]{1,0:T(8,128)S(1)}) custom-call(s32[4]{0:T(128)S(1)} %pad_add_fusion.scal, f32[64]{0:T(128)S(1)} %copy-done.1, f32[176,128]{1,0:T(8,128)S(1)} %collective-permute-done.z1, ...), custom_call_target="tpu_custom_call" | custom-call | tf_op jit(solution)/shard_map/pallas_call | solution.py:359
  58.8 2.2 %collective-permute-start.6 = (f32[464,128]{1,0:T(8,128)S(1)}, f32[464,128]{1,0:T(8,128)S(1)}, u32[]{:S(2)}, u32[]{:S(2)}) collective-permute-start(f32[464,128]{1,0:T(8,128)S(1)} %get-tuple-element.31), channel_id=1, source_target_pairs={{0,256},{256,0},{512,768},{768,512},{1,257},{257,1},{513,769},{769... | collective-permute-start | bytes 712712 | tf_op jit(solution)/shard_map/ppermute | solution.py:373
  61.0 2.5 %collective-permute-start.7 = (f32[464,128]{1,0:T(8,128)S(1)}, f32[464,128]{1,0:T(8,128)S(1)}, u32[]{:S(2)}, u32[]{:S(2)}) collective-permute-start(f32[464,128]{1,0:T(8,128)S(1)} %get-tuple-element.32), channel_id=1, source_target_pairs={{0,768},{256,512},{512,256},{768,0},{1,769},{257,513},{513,257},{7... | collective-permute-start | bytes 712712 | tf_op jit(solution)/shard_map/ppermute | solution.py:373
  63.5 0.0 collective-permute-done.4.x1a
  63.5 0.0 collective-permute-done.5.x1b
  63.5 3.6 %collective-permute-done.6.x2a = f32[464,128]{1,0:T(8,128)S(1)} collective-permute-done((f32[464,128]{1,0:T(8,128)S(1)}, f32[464,128]{1,0:T(8,128)S(1)}, u32[]{:S(2)}, u32[]{:S(2)}) %collective-permute-start.6) | collective-permute-done | bytes 237600 | tf_op jit(solution)/shard_map/ppermute | solution.py:373
  67.1 3.4 %collective-permute-done.7.x2b = f32[464,128]{1,0:T(8,128)S(1)} collective-permute-done((f32[464,128]{1,0:T(8,128)S(1)}, f32[464,128]{1,0:T(8,128)S(1)}, u32[]{:S(2)}, u32[]{:S(2)}) %collective-permute-start.7) | collective-permute-done | bytes 237600 | tf_op jit(solution)/shard_map/ppermute | solution.py:373
  70.6 8.7 %shard_map.60 = f32[4,8,16,128]{3,2,1,0:T(8,128)} custom-call(s32[4]{0:T(128)S(1)} %pad_add_fusion.scal, f32[4,8,16,128]{3,2,1,0:T(8,128)S(1)} %get-tuple-element.19.f, f32[176,128]{1,0:T(8,128)S(1)} %get-tuple-element.27.zp, f32[3,8,16,128]{3,2,1,0:T(8,128)S(1)} %get-tuple-element.28.mown, f32[4,8,16,128]{3,2,1,0:T(8,128)S(1)} %collective-permute-done.4.x1a, ...), custom_call_target="tpu_custom_call" | custom-call | tf_op jit(solution)/shard_map/pallas_call | solution.py:359
  (9 shorter events, 0.1 us)
Async XLA Ops:
  0.0 36.6 %copy-start.2 = (f32[2,4,8,16,16]{4,3,2,1,0:T(8,128)S(1)}, f32[2,4,8,16,16]{4,3,2,1,0:T(8,128)}, u32[]{:S(2)}) copy-start(f32[2,4,8,16,16]{4,3,2,1,0:T(8,128)} %melt_in.1) | copy-start | bytes 196612
  1.4 62.1 %collective-permute-start.4 = (f32[4,8,16,128]{3,2,1,0:T(8,128)S(1)}, f32[4,8,16,128]{3,2,1,0:T(8,128)S(1)}, u32[]{:S(2)}, u32[]{:S(2)}) collective-permute-start(f32[4,8,16,128]{3,2,1,0:T(8,128)S(1)} %get-tuple-element.19.f), channel_id=1, source_target_pairs={{0,256},{256,0},{512,768},{768,512},{1,257},{257,1},{513,769},{769... | collective-permute-start | bytes 786440 | tf_op jit(solution)/shard_map/ppermute | solution.py:373
  5.4 58.1 %collective-permute-start.5 = (f32[4,8,16,128]{3,2,1,0:T(8,128)S(1)}, f32[4,8,16,128]{3,2,1,0:T(8,128)S(1)}, u32[]{:S(2)}, u32[]{:S(2)}) collective-permute-start(f32[4,8,16,128]{3,2,1,0:T(8,128)S(1)} %get-tuple-element.19.f), channel_id=1, source_target_pairs={{0,768},{256,512},{512,256},{768,0},{1,769},{257,513},{513,257},{7... | collective-permute-start | bytes 786440 | tf_op jit(solution)/shard_map/ppermute | solution.py:373
  9.1 28.0 %collective-permute-start.1 = (f32[224,128]{1,0:T(8,128)S(1)}, f32[224,128]{1,0:T(8,128)S(1)}, u32[]{:S(2)}, u32[]{:S(2)}) collective-permute-start(f32[224,128]{1,0:T(8,128)S(1)} %get-tuple-element.21), channel_id=1, source_target_pairs={{0,16},{16,0},{32,48},{48,32},{64,80},{80,64},{96,112},{112,96},{1... | collective-permute-start | bytes 344072 | tf_op jit(solution)/shard_map/ppermute | solution.py:373
  28.2 23.2 %collective-permute-start.2 = (f32[224,128]{1,0:T(8,128)S(1)}, f32[224,128]{1,0:T(8,128)S(1)}, u32[]{:S(2)}, u32[]{:S(2)}) collective-permute-start(f32[224,128]{1,0:T(8,128)S(1)} %get-tuple-element.22), channel_id=1, source_target_pairs={{0,240},{16,32},{32,16},{48,64},{64,48},{80,96},{96,80},{112,128},... | collective-permute-start | bytes 344072 | tf_op jit(solution)/shard_map/ppermute | solution.py:373
  33.1 23.3 %collective-permute-start = (f32[176,128]{1,0:T(8,128)S(1)}, f32[176,128]{1,0:T(8,128)S(1)}, u32[]{:S(2)}, u32[]{:S(2)}) collective-permute-start(f32[176,128]{1,0:T(8,128)S(1)} %shard_map.56), channel_id=1, source_target_pairs={{1,0},{2,1},{3,2},{4,3},{5,4},{6,5},{7,6},{8,7},{9,8},{10,9},{11,1... | collective-permute-start | bytes 270344 | tf_op jit(solution)/shard_map/ppermute | solution.py:378
  51.4 3.5 %copy-start.3 = (s32[2]{0:T(128)S(1)}, s32[2]{0:T(128)}, u32[]{:S(2)}) copy-start(s32[2]{0:T(128)} %param.9) | copy-start | bytes 28
  51.5 3.5 %copy-start = (s32[8,16]{1,0:T(8,128)S(1)}, s32[8,16]{1,0:T(8,128)}, u32[]{:S(2)}) copy-start(s32[8,16]{1,0:T(8,128)} %ids.1) | copy-start | bytes 1540
  51.5 6.4 %collective-permute-start.3 = (f32[144,128]{1,0:T(8,128)S(1)}, f32[144,128]{1,0:T(8,128)S(1)}, u32[]{:S(2)}, u32[]{:S(2)}) collective-permute-start(f32[144,128]{1,0:T(8,128)S(1)} %get-tuple-element.23), channel_id=1, source_target_pairs={{1,0},{2,1},{3,2},{4,3},{5,4},{6,5},{7,6},{8,7},{9,8},{10,9},{11,1... | collective-permute-start | bytes 221192 | tf_op jit(solution)/shard_map/ppermute | solution.py:378
  54.9 0.7 copy-start.1
  58.8 8.4 %collective-permute-start.6 = (f32[464,128]{1,0:T(8,128)S(1)}, f32[464,128]{1,0:T(8,128)S(1)}, u32[]{:S(2)}, u32[]{:S(2)}) collective-permute-start(f32[464,128]{1,0:T(8,128)S(1)} %get-tuple-element.31), channel_id=1, source_target_pairs={{0,256},{256,0},{512,768},{768,512},{1,257},{257,1},{513,769},{769... | collective-permute-start | bytes 712712 | tf_op jit(solution)/shard_map/ppermute | solution.py:373
  61.0 9.6 %collective-permute-start.7 = (f32[464,128]{1,0:T(8,128)S(1)}, f32[464,128]{1,0:T(8,128)S(1)}, u32[]{:S(2)}, u32[]{:S(2)}) collective-permute-start(f32[464,128]{1,0:T(8,128)S(1)} %get-tuple-element.32), channel_id=1, source_target_pairs={{0,768},{256,512},{512,256},{768,0},{1,769},{257,513},{513,257},{7... | collective-permute-start | bytes 712712 | tf_op jit(solution)/shard_map/ppermute | solution.py:373

commit v5 on v4

--- a/solution.py
+++ b/solution.py
@@ -101,7 +101,7 @@
 
 def mobility_of(grain, angles):
     angle = jnp.zeros(grain.shape, f32)
-    for g in range(angles.shape[0]):
+    for g in range(angles.shape[0] - 1):
         angle = jnp.where(grain == float(g), angles[g], angle)
     return [1.0 + 0.6 * jnp.cos(4.0 * angle + 2.0944 * k) for k in range(3)]
 
@@ -113,13 +113,11 @@
         mo[k, X, Y : Y + n, :] = jnp.broadcast_to(0.05 * value, (n, 128))
 
 
-def own_columns(angles, ids, mob, mown):
-    grain = jnp.concatenate([ids[x : x + 1, :].astype(f32) for x in range(8)], axis=1)
-    mob[...] = jnp.zeros(mob.shape, f32)
-    for k, row in enumerate(mobility_of(grain, angles)):
-        mob[k : k + 1, :] = row
+def block_columns(mob, moby, mown):
     for x in range(8):
-        columns(mown, mob, 0, x, x, 0, 0, 16)
+        columns(mown, mob, 0, x, x, 0, 8, 16)
+        columns(mown, moby, 0, x, x, 8, 0, 8)
+        columns(mown, moby, 3, x, x, 0, 24, 8)
 
 
 def tiles_of(src, base, side, dst):
@@ -143,8 +141,11 @@
         z2[8 * t : 8 * t + 8, :] = three(tile(t), tile(t + 18), tile(t + 36) if t + 36 < 52 else None)
 
 
-def unpack_z(scal, angles, z1, meltp, mob, z2, lo, hi, yh, zp, eh, m1, m2, moby, flat, up, dn):
-    top = scal[0] == scal[3] - 1
+def unpack_z(angles, z1, meltp, mine, z2, lo, hi, yh, zp, eh, m1, m2, mob, moby, flat, up, dn):
+    mob[...] = jnp.zeros(mob.shape, f32)
+    for k, row in enumerate(mobility_of(mine[Y_IDS : Y_IDS + 1, :], angles)):
+        mob[k : k + 1, :] = row
+    top = angles[angles.shape[0] - 1] > 0.5
     zp[...] = jnp.where(top, meltp[...], z1[...])
     moby[...] = jnp.zeros(moby.shape, f32)
     for side, src in ((0, lo), (3, hi)):
@@ -199,7 +200,7 @@
     m1[...], m2[...] = swapped(even("gx"), up[...], dn[...])
 
 
-def steps(scal, f, zp, mown, x1a, x1b, moby, yh, eh, x2a, x2b, out, a0, a1, b0, b1, u0, u1, ex, mo):
+def steps(scal, f, zp, mown, x1a, x1b, yh, eh, x2a, x2b, out, a0, a1, b0, b1, u0, u1, ex, mo):
     gz, s1, s2, top = scal[0], scal[1], scal[2], scal[0] == scal[3] - 1
     planes = scal[3] * 128
 
@@ -211,10 +212,7 @@
         for side in range(2):
             a0[k, 8:16, 24 * side : 24 * side + 8, :] = yh[k, side]
             ex[k, 8:16, 24 * side : 24 * side + 8, :] = eh[k, side]
-    mo[:, 8:16, 8:24, :] = mown[...]
-    for x in range(8):
-        columns(mo, moby, 0, x, 8 + x, 8, 0, 8)
-        columns(mo, moby, 3, x, 8 + x, 0, 24, 8)
+    mo[:, 8:16, :, :] = mown[...]
 
     def sides(x1lo, x1hi, x2lo, x2hi):
         for k in range(4):
@@ -398,21 +396,24 @@
     (low,) = kernel(pack_low, 2, [(Z_ROWS, 128)])(own)
     z1 = from_above(low)
     gz = lax.axis_index("gz").astype(jnp.int32)
+    grains = grain_angle.shape[0]
+    at_top = (gz == lax.axis_size("gz") - 1).astype(f32)
+    angles = jnp.pad(grain_angle, (0, 1)) + jnp.where(jnp.arange(grains + 1) == grains, at_top, 0.0)
     scal = jnp.stack([gz, shifts[0], shifts[1], jnp.int32(lax.axis_size("gz"))])
-    mob, mown = kernel(own_columns, 2, [(8, 128), (3, 8, 16, 128)], scalars=1)(grain_angle, grain_ids)
     tiles = (4, 2, 8, 8, 128)
     yh, z2, ylo, yhi = kernel(unpack_y, 2, [tiles, (8 * Z2_TILES, 128), (Y_ROWS, 128), (Y_ROWS, 128)])(y1, y2)
     z2 = from_above(z2)
-    shapes = [(Z_ROWS, 128), tiles, (X2_ROWS, 128), (X2_ROWS, 128), (8, 128)]
-    zp, eh, m1, m2, moby = kernel(unpack_z, 4, shapes, [(416, 128), (X2_ROWS, 128), (X2_ROWS, 128)], scalars=2)(
-        scal, grain_angle, z1, melt_above(melt_planes), mob, z2, ylo, yhi, yh
+    shapes = [(Z_ROWS, 128), tiles, (X2_ROWS, 128), (X2_ROWS, 128), (8, 128), (8, 128)]
+    zp, eh, x2m1, x2m2, mob, moby = kernel(unpack_z, 4, shapes, [(416, 128), (X2_ROWS, 128), (X2_ROWS, 128)], scalars=1)(
+        angles, z1, melt_above(melt_planes), m1, z2, ylo, yhi, yh
     )
-    x2a = swap(m1, "gx", 0)
-    x2b = swap(m2, "gx", 1)
+    x2a = swap(x2m1, "gx", 0)
+    x2b = swap(x2m2, "gx", 1)
+    (mown,) = kernel(block_columns, 2, [(3, 8, 32, 128)])(mob, moby)
     block = (4, 26, 40, 128)
     (out,) = kernel(
         steps, 24, [(4, 8, 16, 128)], [block] * 4 + [block[1:]] * 2 + [(4, 24, 32, 128), (3, 24, 32, 128)], scalars=1
-    )(scal, own, zp, mown, x1a, x1b, moby, yh, eh, x2a, x2b)
+    )(scal, own, zp, mown, x1a, x1b, yh, eh, x2a, x2b)
     return out
 
 

time: 79.6 us -> 86.5 us (1.087)
  the two profiles are of different devices: /device:TPU:1 before, /device:TPU:32 now
where the time goes in v5:
time: 86.5 us; the launch traced here: 86.1 us
  waiting for transfers between devices  37.2 us (43%)
  starting transfers between devices  36.8 us (43%)
  Pallas kernels  11.3 us (13%)
    ppermute x6, waiting for transfers between devices, swap(): lax.ppermute(value, axis, [(i, (i + (1 if (i + stage) % 2 == 0 else -1))...  35.4 us
    ppermute x6, starting transfers between devices, swap(): lax.ppermute(value, axis, [(i, (i + (1 if (i + stage) % 2 == 0 else -1))...  34.2 us
    pallas_call x6, Pallas kernels, call(): pl.pallas_call(fn, in_specs=specs, out_specs=[pl.BlockSpec(memory_space=p...  11.3 us
    ppermute x2, starting transfers between devices, from_above(): return lax.ppermute(value, 'gz', [(i, i - 1) for i in range(1, n)])  2.58 us
    ppermute x2, waiting for transfers between devices, from_above(): return lax.ppermute(value, 'gz', [(i, i - 1) for i in range(1, n)])  1.83 us
  transfers between devices with their start and end apart: 8, of which 5 were waited for; matrix products, arithmetic and copies ran while one was open for 1% of the time, Pallas kernels for 2%

profile of v5, /device:TPU:32, one launch (start us, length us, event | category | flops | bytes accessed | tf_op | source)
XLA Modules:
  0.0 86.1 jit_solution(2660720136498506534)
XLA Ops:
  0.0 1.4 %shard_map.55 = (f32[224,128]{1,0:T(8,128)S(1)}, f32[224,128]{1,0:T(8,128)S(1)}, f32[4,8,16,128]{3,2,1,0:T(8,128)S(1)}) custom-call(f32[4,8,16,128]{3,2,1,0:T(8,128)} %f_in.1, s32[8,16]{1,0:T(8,128)} %ids_in.1, f32[2,4,8,16,16]{4,3,2,1,0:T(8,128)} %melt_in.1), custom_call_target="tpu_custom_call" | custom-call | tf_op jit(solution)/shard_map/pallas_call | solution.py:357
  1.4 4.7 %collective-permute-start.5 = (f32[4,8,16,128]{3,2,1,0:T(8,128)S(1)}, f32[4,8,16,128]{3,2,1,0:T(8,128)S(1)}, u32[]{:S(2)}, u32[]{:S(2)}) collective-permute-start(f32[4,8,16,128]{3,2,1,0:T(8,128)S(1)} %get-tuple-element.18.f), channel_id=1, source_target_pairs={{0,768},{256,512},{512,256},{768,0},{1,769},{257,513},{513,257},{7... | collective-permute-start | bytes 786440 | tf_op jit(solution)/shard_map/ppermute | solution.py:371
  6.1 2.1 %collective-permute-start.4 = (f32[4,8,16,128]{3,2,1,0:T(8,128)S(1)}, f32[4,8,16,128]{3,2,1,0:T(8,128)S(1)}, u32[]{:S(2)}, u32[]{:S(2)}) collective-permute-start(f32[4,8,16,128]{3,2,1,0:T(8,128)S(1)} %get-tuple-element.18.f), channel_id=1, source_target_pairs={{0,256},{256,0},{512,768},{768,512},{1,257},{257,1},{513,769},{769... | collective-permute-start | bytes 786440 | tf_op jit(solution)/shard_map/ppermute | solution.py:371
  8.2 0.1 shard_map.56
  8.4 1.3 %collective-permute-start = (f32[176,128]{1,0:T(8,128)S(1)}, f32[176,128]{1,0:T(8,128)S(1)}, u32[]{:S(2)}, u32[]{:S(2)}) collective-permute-start(f32[176,128]{1,0:T(8,128)S(1)} %shard_map.56), channel_id=1, source_target_pairs={{1,0},{2,1},{3,2},{4,3},{5,4},{6,5},{7,6},{8,7},{9,8},{10,9},{11,1... | collective-permute-start | bytes 270344 | tf_op jit(solution)/shard_map/ppermute | solution.py:376
  9.7 19.2 %collective-permute-start.2 = (f32[224,128]{1,0:T(8,128)S(1)}, f32[224,128]{1,0:T(8,128)S(1)}, u32[]{:S(2)}, u32[]{:S(2)}) collective-permute-start(f32[224,128]{1,0:T(8,128)S(1)} %get-tuple-element.20), channel_id=1, source_target_pairs={{0,240},{16,32},{32,16},{48,64},{64,48},{80,96},{96,80},{112,128},... | collective-permute-start | bytes 344072 | tf_op jit(solution)/shard_map/ppermute | solution.py:371
  28.9 2.0 %collective-permute-start.1 = (f32[224,128]{1,0:T(8,128)S(1)}, f32[224,128]{1,0:T(8,128)S(1)}, u32[]{:S(2)}, u32[]{:S(2)}) collective-permute-start(f32[224,128]{1,0:T(8,128)S(1)} %get-tuple-element.19.mine), channel_id=1, source_target_pairs={{0,16},{16,0},{32,48},{48,32},{64,80},{80,64},{96,112},{112,96},{1... | collective-permute-start | bytes 344072 | tf_op jit(solution)/shard_map/ppermute | solution.py:371
  31.0 0.0 copy-done
  31.0 0.1 pad.30.clone
  31.1 0.1 maximum_maximum_fusion
  31.3 0.1 select_maximum_fusion
  31.4 0.1 select_maximum_fusion.2
  31.5 1.2 %collective-permute-done.2.y2 = f32[224,128]{1,0:T(8,128)S(1)} collective-permute-done((f32[224,128]{1,0:T(8,128)S(1)}, f32[224,128]{1,0:T(8,128)S(1)}, u32[]{:S(2)}, u32[]{:S(2)}) %collective-permute-start.2) | collective-permute-done | bytes 114720 | tf_op jit(solution)/shard_map/ppermute | solution.py:371
  32.8 26.2 %collective-permute-done.1.y1 = f32[224,128]{1,0:T(8,128)S(1)} collective-permute-done((f32[224,128]{1,0:T(8,128)S(1)}, f32[224,128]{1,0:T(8,128)S(1)}, u32[]{:S(2)}, u32[]{:S(2)}) %collective-permute-start.1) | collective-permute-done | bytes 114720 | tf_op jit(solution)/shard_map/ppermute | solution.py:371
  58.9 0.1 shard_map.57
  59.1 0.0 copy-start.2
  59.1 1.3 %collective-permute-start.3 = (f32[144,128]{1,0:T(8,128)S(1)}, f32[144,128]{1,0:T(8,128)S(1)}, u32[]{:S(2)}, u32[]{:S(2)}) collective-permute-start(f32[144,128]{1,0:T(8,128)S(1)} %get-tuple-element.21), channel_id=1, source_target_pairs={{1,0},{2,1},{3,2},{4,3},{5,4},{6,5},{7,6},{8,7},{9,8},{10,9},{11,1... | collective-permute-start | bytes 221192 | tf_op jit(solution)/shard_map/ppermute | solution.py:376
  60.4 0.0 copy-done.2
  60.4 0.0 collective-permute-done.z1
  60.4 1.8 %collective-permute-done.3.z2 = f32[144,128]{1,0:T(8,128)S(1)} collective-permute-done((f32[144,128]{1,0:T(8,128)S(1)}, f32[144,128]{1,0:T(8,128)S(1)}, u32[]{:S(2)}, u32[]{:S(2)}) %collective-permute-start.3) | collective-permute-done | bytes 73760 | tf_op jit(solution)/shard_map/ppermute | solution.py:376
  62.2 0.9 %shard_map.58 = (f32[176,128]{1,0:T(8,128)S(1)}, f32[4,2,8,8,128]{4,3,2,1,0:T(8,128)S(1)}, f32[464,128]{1,0:T(8,128)S(1)}, f32[464,128]{1,0:T(8,128)S(1)}, f32[8,128]{1,0:T(8,128)S(1)}, /*index=5*/f32[8,128]{1,0:T(8,128)S(1)}) custom-call(f32[65]{0:T(128)S(1)} %fusion.angles, f32[176,128]{1,0:T(8,128)S(1)} %collective-permute-done.z1, ...), custom_call_target="tpu_custom_call" | custom-call | tf_op jit(solution)/shard_map/pallas_call | solution.py:357
  63.1 3.7 %collective-permute-start.6 = (f32[464,128]{1,0:T(8,128)S(1)}, f32[464,128]{1,0:T(8,128)S(1)}, u32[]{:S(2)}, u32[]{:S(2)}) collective-permute-start(f32[464,128]{1,0:T(8,128)S(1)} %get-tuple-element.29), channel_id=1, source_target_pairs={{0,256},{256,0},{512,768},{768,512},{1,257},{257,1},{513,769},{769... | collective-permute-start | bytes 712712 | tf_op jit(solution)/shard_map/ppermute | solution.py:371
  66.9 0.0 copy-start.1
  66.9 2.4 %collective-permute-start.7 = (f32[464,128]{1,0:T(8,128)S(1)}, f32[464,128]{1,0:T(8,128)S(1)}, u32[]{:S(2)}, u32[]{:S(2)}) collective-permute-start(f32[464,128]{1,0:T(8,128)S(1)} %get-tuple-element.30), channel_id=1, source_target_pairs={{0,768},{256,512},{512,256},{768,0},{1,769},{257,513},{513,257},{7... | collective-permute-start | bytes 712712 | tf_op jit(solution)/shard_map/ppermute | solution.py:371
  69.3 0.0 copy-done.1
  69.3 0.1 pad_add_fusion.scal
  69.4 0.2 shard_map.59.mown
  69.5 0.0 collective-permute-done.5.x1b
  69.6 0.0 collective-permute-done.4.x1a
  69.6 3.4 %collective-permute-done.6.x2a = f32[464,128]{1,0:T(8,128)S(1)} collective-permute-done((f32[464,128]{1,0:T(8,128)S(1)}, f32[464,128]{1,0:T(8,128)S(1)}, u32[]{:S(2)}, u32[]{:S(2)}) %collective-permute-start.6) | collective-permute-done | bytes 237600 | tf_op jit(solution)/shard_map/ppermute | solution.py:371
  73.0 4.6 %collective-permute-done.7.x2b = f32[464,128]{1,0:T(8,128)S(1)} collective-permute-done((f32[464,128]{1,0:T(8,128)S(1)}, f32[464,128]{1,0:T(8,128)S(1)}, u32[]{:S(2)}, u32[]{:S(2)}) %collective-permute-start.7) | collective-permute-done | bytes 237600 | tf_op jit(solution)/shard_map/ppermute | solution.py:371
  77.5 8.6 %shard_map.60 = f32[4,8,16,128]{3,2,1,0:T(8,128)} custom-call(s32[4]{0:T(128)S(1)} %pad_add_fusion.scal, f32[4,8,16,128]{3,2,1,0:T(8,128)S(1)} %get-tuple-element.18.f, f32[176,128]{1,0:T(8,128)S(1)} %get-tuple-element.25.zp, f32[3,8,32,128]{3,2,1,0:T(8,128)S(1)} %shard_map.59.mown, f32[4,8,16,128]{3,2,1,0:T(8,128)S(1)} %collective-permute-done.4.x1a, ...), custom_call_target="tpu_custom_call" | custom-call | tf_op jit(solution)/shard_map/pallas_call | solution.py:357
  (8 shorter events, 0.1 us)
Async XLA Ops:
  0.0 31.0 %copy-start = (f32[2,4,8,16,16]{4,3,2,1,0:T(8,128)S(1)}, f32[2,4,8,16,16]{4,3,2,1,0:T(8,128)}, u32[]{:S(2)}) copy-start(f32[2,4,8,16,16]{4,3,2,1,0:T(8,128)} %melt_in.1) | copy-start | bytes 196612
  1.4 68.1 %collective-permute-start.5 = (f32[4,8,16,128]{3,2,1,0:T(8,128)S(1)}, f32[4,8,16,128]{3,2,1,0:T(8,128)S(1)}, u32[]{:S(2)}, u32[]{:S(2)}) collective-permute-start(f32[4,8,16,128]{3,2,1,0:T(8,128)S(1)} %get-tuple-element.18.f), channel_id=1, source_target_pairs={{0,768},{256,512},{512,256},{768,0},{1,769},{257,513},{513,257},{7... | collective-permute-start | bytes 786440 | tf_op jit(solution)/shard_map/ppermute | solution.py:371
  6.1 63.5 %collective-permute-start.4 = (f32[4,8,16,128]{3,2,1,0:T(8,128)S(1)}, f32[4,8,16,128]{3,2,1,0:T(8,128)S(1)}, u32[]{:S(2)}, u32[]{:S(2)}) collective-permute-start(f32[4,8,16,128]{3,2,1,0:T(8,128)S(1)} %get-tuple-element.18.f), channel_id=1, source_target_pairs={{0,256},{256,0},{512,768},{768,512},{1,257},{257,1},{513,769},{769... | collective-permute-start | bytes 786440 | tf_op jit(solution)/shard_map/ppermute | solution.py:371
  8.4 52.1 %collective-permute-start = (f32[176,128]{1,0:T(8,128)S(1)}, f32[176,128]{1,0:T(8,128)S(1)}, u32[]{:S(2)}, u32[]{:S(2)}) collective-permute-start(f32[176,128]{1,0:T(8,128)S(1)} %shard_map.56), channel_id=1, source_target_pairs={{1,0},{2,1},{3,2},{4,3},{5,4},{6,5},{7,6},{8,7},{9,8},{10,9},{11,1... | collective-permute-start | bytes 270344 | tf_op jit(solution)/shard_map/ppermute | solution.py:376
  9.7 23.1 %collective-permute-start.2 = (f32[224,128]{1,0:T(8,128)S(1)}, f32[224,128]{1,0:T(8,128)S(1)}, u32[]{:S(2)}, u32[]{:S(2)}) collective-permute-start(f32[224,128]{1,0:T(8,128)S(1)} %get-tuple-element.20), channel_id=1, source_target_pairs={{0,240},{16,32},{32,16},{48,64},{64,48},{80,96},{96,80},{112,128},... | collective-permute-start | bytes 344072 | tf_op jit(solution)/shard_map/ppermute | solution.py:371
  28.9 30.0 %collective-permute-start.1 = (f32[224,128]{1,0:T(8,128)S(1)}, f32[224,128]{1,0:T(8,128)S(1)}, u32[]{:S(2)}, u32[]{:S(2)}) collective-permute-start(f32[224,128]{1,0:T(8,128)S(1)} %get-tuple-element.19.mine), channel_id=1, source_target_pairs={{0,16},{16,0},{32,48},{48,32},{64,80},{80,64},{96,112},{112,96},{1... | collective-permute-start | bytes 344072 | tf_op jit(solution)/shard_map/ppermute | solution.py:371
  59.1 1.3 %copy-start.2 = (f32[64]{0:T(128)S(1)}, f32[64]{0:T(128)}, u32[]{:S(2)}) copy-start(f32[64]{0:T(128)} %param.7) | copy-start | bytes 772
  59.1 3.2 %collective-permute-start.3 = (f32[144,128]{1,0:T(8,128)S(1)}, f32[144,128]{1,0:T(8,128)S(1)}, u32[]{:S(2)}, u32[]{:S(2)}) collective-permute-start(f32[144,128]{1,0:T(8,128)S(1)} %get-tuple-element.21), channel_id=1, source_target_pairs={{1,0},{2,1},{3,2},{4,3},{5,4},{6,5},{7,6},{8,7},{9,8},{10,9},{11,1... | collective-permute-start | bytes 221192 | tf_op jit(solution)/shard_map/ppermute | solution.py:376
  63.1 9.8 %collective-permute-start.6 = (f32[464,128]{1,0:T(8,128)S(1)}, f32[464,128]{1,0:T(8,128)S(1)}, u32[]{:S(2)}, u32[]{:S(2)}) collective-permute-start(f32[464,128]{1,0:T(8,128)S(1)} %get-tuple-element.29), channel_id=1, source_target_pairs={{0,256},{256,0},{512,768},{768,512},{1,257},{257,1},{513,769},{769... | collective-permute-start | bytes 712712 | tf_op jit(solution)/shard_map/ppermute | solution.py:371
  66.9 2.4 %copy-start.1 = (s32[2]{0:T(128)S(1)}, s32[2]{0:T(128)}, u32[]{:S(2)}) copy-start(s32[2]{0:T(128)} %param.9) | copy-start | bytes 28
  66.9 10.7 %collective-permute-start.7 = (f32[464,128]{1,0:T(8,128)S(1)}, f32[464,128]{1,0:T(8,128)S(1)}, u32[]{:S(2)}, u32[]{:S(2)}) collective-permute-start(f32[464,128]{1,0:T(8,128)S(1)} %get-tuple-element.30), channel_id=1, source_target_pairs={{0,768},{256,512},{512,256},{768,0},{1,769},{257,513},{513,257},{7... | collective-permute-start | bytes 712712 | tf_op jit(solution)/shard_map/ppermute | solution.py:371

commit v6 on v5

--- a/solution.py
+++ b/solution.py
@@ -89,7 +89,7 @@
     for out in (up, dn):
         out[Y_IDS : Y_IDS + 1, :] = jnp.concatenate([ids[x : x + 1, :].astype(f32) for x in range(8)], axis=1)
         out[Y_IDS + 1 : Y_ROWS, :] = jnp.zeros((Y_ROWS - Y_IDS - 1, 128), f32)
-    m1[...], m2[...] = swapped(even("gy"), up[...], dn[...])
+    m1[...], m2[...] = swapped(even("gy"), dn[...], up[...])
 
 
 def pack_low(f, zp):
@@ -130,7 +130,7 @@
 
 
 def unpack_y(y1, y2, yh, z2, lo, hi):
-    hi[...], lo[...] = swapped(even("gy"), y1[...], y2[...])
+    lo[...], hi[...] = swapped(even("gy"), y1[...], y2[...])
     tiles_of(lo, 0, 0, yh)
     tiles_of(hi, 0, 1, yh)
 
@@ -389,8 +389,8 @@
     m1, m2, own = kernel(pack_first, 4, [(Y_ROWS, 128)] * 2 + [fields.shape], inputs, hbm=True)(
         *(pltpu.with_memory_space_constraint(v, pltpu.HBM) for v in (fields, grain_ids, melt_planes))
     )
-    y1 = swap(m1, "gy", 0)
-    y2 = swap(m2, "gy", 1)
+    y1 = swap(m1, "gy", 1)
+    y2 = swap(m2, "gy", 0)
     x1a = swap(own, "gx", 0)
     x1b = swap(own, "gx", 1)
     (low,) = kernel(pack_low, 2, [(Z_ROWS, 128)])(own)

time: 86.5 us -> 83.8 us (0.969)
  the two profiles are of different devices: /device:TPU:32 before, /device:TPU:1 now
where the time goes in v6:
time: 83.8 us; the launch traced here: 83.5 us
  starting transfers between devices  42.3 us (50%)
  waiting for transfers between devices  29.1 us (35%)
  Pallas kernels  11.3 us (13%)
    ppermute x6, starting transfers between devices, swap(): lax.ppermute(value, axis, [(i, (i + (1 if (i + stage) % 2 == 0 else -1))...  26.9 us
    ppermute x6, waiting for transfers between devices, swap(): lax.ppermute(value, axis, [(i, (i + (1 if (i + stage) % 2 == 0 else -1))...  25.3 us
    ppermute x2, starting transfers between devices, from_above(): return lax.ppermute(value, 'gz', [(i, i - 1) for i in range(1, n)])  15.4 us
    pallas_call x6, Pallas kernels, call(): pl.pallas_call(fn, in_specs=specs, out_specs=[pl.BlockSpec(memory_space=p...  11.3 us
    ppermute x2, waiting for transfers between devices, from_above(): return lax.ppermute(value, 'gz', [(i, i - 1) for i in range(1, n)])  3.83 us
  transfers between devices with their start and end apart: 8, of which 5 were waited for; matrix products, arithmetic and copies ran while one was open for 1% of the time, Pallas kernels for 2%

profile of v6, /device:TPU:1, one launch (start us, length us, event | category | flops | bytes accessed | tf_op | source)
XLA Modules:
  0.0 83.5 jit_solution(16855945456032419135)
XLA Ops:
  0.0 1.4 %shard_map.55 = (f32[224,128]{1,0:T(8,128)S(1)}, f32[224,128]{1,0:T(8,128)S(1)}, f32[4,8,16,128]{3,2,1,0:T(8,128)S(1)}) custom-call(f32[4,8,16,128]{3,2,1,0:T(8,128)} %f_in.1, s32[8,16]{1,0:T(8,128)} %ids_in.1, f32[2,4,8,16,16]{4,3,2,1,0:T(8,128)} %melt_in.1), custom_call_target="tpu_custom_call" | custom-call | tf_op jit(solution)/shard_map/pallas_call | solution.py:357
  1.4 5.2 %collective-permute-start.5 = (f32[4,8,16,128]{3,2,1,0:T(8,128)S(1)}, f32[4,8,16,128]{3,2,1,0:T(8,128)S(1)}, u32[]{:S(2)}, u32[]{:S(2)}) collective-permute-start(f32[4,8,16,128]{3,2,1,0:T(8,128)S(1)} %get-tuple-element.18.f), channel_id=1, source_target_pairs={{0,768},{256,512},{512,256},{768,0},{1,769},{257,513},{513,257},{7... | collective-permute-start | bytes 786440 | tf_op jit(solution)/shard_map/ppermute | solution.py:371
  6.6 1.9 %collective-permute-start.4 = (f32[4,8,16,128]{3,2,1,0:T(8,128)S(1)}, f32[4,8,16,128]{3,2,1,0:T(8,128)S(1)}, u32[]{:S(2)}, u32[]{:S(2)}) collective-permute-start(f32[4,8,16,128]{3,2,1,0:T(8,128)S(1)} %get-tuple-element.18.f), channel_id=1, source_target_pairs={{0,256},{256,0},{512,768},{768,512},{1,257},{257,1},{513,769},{769... | collective-permute-start | bytes 786440 | tf_op jit(solution)/shard_map/ppermute | solution.py:371
  8.6 0.1 shard_map.56
  8.7 12.7 %collective-permute-start = (f32[176,128]{1,0:T(8,128)S(1)}, f32[176,128]{1,0:T(8,128)S(1)}, u32[]{:S(2)}, u32[]{:S(2)}) collective-permute-start(f32[176,128]{1,0:T(8,128)S(1)} %shard_map.56), channel_id=1, source_target_pairs={{1,0},{2,1},{3,2},{4,3},{5,4},{6,5},{7,6},{8,7},{9,8},{10,9},{11,1... | collective-permute-start | bytes 270344 | tf_op jit(solution)/shard_map/ppermute | solution.py:376
  21.4 9.4 %collective-permute-start.2 = (f32[224,128]{1,0:T(8,128)S(1)}, f32[224,128]{1,0:T(8,128)S(1)}, u32[]{:S(2)}, u32[]{:S(2)}) collective-permute-start(f32[224,128]{1,0:T(8,128)S(1)} %get-tuple-element.20), channel_id=1, source_target_pairs={{0,16},{16,0},{32,48},{48,32},{64,80},{80,64},{96,112},{112,96},{1... | collective-permute-start | bytes 344072 | tf_op jit(solution)/shard_map/ppermute | solution.py:371
  30.9 4.8 %collective-permute-start.1 = (f32[224,128]{1,0:T(8,128)S(1)}, f32[224,128]{1,0:T(8,128)S(1)}, u32[]{:S(2)}, u32[]{:S(2)}) collective-permute-start(f32[224,128]{1,0:T(8,128)S(1)} %get-tuple-element.19.mine), channel_id=1, source_target_pairs={{0,240},{16,32},{32,16},{48,64},{64,48},{80,96},{96,80},{112,128},... | collective-permute-start | bytes 344072 | tf_op jit(solution)/shard_map/ppermute | solution.py:371
  35.7 0.0 copy-done
  35.8 0.1 pad.30.clone
  35.8 0.1 maximum_maximum_fusion
  36.0 0.1 select_maximum_fusion
  36.1 0.1 select_maximum_fusion.2
  36.2 0.7 collective-permute-done.2.y2
  36.9 18.2 %collective-permute-done.1.y1 = f32[224,128]{1,0:T(8,128)S(1)} collective-permute-done((f32[224,128]{1,0:T(8,128)S(1)}, f32[224,128]{1,0:T(8,128)S(1)}, u32[]{:S(2)}, u32[]{:S(2)}) %collective-permute-start.1) | collective-permute-done | bytes 114720 | tf_op jit(solution)/shard_map/ppermute | solution.py:371
  55.2 0.1 shard_map.57
  55.3 0.0 copy-start.2
  55.3 2.6 %collective-permute-start.3 = (f32[144,128]{1,0:T(8,128)S(1)}, f32[144,128]{1,0:T(8,128)S(1)}, u32[]{:S(2)}, u32[]{:S(2)}) collective-permute-start(f32[144,128]{1,0:T(8,128)S(1)} %get-tuple-element.21), channel_id=1, source_target_pairs={{1,0},{2,1},{3,2},{4,3},{5,4},{6,5},{7,6},{8,7},{9,8},{10,9},{11,1... | collective-permute-start | bytes 221192 | tf_op jit(solution)/shard_map/ppermute | solution.py:376
  58.0 0.0 copy-done.2
  58.0 0.0 collective-permute-done.z1
  58.0 3.8 %collective-permute-done.3.z2 = f32[144,128]{1,0:T(8,128)S(1)} collective-permute-done((f32[144,128]{1,0:T(8,128)S(1)}, f32[144,128]{1,0:T(8,128)S(1)}, u32[]{:S(2)}, u32[]{:S(2)}) %collective-permute-start.3) | collective-permute-done | bytes 73760 | tf_op jit(solution)/shard_map/ppermute | solution.py:376
  61.8 0.9 %shard_map.58 = (f32[176,128]{1,0:T(8,128)S(1)}, f32[4,2,8,8,128]{4,3,2,1,0:T(8,128)S(1)}, f32[464,128]{1,0:T(8,128)S(1)}, f32[464,128]{1,0:T(8,128)S(1)}, f32[8,128]{1,0:T(8,128)S(1)}, /*index=5*/f32[8,128]{1,0:T(8,128)S(1)}) custom-call(f32[65]{0:T(128)S(1)} %fusion.angles, f32[176,128]{1,0:T(8,128)S(1)} %collective-permute-done.z1, ...), custom_call_target="tpu_custom_call" | custom-call | tf_op jit(solution)/shard_map/pallas_call | solution.py:357
  62.7 3.4 %collective-permute-start.6 = (f32[464,128]{1,0:T(8,128)S(1)}, f32[464,128]{1,0:T(8,128)S(1)}, u32[]{:S(2)}, u32[]{:S(2)}) collective-permute-start(f32[464,128]{1,0:T(8,128)S(1)} %get-tuple-element.29), channel_id=1, source_target_pairs={{0,256},{256,0},{512,768},{768,512},{1,257},{257,1},{513,769},{769... | collective-permute-start | bytes 712712 | tf_op jit(solution)/shard_map/ppermute | solution.py:371
  66.2 0.0 copy-start.1
  66.2 2.1 %collective-permute-start.7 = (f32[464,128]{1,0:T(8,128)S(1)}, f32[464,128]{1,0:T(8,128)S(1)}, u32[]{:S(2)}, u32[]{:S(2)}) collective-permute-start(f32[464,128]{1,0:T(8,128)S(1)} %get-tuple-element.30), channel_id=1, source_target_pairs={{0,768},{256,512},{512,256},{768,0},{1,769},{257,513},{513,257},{7... | collective-permute-start | bytes 712712 | tf_op jit(solution)/shard_map/ppermute | solution.py:371
  68.3 0.0 copy-done.1
  68.3 0.1 pad_add_fusion.scal
  68.4 0.2 shard_map.59.mown
  68.6 0.0 collective-permute-done.5.x1b
  68.6 0.0 collective-permute-done.4.x1a
  68.6 1.7 %collective-permute-done.6.x2a = f32[464,128]{1,0:T(8,128)S(1)} collective-permute-done((f32[464,128]{1,0:T(8,128)S(1)}, f32[464,128]{1,0:T(8,128)S(1)}, u32[]{:S(2)}, u32[]{:S(2)}) %collective-permute-start.6) | collective-permute-done | bytes 237600 | tf_op jit(solution)/shard_map/ppermute | solution.py:371
  70.3 4.6 %collective-permute-done.7.x2b = f32[464,128]{1,0:T(8,128)S(1)} collective-permute-done((f32[464,128]{1,0:T(8,128)S(1)}, f32[464,128]{1,0:T(8,128)S(1)}, u32[]{:S(2)}, u32[]{:S(2)}) %collective-permute-start.7) | collective-permute-done | bytes 237600 | tf_op jit(solution)/shard_map/ppermute | solution.py:371
  74.9 8.6 %shard_map.60 = f32[4,8,16,128]{3,2,1,0:T(8,128)} custom-call(s32[4]{0:T(128)S(1)} %pad_add_fusion.scal, f32[4,8,16,128]{3,2,1,0:T(8,128)S(1)} %get-tuple-element.18.f, f32[176,128]{1,0:T(8,128)S(1)} %get-tuple-element.25.zp, f32[3,8,32,128]{3,2,1,0:T(8,128)S(1)} %shard_map.59.mown, f32[4,8,16,128]{3,2,1,0:T(8,128)S(1)} %collective-permute-done.4.x1a, ...), custom_call_target="tpu_custom_call" | custom-call | tf_op jit(solution)/shard_map/pallas_call | solution.py:357
  (8 shorter events, 0.1 us)
Async XLA Ops:
  0.0 35.7 %copy-start = (f32[2,4,8,16,16]{4,3,2,1,0:T(8,128)S(1)}, f32[2,4,8,16,16]{4,3,2,1,0:T(8,128)}, u32[]{:S(2)}) copy-start(f32[2,4,8,16,16]{4,3,2,1,0:T(8,128)} %melt_in.1) | copy-start | bytes 196612
  1.4 67.1 %collective-permute-start.5 = (f32[4,8,16,128]{3,2,1,0:T(8,128)S(1)}, f32[4,8,16,128]{3,2,1,0:T(8,128)S(1)}, u32[]{:S(2)}, u32[]{:S(2)}) collective-permute-start(f32[4,8,16,128]{3,2,1,0:T(8,128)S(1)} %get-tuple-element.18.f), channel_id=1, source_target_pairs={{0,768},{256,512},{512,256},{768,0},{1,769},{257,513},{513,257},{7... | collective-permute-start | bytes 786440 | tf_op jit(solution)/shard_map/ppermute | solution.py:371
  6.6 61.9 %collective-permute-start.4 = (f32[4,8,16,128]{3,2,1,0:T(8,128)S(1)}, f32[4,8,16,128]{3,2,1,0:T(8,128)S(1)}, u32[]{:S(2)}, u32[]{:S(2)}) collective-permute-start(f32[4,8,16,128]{3,2,1,0:T(8,128)S(1)} %get-tuple-element.18.f), channel_id=1, source_target_pairs={{0,256},{256,0},{512,768},{768,512},{1,257},{257,1},{513,769},{769... | collective-permute-start | bytes 786440 | tf_op jit(solution)/shard_map/ppermute | solution.py:371
  8.7 49.3 %collective-permute-start = (f32[176,128]{1,0:T(8,128)S(1)}, f32[176,128]{1,0:T(8,128)S(1)}, u32[]{:S(2)}, u32[]{:S(2)}) collective-permute-start(f32[176,128]{1,0:T(8,128)S(1)} %shard_map.56), channel_id=1, source_target_pairs={{1,0},{2,1},{3,2},{4,3},{5,4},{6,5},{7,6},{8,7},{9,8},{10,9},{11,1... | collective-permute-start | bytes 270344 | tf_op jit(solution)/shard_map/ppermute | solution.py:376
  21.4 15.5 %collective-permute-start.2 = (f32[224,128]{1,0:T(8,128)S(1)}, f32[224,128]{1,0:T(8,128)S(1)}, u32[]{:S(2)}, u32[]{:S(2)}) collective-permute-start(f32[224,128]{1,0:T(8,128)S(1)} %get-tuple-element.20), channel_id=1, source_target_pairs={{0,16},{16,0},{32,48},{48,32},{64,80},{80,64},{96,112},{112,96},{1... | collective-permute-start | bytes 344072 | tf_op jit(solution)/shard_map/ppermute | solution.py:371
  30.9 24.3 %collective-permute-start.1 = (f32[224,128]{1,0:T(8,128)S(1)}, f32[224,128]{1,0:T(8,128)S(1)}, u32[]{:S(2)}, u32[]{:S(2)}) collective-permute-start(f32[224,128]{1,0:T(8,128)S(1)} %get-tuple-element.19.mine), channel_id=1, source_target_pairs={{0,240},{16,32},{32,16},{48,64},{64,48},{80,96},{96,80},{112,128},... | collective-permute-start | bytes 344072 | tf_op jit(solution)/shard_map/ppermute | solution.py:371
  55.3 2.7 %copy-start.2 = (f32[64]{0:T(128)S(1)}, f32[64]{0:T(128)}, u32[]{:S(2)}) copy-start(f32[64]{0:T(128)} %param.7) | copy-start | bytes 772
  55.3 6.5 %collective-permute-start.3 = (f32[144,128]{1,0:T(8,128)S(1)}, f32[144,128]{1,0:T(8,128)S(1)}, u32[]{:S(2)}, u32[]{:S(2)}) collective-permute-start(f32[144,128]{1,0:T(8,128)S(1)} %get-tuple-element.21), channel_id=1, source_target_pairs={{1,0},{2,1},{3,2},{4,3},{5,4},{6,5},{7,6},{8,7},{9,8},{10,9},{11,1... | collective-permute-start | bytes 221192 | tf_op jit(solution)/shard_map/ppermute | solution.py:376
  62.7 7.5 %collective-permute-start.6 = (f32[464,128]{1,0:T(8,128)S(1)}, f32[464,128]{1,0:T(8,128)S(1)}, u32[]{:S(2)}, u32[]{:S(2)}) collective-permute-start(f32[464,128]{1,0:T(8,128)S(1)} %get-tuple-element.29), channel_id=1, source_target_pairs={{0,256},{256,0},{512,768},{768,512},{1,257},{257,1},{513,769},{769... | collective-permute-start | bytes 712712 | tf_op jit(solution)/shard_map/ppermute | solution.py:371
  66.2 2.1 %copy-start.1 = (s32[2]{0:T(128)S(1)}, s32[2]{0:T(128)}, u32[]{:S(2)}) copy-start(s32[2]{0:T(128)} %param.9) | copy-start | bytes 28
  66.2 8.7 %collective-permute-start.7 = (f32[464,128]{1,0:T(8,128)S(1)}, f32[464,128]{1,0:T(8,128)S(1)}, u32[]{:S(2)}, u32[]{:S(2)}) collective-permute-start(f32[464,128]{1,0:T(8,128)S(1)} %get-tuple-element.30), channel_id=1, source_target_pairs={{0,768},{256,512},{512,256},{768,0},{1,769},{257,513},{513,257},{7... | collective-permute-start | bytes 712712 | tf_op jit(solution)/shard_map/ppermute | solution.py:371
